TPU v7x, 32 devices: a whole 2x2x4 slice. The times are simulated.
32 devices in a mesh: ep: 4 (over z), fsdp: 8 (over y, x, core).
Axes of the slice: x: 2, y: 2, z: 4, core: 2. Of those that a mesh axis runs over, the one named last changes fastest.
Arguments:
- x_in: bfloat16 [32, 512, 768], P(('ep', 'fsdp'))
- grad_y: bfloat16 [32, 512, 768], P(('ep', 'fsdp'))
- w_q: bfloat16 [768, 12, 64], P(('ep', 'fsdp'))
- w_k: bfloat16 [768, 12, 64], P(('ep', 'fsdp'))
- w_v: bfloat16 [768, 12, 64], P(('ep', 'fsdp'))
- w_o: bfloat16 [12, 64, 768], P(None, None, ('ep', 'fsdp'))
- gamma_attn: bfloat16 [768], P(('ep', 'fsdp'))
- gamma_mlp: bfloat16 [768], P(('ep', 'fsdp'))
- w_router: float32 [768, 8], P(('ep', 'fsdp'))
- w1_shared: bfloat16 [768, 3072], P(('ep', 'fsdp'))
- w3_shared: bfloat16 [768, 3072], P(('ep', 'fsdp'))
- w2_shared: bfloat16 [3072, 768], P(None, ('ep', 'fsdp'))
- w1_expert: bfloat16 [8, 768, 3072], P('ep', 'fsdp')
- w3_expert: bfloat16 [8, 768, 3072], P('ep', 'fsdp')
- w2_expert: bfloat16 [8, 3072, 768], P('ep', 'fsdp')
- expert_ids: int32 [32, 512], P(('ep', 'fsdp'))
Outputs:
- output 1: bfloat16 [32, 512, 768], P(('ep', 'fsdp'))
- output 2: bfloat16 [32, 512, 768], P(('ep', 'fsdp'))
- output 3: float32 [768, 12, 64], P(('ep', 'fsdp'))
- output 4: float32 [768, 12, 64], P(('ep', 'fsdp'))
- output 5: float32 [768, 12, 64], P(('ep', 'fsdp'))
- output 6: float32 [12, 64, 768], P(None, None, ('ep', 'fsdp'))
- output 7: float32 [768], P(('ep', 'fsdp'))
- output 8: float32 [768], P(('ep', 'fsdp'))
- output 9: float32 [768, 8], P(('ep', 'fsdp'))
- output 10: float32 [768, 3072], P(('ep', 'fsdp'))
- output 11: float32 [768, 3072], P(('ep', 'fsdp'))
- output 12: float32 [3072, 768], P(None, ('ep', 'fsdp'))
- output 13: float32 [8, 768, 3072], P('ep', 'fsdp')
- output 14: float32 [8, 768, 3072], P('ep', 'fsdp')
- output 15: float32 [8, 3072, 768], P('ep', 'fsdp')
All inputs are finite; a program needn't handle non-finite values.
Results may differ from a plain program's by a relative error of at most 0.02.
Values are sent between devices in bfloat16 or wider.
A program may use at most 1 GiB of HBM per device.

v0:
```python
import jax
import jax.numpy as jnp
import numpy as np
from jax import lax
from jax.experimental import pallas as pl
from jax.experimental.pallas import tpu as pltpu
from jax.sharding import Mesh, PartitionSpec as P

EPS_NORM = 1e-5
EPS_QK = 1e-6
ROPE_BASE = 500000.0
QUERY_BLOCK = 256
VMEM_LIMIT = 60 * 1024 * 1024
AXES = ('z', 'y', 'x', 'c')
Z_STEPS = (1, 2, 3)
SWAP = ((0, 1), (1, 0))
F32 = jnp.float32
BF16 = jnp.bfloat16


def rms_norm(tokens, gamma_vec):
    tok_f32 = tokens.astype(F32)
    inv_rms = lax.rsqrt(jnp.mean(tok_f32 * tok_f32, axis=-1, keepdims=True) + EPS_NORM)
    return (tok_f32 * inv_rms * gamma_vec.astype(F32)).astype(BF16)


def rope_tables(seq_len, head_dim):
    half_dim = head_dim // 2
    inv_freq = ROPE_BASE ** (-(jnp.arange(half_dim, dtype=F32) * 2.0 / head_dim))
    angles = jnp.arange(seq_len, dtype=F32)[:, None] * inv_freq[None, :]
    cos_tab, sin_tab = jnp.cos(angles), jnp.sin(angles)
    return jnp.concatenate([cos_tab] * 4, axis=1), jnp.concatenate([-sin_tab, sin_tab] * 2, axis=1)


def lane_masks(rows):
    lane = lax.broadcasted_iota(jnp.int32, (rows, 128), 1)
    return lane % 64 < 32, lane < 64


def turn(vals, cos_tab, sin_tab, low_half):
    partner = jnp.where(low_half, pltpu.roll(vals, 96, 1), pltpu.roll(vals, 32, 1))
    return vals * cos_tab + partner * sin_tab


def head_mean(vals, head_a):
    sum_a = jnp.sum(jnp.where(head_a, vals, 0.0), axis=1, keepdims=True)
    sum_b = jnp.sum(jnp.where(head_a, 0.0, vals), axis=1, keepdims=True)
    return jnp.where(head_a, sum_a, sum_b) * (1.0 / 64)


def rope_norm(vals, cos_tab, sin_tab, low_half, head_a):
    rotated = turn(vals.astype(F32), cos_tab, sin_tab, low_half)
    inv = lax.rsqrt(head_mean(rotated * rotated, head_a) + EPS_QK)
    return rotated, inv, (rotated * inv).astype(BF16)


def rope_norm_back(d_out, rotated, inv, cos_tab, sin_tab, low_half, head_a):
    d_rot = inv * d_out - rotated * (inv * inv * inv * head_mean(d_out * rotated, head_a))
    return turn(d_rot, cos_tab, -sin_tab, low_half).astype(BF16)


def dot_nn(lhs, rhs):
    return jnp.einsum('ik,kj->ij', lhs, rhs, preferred_element_type=F32)


def dot_nt(lhs, rhs):
    return jnp.einsum('ik,jk->ij', lhs, rhs, preferred_element_type=F32)


def dot_tn(lhs, rhs):
    return jnp.einsum('ki,kj->ij', lhs, rhs, preferred_element_type=F32)


def softmax_block(q_rows, k_all, start, keys):
    scores = dot_nt(q_rows, k_all[:keys]) * 0.125
    row = start + lax.broadcasted_iota(jnp.int32, scores.shape, 0)
    col = lax.broadcasted_iota(jnp.int32, scores.shape, 1)
    scores = jnp.where(row >= col, scores, -1e30)
    weights = jnp.exp(scores - jnp.max(scores, axis=1, keepdims=True))
    return weights / jnp.sum(weights, axis=1, keepdims=True)


def attn_fwd_kernel(q_ref, k_ref, v_ref, cos_ref, sin_ref, o_ref):
    seq = q_ref.shape[0]
    low_half, head_a = lane_masks(seq)
    cos_tab, sin_tab = cos_ref[:], sin_ref[:]
    q_rot = rope_norm(q_ref[:], cos_tab, sin_tab, low_half, head_a)[-1]
    k_rot = rope_norm(k_ref[:], cos_tab, sin_tab, low_half, head_a)[-1]
    v_all = v_ref[:]
    zero = jnp.zeros_like(q_rot)
    q_heads = jnp.where(head_a, q_rot, zero), jnp.where(head_a, zero, q_rot)
    for start in range(0, seq, QUERY_BLOCK):
        keys = start + QUERY_BLOCK
        outs = [dot_nn(softmax_block(q_head[start:keys], k_rot, start, keys).astype(BF16), v_all[:keys]) for q_head in q_heads]
        o_ref[start:keys, :] = jnp.where(head_a[:QUERY_BLOCK], outs[0], outs[1]).astype(BF16)


def attn_bwd_kernel(q_ref, k_ref, v_ref, do_ref, cos_ref, sin_ref, dq_ref, dk_ref, dv_ref):
    seq = q_ref.shape[0]
    low_half, head_a = lane_masks(seq)
    cos_tab, sin_tab = cos_ref[:], sin_ref[:]
    q_raw, q_inv, q_rot = rope_norm(q_ref[:], cos_tab, sin_tab, low_half, head_a)
    k_raw, k_inv, k_rot = rope_norm(k_ref[:], cos_tab, sin_tab, low_half, head_a)
    v_all, d_o = v_ref[:], do_ref[:]
    zero = jnp.zeros_like(q_rot)
    grads = []
    for head in range(2):
        def only(vals, head=head):
            return jnp.where(head_a, vals, zero) if head == 0 else jnp.where(head_a, zero, vals)

        q_head, do_head = only(q_rot), only(d_o)
        dq_rows, dk_sum, dv_sum = [], None, None
        for start in range(0, seq, QUERY_BLOCK):
            keys = start + QUERY_BLOCK
            probs = softmax_block(q_head[start:keys], k_rot, start, keys)
            d_probs = dot_nt(do_head[start:keys], v_all[:keys])
            d_scores = probs * (d_probs - jnp.sum(probs * d_probs, axis=1, keepdims=True)) * 0.125
            d_scores = d_scores.astype(BF16)
            dq_rows.append(dot_nn(d_scores, k_rot[:keys]))
            dk_part = dot_tn(d_scores, q_head[start:keys])
            dv_part = dot_tn(probs.astype(BF16), do_head[start:keys])
            if keys < seq:
                pad = jnp.zeros((seq - keys, 128), F32)
                dk_part, dv_part = jnp.concatenate([dk_part, pad]), jnp.concatenate([dv_part, pad])
            dk_sum = dk_part if dk_sum is None else dk_sum + dk_part
            dv_sum = dv_part if dv_sum is None else dv_sum + dv_part
        grads.append((jnp.concatenate(dq_rows), dk_sum, dv_sum))
    d_q, d_k, d_v = (jnp.where(head_a, part_a, part_b) for part_a, part_b in zip(*grads))
    dq_ref[:] = rope_norm_back(d_q, q_raw, q_inv, cos_tab, sin_tab, low_half, head_a)
    dk_ref[:] = rope_norm_back(d_k, k_raw, k_inv, cos_tab, sin_tab, low_half, head_a)
    dv_ref[:] = d_v.astype(BF16)


def fixed(*shape):
    return pl.BlockSpec(shape, lambda *_: (0,) * len(shape))


def kernel_cost(flops, moved):
    return pl.CostEstimate(flops=flops, bytes_accessed=moved, transcendentals=0)


def attn_specs(seq, pairs):
    head_specs = [pl.BlockSpec((seq, 128), lambda pair, part=part: (0, part * pairs + pair)) for part in range(3)]
    one = pl.BlockSpec((seq, 128), lambda pair: (0, pair))
    table = fixed(seq, 128)
    return head_specs, one, table


def attn_fwd(qkv, cos_tab, sin_tab):
    seq, width = qkv.shape[0], qkv.shape[1] // 3
    head_specs, one, table = attn_specs(seq, width // 128)
    return pl.pallas_call(
        attn_fwd_kernel, grid=(width // 128,), in_specs=head_specs + [table, table], out_specs=one,
        out_shape=jax.ShapeDtypeStruct((seq, width), BF16),
        compiler_params=pltpu.CompilerParams(vmem_limit_bytes=VMEM_LIMIT),
        cost_estimate=kernel_cost(40 * seq * seq * width, seq * width),
    )(qkv, qkv, qkv, cos_tab, sin_tab)


def attn_bwd(qkv, d_o, cos_tab, sin_tab):
    seq, width = qkv.shape[0], qkv.shape[1] // 3
    head_specs, one, table = attn_specs(seq, width // 128)
    return pl.pallas_call(
        attn_bwd_kernel, grid=(width // 128,), in_specs=head_specs + [one, table, table], out_specs=[one] * 3,
        out_shape=[jax.ShapeDtypeStruct((seq, width), BF16)] * 3,
        compiler_params=pltpu.CompilerParams(vmem_limit_bytes=VMEM_LIMIT),
        cost_estimate=kernel_cost(80 * seq * seq * width, seq * width),
    )(qkv, qkv, qkv, d_o, cos_tab, sin_tab)


def route_slots(flat_ids, n_experts, capacity):
    onehot = flat_ids[:, None] == jnp.arange(n_experts)[None, :]
    running = jnp.cumsum(onehot.astype(jnp.int32), axis=0)
    slot_idx = jnp.sum(jnp.where(onehot, running, 0), axis=1) - 1
    return onehot, flat_ids * capacity + slot_idx


def hop(block, axis):
    return lax.ppermute(block, axis, SWAP)


def z_hop(block, step):
    return lax.ppermute(block, 'z', [(z_idx, z_idx ^ step) for z_idx in range(4)])


def pick(array, idx, axis):
    return lax.dynamic_index_in_dim(array, idx, axis, keepdims=False)


def in_core_order(mine, other, axis):
    first = lax.axis_index('c') == 0
    return jnp.concatenate([jnp.where(first, mine, other), jnp.where(first, other, mine)], axis=axis)


def plane_first(block):
    return block, hop(block, 'x'), hop(block, 'y')


def plane_pieces(first):
    block, from_x, from_y = first
    half = block.shape[0] // 2
    return block, from_x, from_y, hop(from_y[:half], 'x'), hop(from_x[half:], 'y')


def after(value, *anchors):
    return lax.optimization_barrier((value,) + anchors)[0]


def z_stack(parts):
    half = parts[0].shape[1] // 2
    c_me = lax.axis_index('c')

    def side(core):
        return jnp.concatenate([lax.dynamic_slice_in_dim(part, core * half, half, 1) for part in parts], axis=1)

    chip = in_core_order(side(c_me), hop(side(1 - c_me), 'c'), 0)
    return [chip] + [z_hop(chip, step) for step in Z_STEPS]


def weight_kernel(att_ref, small_ref, att_out, small_out, local_sems, send_sems, recv_sems):
    z_me, y_me, x_me, c_me = (lax.axis_index(name) for name in AXES)
    peers = [((z_me + step) % 4, y_me, x_me, c_me) for step in Z_STEPS]
    peer_x, peer_y, peer_c = (z_me, y_me, 1 - x_me, c_me), (z_me, 1 - y_me, x_me, c_me), (z_me, y_me, x_me, 1 - c_me)
    barrier = pltpu.get_barrier_semaphore()
    everyone = peers + [peer_x, peer_y, peer_c]
    for peer in everyone:
        pl.semaphore_signal(barrier, inc=1, device_id=peer, device_id_type=pl.DeviceIdType.MESH)
    pl.semaphore_wait(barrier, len(everyone))

    def slot(back, rel, core):
        y_at, x_at = (1 - y_me if rel >= 2 else y_me), (1 - x_me if rel % 2 else x_me)
        return (((z_me + 4 - back) % 4 * 2 + y_at) * 2 + x_at) * 2 + core

    pairs = ((att_ref, att_out), (small_ref, small_out))

    started = []

    def send(back, rel, peer, sem, own=False):
        at = slot(back, rel, c_me)
        for kind, (src, out) in enumerate(pairs):
            copy = pltpu.make_async_remote_copy(
                src_ref=src if own else out.at[at], dst_ref=out.at[at], send_sem=send_sems.at[kind, sem], recv_sem=recv_sems.at[kind, sem],
                device_id=peer, device_id_type=pl.DeviceIdType.MESH)
            copy.start()
            started.append(copy)

    def landed(back, rel, sem, core=c_me):
        for kind, (src, out) in enumerate(pairs):
            pltpu.make_async_copy(src, out.at[slot(back, rel, core)], recv_sems.at[kind, sem]).wait()

    z_sem, x_sem, y_sem, far_sem, c_sem = range(0, 20, 4)
    for step, peer in zip(Z_STEPS, peers):
        send(0, 0, peer, z_sem + step, own=True)
    for back in range(4):
        if back:
            landed(back, 0, z_sem + back)
        send(back, 0, peer_x, x_sem + back, own=not back)
        send(back, 0, peer_y, y_sem + back, own=not back)
        send(back, 0, peer_c, c_sem + 4 * back, own=not back)
    for back in range(4):
        landed(back, 1, x_sem + back)
        if back >= 2:
            send(back, 1, peer_y, far_sem + back)
        send(back, 1, peer_c, c_sem + 4 * back + 1)
        landed(back, 2, y_sem + back)
        if back < 2:
            send(back, 2, peer_x, far_sem + back)
        send(back, 2, peer_c, c_sem + 4 * back + 2)
    for back in range(4):
        landed(back, 3, far_sem + back)
        send(back, 3, peer_c, c_sem + 4 * back + 3)
    local = [pltpu.make_async_copy(src, out.at[slot(0, 0, c_me)], local_sems.at[kind]) for kind, (src, out) in enumerate(pairs)]
    for copy in local:
        copy.start()
    for back in range(4):
        for rel in range(4):
            landed(back, rel, c_sem + 4 * back + rel, 1 - c_me)
    for copy in local:
        copy.wait()
    for copy in started:
        copy.wait_send()


def gather_weights(att_block, small):
    any_spec = pl.BlockSpec(memory_space=pl.ANY)
    blocks = (att_block, small)
    return pl.pallas_call(
        weight_kernel, in_specs=[any_spec] * 2, out_specs=[any_spec] * 2,
        out_shape=[jax.ShapeDtypeStruct((32,) + block.shape, block.dtype) for block in blocks],
        scratch_shapes=[pltpu.SemaphoreType.DMA((2,)), pltpu.SemaphoreType.DMA((2, 32)), pltpu.SemaphoreType.DMA((2, 32))],
        compiler_params=pltpu.CompilerParams(collective_id=0, has_side_effects=True),
        cost_estimate=kernel_cost(att_block.size * 10 ** 5, att_block.size),
    )(*blocks)


def expert_chips(w1_expert, w3_expert, w2_expert):
    c_me = lax.axis_index('c')
    up = jnp.stack([w1_expert, w3_expert])
    up_chip = in_core_order(pick(up, c_me, 1), hop(pick(up, 1 - c_me, 1), 'c'), 1)
    down_chip = in_core_order(pick(w2_expert, c_me, 0), hop(pick(w2_expert, 1 - c_me, 0), 'c'), 0)
    return up_chip, down_chip.reshape(2, -1, down_chip.shape[1])


def dot32(lhs, rhs):
    return jnp.dot(lhs, rhs, preferred_element_type=F32)


def ffn_rows(rows_ref, dd_ref, w1_ref, w3_ref, w2_ref, w2_turned, wait_w2, act_ref, dg_ref, dl_ref, out_acc, back_acc):
    chunk = 512

    def step(idx, carry):
        at = pl.ds(pl.multiple_of(idx * chunk, chunk), chunk)
        gate, lin = dot_nn(rows_ref[at, :], w1_ref[:]), dot_nn(rows_ref[at, :], w3_ref[:])
        sig = jax.nn.sigmoid(gate)
        silu = gate * sig
        act = (silu * lin).astype(BF16)
        act_ref[at, :] = act
        if wait_w2 is not None:
            wait_w2(idx)
        w2 = w2_ref[:]
        d_act = (dot_nn(dd_ref[at, :], w2) if w2_turned else dot_nt(dd_ref[at, :], w2)).astype(BF16).astype(F32)
        d_lin = (d_act * silu).astype(BF16)
        d_gate = (d_act * lin * (sig + silu * (1.0 - sig))).astype(BF16)
        dg_ref[at, :] = d_gate
        dl_ref[at, :] = d_lin
        out_acc[at, :] += dot_nt(act, w2) if w2_turned else dot_nn(act, w2)
        back_acc[at, :] += dot_nt(d_gate, w1_ref[:]) + dot_nt(d_lin, w3_ref[:])
        return carry

    lax.fori_loop(0, rows_ref.shape[0] // chunk, step, 0)


def up_grads(lhs_s, dg_s, dl_s, g1_away, g1_near, g3_away, g3_near):
    for slot in range(2):
        for ref, rel, grad in ((g1_away, 2 * slot + 1, dg_s), (g1_near, 2 * slot, dg_s), (g3_away, slot + 2, dl_s), (g3_near, slot, dl_s)):
            ref[slot] = dot_nn(lhs_s[rel], grad[:])


def expert_kernel(half, info, rows_ref, dd_ref, rows_t_ref, dd_t_ref, *refs):
    up_refs, down_refs, refs = refs[:8], refs[8:13], refs[13:]
    if half == 1:
        acc_in, refs = refs[:2], refs[2:]
    out_ref, back_ref, g1_away, g1_near, g3_away, g3_near, g2_away, g2_near = refs[:8]
    w1, w3, w2, act_s, dg_s, dl_s, out_acc, back_acc, lhs_s, sems = refs[8:]
    step, me = pl.program_id(0), info[0]
    same_y = (me // 2) == half
    pieces = [(ref.at[0], ref.at[1]) for ref in down_refs[:3]] + [[ref.at[0] for ref in down_refs[3:]]]
    w2_halves = [w2.at[pl.ds(part * 384, 384)] for part in range(2)]
    for rel, srcs in enumerate(pieces):
        @pl.when(jnp.logical_and(same_y == (rel < 2), (step == 0) == (rel % 2 == 1)))
        def _(srcs=srcs):
            for part, src in enumerate(srcs):
                pltpu.make_async_copy(src, w2_halves[part], sems.at[part]).start()

    @pl.when(step == 0)
    def _():
        if half == 1:
            out_acc[:] = acc_in[0][:]
            back_acc[:] = acc_in[1][:]
        else:
            out_acc[:] = jnp.zeros_like(out_acc)
            back_acc[:] = jnp.zeros_like(back_acc)
        for rel in range(4):
            lhs_s[rel] = rows_t_ref[pl.ds(pl.multiple_of((me ^ rel) * 192, 64), 192), :]

    for rel in range(4):
        at = pl.ds(pl.multiple_of((me ^ rel) * 192, 64), 192)
        w1[at, :] = up_refs[rel][0]
        w3[at, :] = up_refs[4 + rel][0]

    def wait_w2(idx):
        @pl.when(idx == 0)
        def _():
            for part, src in enumerate(pieces[0]):
                pltpu.make_async_copy(src, w2_halves[part], sems.at[part]).wait()

    ffn_rows(rows_ref, dd_ref, w1, w3, w2, False, wait_w2, act_s, dg_s, dl_s, out_acc, back_acc)
    up_grads(lhs_s, dg_s, dl_s, g1_away, g1_near, g3_away, g3_near)

    for near in range(2):
        @pl.when(step == near)
        def _(g2_ref=(g2_away, g2_near)[near]):
            for part in range(2):
                at = slice(part * 384, part * 384 + 384)
                g2_ref[at, :] = dot_nn(dd_t_ref[at, :], act_s[:])

    @pl.when(step == 1)
    def _():
        out_ref[:] = out_acc[:].astype(out_ref.dtype)
        back_ref[:] = back_acc[:].astype(back_ref.dtype)


def expert_half(half, rows, dd, rows_t, dd_t, up, down, acc):
    tok, dim = rows.shape
    y_me, x_me = lax.axis_index('y'), lax.axis_index('x')
    info = jnp.stack([2 * y_me + x_me, 2 * half + 1 - x_me, 2 * half + x_me]).astype(jnp.int32)
    whole, turned = fixed(tok, dim), fixed(dim, tok)

    def up_spec(mat):
        return pl.BlockSpec((1, dim // 4, dim), lambda step, info_ref, mat=mat: (mat, 0, info_ref[1 + step]))

    own, from_x, from_y, low, high = up
    up_args = (own, from_x, from_y, low, own, from_x, from_y, high)
    up_specs = [up_spec(0)] * 4 + [up_spec(1)] * 3 + [up_spec(0)]
    any_spec = pl.BlockSpec(memory_space=pl.ANY)
    row_out = pl.BlockSpec((2, dim // 4, dim), lambda step, info_ref: (0, 0, info_ref[1 + step] - 2 * half))
    square = fixed(dim, dim)
    acc_type = F32 if half == 0 else BF16
    row_shape, square_shape = jax.ShapeDtypeStruct((2, dim // 4, 2 * dim), F32), jax.ShapeDtypeStruct((dim, dim), F32)
    return pl.pallas_call(
        lambda *refs: expert_kernel(half, *refs),
        grid_spec=pltpu.PrefetchScalarGridSpec(
            num_scalar_prefetch=1, grid=(2,),
            in_specs=[whole, whole, turned, turned] + up_specs + [any_spec] * 5 + [whole] * len(acc),
            out_specs=[whole, whole] + [row_out] * 4 + [square] * 2,
            scratch_shapes=[pltpu.VMEM((dim, dim), BF16)] * 3 + [pltpu.VMEM((tok, dim), BF16)] * 3 + [pltpu.VMEM((tok, dim), F32)] * 2 + [pltpu.VMEM((4, dim // 4, tok), BF16), pltpu.SemaphoreType.DMA((2,))]),
        out_shape=[jax.ShapeDtypeStruct((tok, dim), acc_type)] * 2 + [row_shape] * 4 + [square_shape] * 2,
        compiler_params=pltpu.CompilerParams(vmem_limit_bytes=VMEM_LIMIT),
        cost_estimate=kernel_cost(36 * tok * dim * dim, dim * dim),
    )(info, rows, dd, rows_t, dd_t, *up_args, *down, *acc)


def shared_kernel(info, rows_ref, dd_ref, rows_t_ref, dd_t_ref, *refs):
    pieces, refs = [refs[5 * mat:5 * mat + 5] for mat in range(3)], refs[15:]
    out_ref, back_ref, g1_away, g1_near, g3_away, g3_near = refs[:6]
    g2_refs = refs[6:10]
    w1, w3, w2, act_s, dg_s, dl_s, lhs_s, dd_s = refs[10:]
    step, me, z_me = pl.program_id(0), info[0], info[1]

    def spot(rel, turn_z):
        return pl.ds(pl.multiple_of(((z_me ^ turn_z) * 4 + (me ^ rel)) * 48, 16), 48)

    @pl.when(step == 0)
    def _():
        out_ref[:] = jnp.zeros_like(out_ref)
        back_ref[:] = jnp.zeros_like(back_ref)
        for rel in range(4):
            for turn_z in range(4):
                lhs_s[rel, turn_z * 48:(turn_z + 1) * 48, :] = rows_t_ref[spot(rel, turn_z), :]
                dd_s[turn_z, rel * 48:(rel + 1) * 48, :] = dd_t_ref[spot(rel, turn_z), :]

    for w_ref, (own, from_x, from_y, low, high) in zip((w1, w3, w2), pieces):
        for turn_z in range(4):
            for rel, src in ((0, own.at[turn_z]), (1, from_x.at[turn_z]), (2, from_y.at[turn_z]), (3, low.at[turn_z] if turn_z < 2 else high.at[turn_z - 2])):
                w_ref[spot(rel, turn_z), :] = src[:]

    ffn_rows(rows_ref, dd_ref, w1, w3, w2, True, None, act_s, dg_s, dl_s, out_ref, back_ref)
    up_grads(lhs_s, dg_s, dl_s, g1_away, g1_near, g3_away, g3_near)
    for turn_z in range(4):
        g2_refs[turn_z][:] = dot_nn(dd_s[turn_z], act_s[:])


def shared_ffn(rows, dd, rows_t, dd_t, pieces):
    tok, dim = rows.shape
    width = pieces[0].shape[2] // 3
    steps = width // dim
    info = jnp.stack([2 * lax.axis_index('y') + lax.axis_index('x'), lax.axis_index('z')]).astype(jnp.int32)
    whole, turned = fixed(tok, dim), fixed(dim, tok)
    piece_specs = [pl.BlockSpec((piece.shape[0], 48, dim), lambda step, info_ref, mat=mat: (0, 0, mat * steps + step)) for mat in range(3) for piece in pieces]
    row_out = pl.BlockSpec((2, dim // 4, dim), lambda step, info_ref: (0, 0, step))
    z_out = pl.BlockSpec((dim // 4, dim), lambda step, info_ref: (0, step))
    return pl.pallas_call(
        shared_kernel,
        grid_spec=pltpu.PrefetchScalarGridSpec(
            num_scalar_prefetch=1, grid=(steps,),
            in_specs=[whole, whole, turned, turned] + piece_specs,
            out_specs=[whole, whole] + [row_out] * 4 + [z_out] * 4,
            scratch_shapes=[pltpu.VMEM((dim, dim), BF16)] * 3 + [pltpu.VMEM((tok, dim), BF16)] * 3 + [pltpu.VMEM((4, dim // 4, tok), BF16)] * 2),
        out_shape=[jax.ShapeDtypeStruct((tok, dim), F32)] * 2 + [jax.ShapeDtypeStruct((2, dim // 4, width), F32)] * 4 + [jax.ShapeDtypeStruct((dim // 4, width), F32)] * 4,
        compiler_params=pltpu.CompilerParams(vmem_limit_bytes=VMEM_LIMIT),
        cost_estimate=kernel_cost(18 * tok * dim * width, dim * width),
    )(info, rows, dd, rows_t, dd_t, *(list(pieces) * 3))


def z_sum(plane):
    summed = plane[0]
    for step in (1, 2, 3):
        summed = summed + z_hop(plane[step], step)
    return summed


def swap_rows(summed):
    halves = summed.reshape(summed.shape[:-2] + (2, -1, summed.shape[-1]))
    axis, c_me = halves.ndim - 3, lax.axis_index('c')
    return pick(halves, c_me, axis), hop(pick(halves, 1 - c_me, axis), 'c')


def plane_sum_values(total):
    y_me, x_me = lax.axis_index('y'), lax.axis_index('x')
    ways = tuple(zip((total[:2], total[2:]), ((2, x_me, y_me, 'x', 'y'), (1, y_me, x_me, 'y', 'x'))))
    gives = [pick(part, 1 - me_1, axis_1) for part, (axis_1, me_1, *_) in ways]

    def rest():
        planes = []
        for give, (part, (axis_1, me_1, me_2, name_1, name_2)) in zip(gives, ways):
            got, keep = hop(give, name_1), pick(part, me_1, axis_1)
            got_2 = hop(pick(keep, 1 - me_2, 1) + pick(got, 1 - me_2, 1), name_2)
            planes.append(pick(keep, me_2, 1) + pick(got, me_2, 1) + got_2)
        return jnp.concatenate(planes, axis=0)

    return gives, rest


def swap_experts(summed):
    return in_core_order(*(part[None] for part in swap_rows(summed)), 0)


def scatter_small(grad):
    sums = grad.reshape(4, 2, 2, 2, 24, -1)
    for axis, name in ((1, 'y'), (1, 'x'), (1, 'c')):
        me = lax.axis_index(name)
        sums = pick(sums, me, axis) + hop(pick(sums, 1 - me, axis), name)
    z_me = lax.axis_index('z')
    total = pick(sums, z_me, 0)
    for step in (1, 2, 3):
        total = total + z_hop(pick(sums, z_me ^ step, 0), step)
    return total


def layer_step(x_in, grad_y, w_q, w_k, w_v, w_o, gamma_attn, gamma_mlp, w_router, w1_shared, w3_shared, w2_shared, w1_expert, w3_expert, w2_expert, expert_ids):
    n_batch, seq_len, model_dim = x_in.shape
    n_tok = n_batch * seq_len
    n_heads, head_dim = w_q.shape[1], w_q.shape[2]
    att_dim, att_half = n_heads * head_dim, n_heads * head_dim // 2
    n_experts = w_router.shape[1]
    ff_half = w1_shared.shape[1] // 2
    capacity = 2 * n_tok // n_experts
    n_slots = n_experts * capacity

    att_parts = (w_q.reshape(-1, att_dim), w_k.reshape(-1, att_dim), w_v.reshape(-1, att_dim), w_o.reshape(att_dim, -1).T)
    att_block = jnp.concatenate([part[:, :att_half] for part in att_parts] + [part[:, att_half:] for part in att_parts], axis=1)
    small = jnp.concatenate([gamma_attn.astype(F32)[:, None], gamma_mlp.astype(F32)[:, None], w_router], axis=1)
    small = jnp.pad(small, ((0, 0), (0, 128 - small.shape[1])))
    up_chip, down_chip = expert_chips(w1_expert, w3_expert, w2_expert)
    att_all, small_all = gather_weights(att_block, small)
    att_all, small_all = att_all.reshape(model_dim, -1), small_all.reshape(model_dim, -1)
    att_w = jnp.split(att_all, 2, axis=1)
    ga_all, gm_all, wr_all = small_all[:, 0], small_all[:, 1], small_all[:, 2:2 + n_experts]
    down_first = plane_first(down_chip)
    up_first = plane_first(up_chip)
    sh_parts = z_stack((w1_shared, w3_shared, w2_shared.T))

    d_out = grad_y.reshape(n_tok, model_dim)
    onehot, dest_row = route_slots(expert_ids.reshape(n_tok), n_experts, capacity)
    place = (dest_row[:, None] == jnp.arange(n_slots)[None, :]).astype(BF16)

    def exchange(values):
        return lax.all_to_all(values.reshape(n_experts, capacity, model_dim), ('z', 'c'), 0, 0, tiled=True).reshape(n_slots, model_dim)

    def dispatch(values):
        return exchange(jnp.einsum('ts,td->sd', place, values, preferred_element_type=F32).astype(BF16))

    d_out_both = jnp.concatenate([d_out, hop(d_out, 'c')], axis=0)
    d_out_t = d_out_both.T
    cos_tab, sin_tab = rope_tables(seq_len, head_dim)

    tokens = x_in.reshape(n_tok, model_dim)
    normed1, norm1_pull = jax.vjp(rms_norm, tokens, ga_all)
    qkv = [dot32(normed1, w_half[:, :3 * att_half]).astype(BF16) for w_half in att_w]
    attn_parts = [attn_fwd(half, cos_tab, sin_tab) for half in qkv]
    wot = [w_half[:, 3 * att_half:] for w_half in att_w]
    attn_out = sum(jnp.einsum('tk,dk->td', part, w_half, preferred_element_type=F32) for part, w_half in zip(attn_parts, wot))
    hidden = (tokens.astype(F32) + attn_out).astype(BF16)
    normed2, norm2_pull = jax.vjp(rms_norm, hidden, gm_all)
    normed2_f = normed2.astype(F32)
    logits = jnp.dot(normed2, wr_all, preferred_element_type=F32, precision=lax.Precision.HIGHEST)
    gate_val = jax.nn.sigmoid(jnp.sum(jnp.where(onehot, logits, 0.0), axis=1))
    routed_in = (gate_val[:, None] * normed2_f).astype(BF16)
    rows = dispatch(routed_in)
    d_down = dispatch(after(d_out, routed_in))
    d_down_t = d_down.T

    normed2_both = jnp.concatenate([normed2, hop(normed2, 'c')], axis=0)
    sh_first = plane_first(jnp.stack([after(part, attn_parts[1]) for part in sh_parts]))
    sh_pieces = plane_pieces([after(piece, routed_in) for piece in sh_first])
    down_pieces = plane_pieces([after(piece, routed_in) for piece in down_first])
    up_pieces = plane_pieces([after(piece, routed_in) for piece in up_first])
    shared_part, d_part, s1_away, s1_near, s3_away, s3_near, *s2 = shared_ffn(normed2_both, d_out_both, normed2_both.T, d_out_t, sh_pieces)
    shared_out = shared_part[:n_tok] + hop(shared_part[n_tok:], 'c')
    d_normed2 = d_part[:n_tok] + hop(d_part[n_tok:], 'c')

    rows_t = rows.T
    *acc, a1_away, a1_near, a3_away, a3_near, a2_away, a2_near = expert_half(0, rows, d_down, rows_t, d_down_t, up_pieces, down_pieces, ())
    down_rows, d_rows, b1_away, b1_near, b3_away, b3_near, b2_away, b2_near = expert_half(1, rows, d_down, rows_t, d_down_t, up_pieces, down_pieces, acc)
    d_back = exchange(d_rows)

    def first_sum(away, near, axis, gate):
        keep, give = near + after(hop(away, axis), *gate)
        return keep, hop(give, 'y' if axis == 'x' else 'x')

    s1, s3 = first_sum(s1_away, s1_near, 'x', [d_rows]), first_sum(s3_away, s3_near, 'y', [d_rows])
    a1, a3 = first_sum(a1_away, a1_near, 'x', [d_rows]), first_sum(a3_away, a3_near, 'y', [d_rows])
    routed = jnp.einsum('ts,sd->td', place, exchange(down_rows), preferred_element_type=F32)
    layer_out = (hidden.astype(F32) + routed + shared_out).astype(BF16)

    d_routed_in = jnp.einsum('ts,sd->td', place, d_back, preferred_element_type=F32)
    d_normed2 = d_normed2 + gate_val[:, None] * d_routed_in
    d_gate_val = jnp.sum(d_routed_in * normed2_f, axis=1) * gate_val * (1.0 - gate_val)
    d_logits = jnp.where(onehot, d_gate_val[:, None], 0.0)
    g_wr = jnp.einsum('td,te->de', normed2_f, d_logits, precision=lax.Precision.HIGHEST)
    d_normed2 = d_normed2 + jnp.einsum('te,de->td', d_logits, wr_all, precision=lax.Precision.HIGHEST)
    d_hid_norm, g_gm = norm2_pull(d_normed2.astype(BF16))
    d_hidden = (d_out.astype(F32) + d_hid_norm.astype(F32)).astype(BF16)

    d_hidden_t, normed1_t = d_hidden.T, normed1.T
    d_qkv = [jnp.concatenate(attn_bwd(half, dot32(d_hidden, w_half).astype(BF16), cos_tab, sin_tab), axis=1) for half, w_half in zip(qkv, wot)]
    c_me = lax.axis_index('c')
    core_0 = c_me == 0

    def core_pick(pair):
        first, second = pair
        return jnp.where(core_0, first, second), jnp.where(core_0, second, first)

    g_att = []
    for lhs_t, pair in ((normed1_t, d_qkv), (d_hidden_t, attn_parts)):
        mine, other = core_pick(pair)
        g_att.append(dot32(lhs_t, mine) + hop(dot32(lhs_t, other), 'c'))
    att_gives, att_rest = plane_sum_values(jnp.concatenate(g_att, axis=1).reshape(4, 2, 2, 48, -1))

    def later(value):
        return after(value, *att_gives)

    s2_total = s2[0]
    for step in Z_STEPS:
        s2_total = s2_total + later(z_hop(s2[step], step))
    b1, b3 = first_sum(b1_away, b1_near, 'x', att_gives), first_sum(b3_away, b3_near, 'y', att_gives)
    low_y = lax.axis_index('y') == 0
    g2_sums = a2_near + later(hop(a2_away, 'x')), b2_near + later(hop(b2_away, 'x'))
    g2_low, g2_high = g2_sums
    g2_keep, g2_give = jnp.where(low_y, g2_low, g2_high), jnp.where(low_y, g2_high, g2_low)

    def finish(pairs):
        return jnp.concatenate([mine + later(got) for mine, got in pairs], axis=1)

    g_w1, g_w3 = finish((a1, b1)), finish((a3, b3))
    g_w2 = (g2_keep + hop(g2_give, 'y')).T
    s2_keep, s2_give = jnp.split(s2_total.reshape(2, 2, 48, -1), 2, axis=1)
    s2_keep, s2_give = s2_keep + hop(s2_give, 'x')
    g_s2 = (s2_keep + hop(s2_give, 'y')).reshape(48, -1)
    g_sh = jnp.concatenate([z_sum(finish((pair,)).reshape(4, 48, -1)) for pair in (s1, s3)] + [g_s2], axis=1)
    g_sh_mine, g_sh_other = swap_rows(g_sh)
    g_w2e = swap_experts(g_w2)
    g_up = swap_experts(jnp.stack([g_w1, g_w3]))
    z_me = lax.axis_index('z')
    att_plane = att_rest()
    g_att_mine, g_att_other = swap_rows(z_sum([pick(att_plane, z_me ^ step, 0) for step in range(4)]))
    d_normed1 = sum(jnp.einsum('tk,dk->td', half, w_half[:, :3 * att_half], preferred_element_type=F32) for half, w_half in zip(d_qkv, att_w))
    d_tok_norm, g_ga = norm1_pull(d_normed1.astype(BF16))
    d_x = (d_hidden.astype(F32) + d_tok_norm.astype(F32)).astype(BF16).reshape(n_batch, seq_len, model_dim)

    g_small = scatter_small(later(jnp.concatenate([g_ga[:, None], g_gm[:, None], g_wr, jnp.zeros((model_dim, 6), F32)], axis=1)))
    g_att = in_core_order(g_att_mine.reshape(-1, 4, att_half), g_att_other.reshape(-1, 4, att_half), 2)
    g_q, g_k, g_v = (g_att[:, part].reshape(-1, n_heads, head_dim) for part in range(3))
    g_wo = g_att[:, 3].T.reshape(n_heads, head_dim, -1)
    g_sh = in_core_order(g_sh_mine.reshape(-1, 3, ff_half), g_sh_other.reshape(-1, 3, ff_half), 2)
    return (layer_out.reshape(n_batch, seq_len, model_dim), d_x, g_q, g_k, g_v, g_wo, g_small[:, 0], g_small[:, 1], g_small[:, 2:2 + n_experts], g_sh[:, 0], g_sh[:, 1], g_sh[:, 2].T, g_up[:, 0], g_up[:, 1], g_w2e)


def solution(mesh):
    fine_mesh = Mesh(np.asarray(mesh.devices).reshape(4, 2, 2, 2), AXES)
    row_spec, wo_spec, w2s_spec, exp_spec = P(AXES), P(None, None, AXES), P(None, AXES), P('z', AXES[1:])
    weight_specs = (row_spec,) * 3 + (wo_spec,) + (row_spec,) * 5 + (w2s_spec,) + (exp_spec,) * 3
    out_specs = (row_spec, row_spec) + weight_specs
    in_specs = out_specs + (row_spec,)
    return jax.shard_map(layer_step, mesh=fine_mesh, in_specs=in_specs, out_specs=out_specs, check_vma=False)
```

profile of v0, /device:TPU:0, one launch (start us, length us, event | category | flops | bytes accessed | tf_op | source)
XLA Modules:
  0.0 1020.9 jit_solution(13072281940136895779)
XLA Ops:
  8.2 39.6 %shard_map.271 = (bf16[32,24,3072]{2,1,0:T(8,128)(2,1)}, f32[32,24,128]{2,1,0:T(8,128)}) custom-call(bf16[24,3072]{1,0:T(8,128)(2,1)} %copy-done.72, f32[24,128]{1,0:T(8,128)} %select_maximum_fusion.small_ref), custom_call_target="tpu_custom_call" | custom-call | flops 7372800000 | bytes 73728 | tf_op jit(solution)/shard_map/pallas_call | solution.py:287
  50.1 3.9 convolution_convert_fusion.1.q_ref.k_ref.v_ref
  54.0 3.8 convolution_convert_fusion.q_ref.k_ref.v_ref
  60.1 10.8 %shard_map.272 = bf16[512,384]{1,0:T(8,128)(2,1)} custom-call(bf16[512,1152]{1,0:T(8,128)(2,1)} %convolution_convert_fusion.1.q_ref.k_ref.v_ref, bf16[512,1152]{1,0:T(8,128)(2,1)} %convolution_convert_fusion.1.q_ref.k_ref.v_ref, bf16[512,1152]{1,0:T(8,128)(2,1)} %convolution_convert_fusion.1.q_ref.k_ref.v_ref, f32[512,128]{1,0:T(8,128)} %get-tuple-element.285.cos_ref, ...), custom_call_target="tpu_custom_call" | custom-call | flops 4026531840 | bytes 196608 | tf_op jit(solution)/shard_map/pallas_call | solution.py:152
  72.6 10.7 %shard_map.273 = bf16[512,384]{1,0:T(8,128)(2,1)} custom-call(bf16[512,1152]{1,0:T(8,128)(2,1)} %convolution_convert_fusion.q_ref.k_ref.v_ref, bf16[512,1152]{1,0:T(8,128)(2,1)} %convolution_convert_fusion.q_ref.k_ref.v_ref, bf16[512,1152]{1,0:T(8,128)(2,1)} %convolution_convert_fusion.q_ref.k_ref.v_ref, f32[512,128]{1,0:T(8,128)} %get-tuple-element.285.cos_ref, ...), custom_call_target="tpu_custom_call" | custom-call | flops 4026531840 | bytes 196608 | tf_op jit(solution)/shard_map/pallas_call | solution.py:152
  88.6 3.1 reduce-window.6
  100.9 6.8 all-to-all-start
  122.1 3.5 collective-permute-start.15
  128.0 3.0 convolution_convert_fusion.2
  133.6 14.7 %collective-permute-done.15 = bf16[48,4608]{1,0:T(8,128)(2,1)} collective-permute-done((bf16[48,4608]{1,0:T(8,128)(2,1)}, bf16[48,4608]{1,0:T(8,128)(2,1)}, u32[]{:S(2)}, u32[]{:S(2)}) %collective-permute-start.15) | collective-permute-done | bytes 442400 | tf_op jit(solution)/shard_map/ppermute | solution.py:183
  150.6 32.9 %collective-permute-done.14 = bf16[48,4608]{1,0:T(8,128)(2,1)} collective-permute-done((bf16[48,4608]{1,0:T(8,128)(2,1)}, bf16[48,4608]{1,0:T(8,128)(2,1)}, u32[]{:S(2)}, u32[]{:S(2)}) %collective-permute-start.14) | collective-permute-done | bytes 442400 | tf_op jit(solution)/shard_map/ppermute | solution.py:183
  183.6 4.5 all-to-all-start.1
  188.1 3.0 pad_maximum_fusion.6.refs_0_.refs_5_.refs_10_
  203.2 54.9 %collective-permute-done.6.refs_14_ = bf16[2,384,768]{2,1,0:T(8,128)(2,1)} collective-permute-done((bf16[2,384,768]{2,1,0:T(8,128)(2,1)}, bf16[2,384,768]{2,1,0:T(8,128)(2,1)}, u32[]{:S(2)}, u32[]{:S(2)}) %collective-permute-start.6) | collective-permute-done | bytes 1179680 | tf_op jit(solution)/shard_map/ppermute | solution.py:179
  260.2 3.2 fusion.130
  266.0 3.2 fusion.129
  281.8 3.5 fusion.127
  287.9 3.5 fusion.128
  298.0 39.7 %shard_map.274 = (f32[1024,768]{1,0:T(8,128)}, f32[1024,768]{1,0:T(8,128)}, f32[2,192,1536]{2,1,0:T(8,128)}, f32[2,192,1536]{2,1,0:T(8,128)}, f32[2,192,1536]{2,...) custom-call(s32[3]{0:T(128)} %get-tuple-element.288.refs_0_, ...), custom_call_target="tpu_custom_call" | custom-call | flops 21743271936 | bytes 589824 | tf_op jit(solution)/shard_map/pallas_call | solution.py:410
  337.8 41.0 %shard_map.275 = (bf16[1024,768]{1,0:T(8,128)(2,1)}, bf16[1024,768]{1,0:T(8,128)(2,1)}, f32[2,192,1536]{2,1,0:T(8,128)}, f32[2,192,1536]{2,1,0:T(8,128)}, f32[2,...) custom-call(s32[3]{0:T(128)} %get-tuple-element.287.refs_0_, ...), custom_call_target="tpu_custom_call" | custom-call | flops 21743271936 | bytes 589824 | tf_op jit(solution)/shard_map/pallas_call | solution.py:410
  378.8 4.8 all-to-all-start.3
  383.7 31.9 %shard_map.276 = (f32[1024,768]{1,0:T(8,128)}, f32[1024,768]{1,0:T(8,128)}, f32[2,192,1536]{2,1,0:T(8,128)}, f32[2,192,1536]{2,1,0:T(8,128)}, f32[2,192,1536]{2,...) custom-call(s32[2]{0:T(128)} %pad_add_fusion.2.info, ...), custom_call_target="tpu_custom_call" | custom-call | flops 21743271936 | bytes 1179648 | tf_op jit(solution)/shard_map/pallas_call | solution.py:462
  417.9 3.6 all-to-all-done.3
  421.5 4.5 all-to-all-start.2
  426.0 3.5 copy.181
  433.2 3.6 copy.179
  439.8 3.8 collective-permute-start.50
  443.6 26.0 %collective-permute-done.43 = f32[2,192,1536]{2,1,0:T(8,128)} collective-permute-done((f32[2,192,1536]{2,1,0:T(8,128)}, f32[2,192,1536]{2,1,0:T(8,128)}, u32[]{:S(2)}, u32[]{:S(2)}) %collective-permute-start.43) | collective-permute-done | bytes 2359328 | tf_op jit(solution)/shard_map/ppermute | solution.py:179
  476.0 4.2 add.359
  486.3 3.7 fusion.19
  490.0 24.9 %all-to-all-done.2 = bf16[8,128,768]{2,1,0:T(8,128)(2,1)} async-done(((bf16[8,128,768]{2,1,0:T(8,128)(2,1)}), bf16[8,128,768]{2,1,0:T(8,128)(2,1)}, u32[]{:S(2)}, u32[]{:S(2)}) %all-to-all-start.2) | async-done | bytes 1572896 | tf_op jit(solution)/shard_map/all_to_all | solution.py:548
  517.7 3.0 add_convert_fusion.2
  525.6 16.6 %shard_map.278 = (bf16[512,384]{1,0:T(8,128)(2,1)}, bf16[512,384]{1,0:T(8,128)(2,1)}, bf16[512,384]{1,0:T(8,128)(2,1)}) custom-call(bf16[512,1152]{1,0:T(8,128)(2,1)} %convolution_convert_fusion.q_ref.k_ref.v_ref, bf16[512,1152]{1,0:T(8,128)(2,1)} %convolution_convert_fusion.q_ref.k_ref.v_ref, bf16[512,1152]{1,0:T(8,128)(2,1)} %convolution_convert_fusion.q_ref.k_ref.v_ref, ...), custom_call_target="tpu_custom_call" | custom-call | flops 8053063680 | bytes 196608 | tf_op jit(solution)/shard_map/pallas_call | solution.py:163
  543.2 16.8 %shard_map.277 = (bf16[512,384]{1,0:T(8,128)(2,1)}, bf16[512,384]{1,0:T(8,128)(2,1)}, bf16[512,384]{1,0:T(8,128)(2,1)}) custom-call(bf16[512,1152]{1,0:T(8,128)(2,1)} %convolution_convert_fusion.1.q_ref.k_ref.v_ref, bf16[512,1152]{1,0:T(8,128)(2,1)} %convolution_convert_fusion.1.q_ref.k_ref.v_ref, ...), custom_call_target="tpu_custom_call" | custom-call | flops 8053063680 | bytes 196608 | tf_op jit(solution)/shard_map/pallas_call | solution.py:163
  561.9 3.2 fusion.53
  570.1 3.1 add.378
  579.0 2.9 fusion.20
  593.1 3.3 convolution_add_fusion
  601.4 17.2 %collective-permute-done.48 = f32[192,1536]{1,0:T(8,128)S(1)} collective-permute-done((f32[192,1536]{1,0:T(8,128)}, f32[192,1536]{1,0:T(8,128)S(1)}, u32[]{:S(2)}, u32[]{:S(2)}) %collective-permute-start.48) | collective-permute-done | bytes 1179680 | tf_op jit(solution)/shard_map/ppermute | solution.py:183
  619.4 26.5 %collective-permute-done.44 = f32[192,1536]{1,0:T(8,128)S(1)} collective-permute-done((f32[192,1536]{1,0:T(8,128)S(1)}, f32[192,1536]{1,0:T(8,128)S(1)}, u32[]{:S(2)}, u32[]{:S(2)}) %collective-permute-start.44) | collective-permute-done | bytes 1179680 | tf_op jit(solution)/shard_map/ppermute | solution.py:179
  650.2 3.3 add_add_fusion.2
  654.7 22.1 %collective-permute-done.39 = f32[192,1536]{1,0:T(8,128)} collective-permute-done((f32[192,1536]{1,0:T(8,128)S(1)}, f32[192,1536]{1,0:T(8,128)}, u32[]{:S(2)}, u32[]{:S(2)}) %collective-permute-start.39) | collective-permute-done | bytes 1179680 | tf_op jit(solution)/shard_map/ppermute | solution.py:179
  680.9 20.4 %collective-permute-done.55 = f32[192,1536]{1,0:T(8,128)} collective-permute-done((f32[192,1536]{1,0:T(8,128)}, f32[192,1536]{1,0:T(8,128)}, u32[]{:S(2)}, u32[]{:S(2)}) %collective-permute-start.55) | collective-permute-done | bytes 1179680 | tf_op jit(solution)/shard_map/ppermute | solution.py:179
  703.2 18.6 %collective-permute-done.59 = f32[192,1536]{1,0:T(8,128)} collective-permute-done((f32[192,1536]{1,0:T(8,128)}, f32[192,1536]{1,0:T(8,128)}, u32[]{:S(2)}, u32[]{:S(2)}) %collective-permute-start.59) | collective-permute-done | bytes 1179680 | tf_op jit(solution)/shard_map/ppermute | solution.py:179
  723.3 2.9 add.380
  735.8 36.6 %collective-permute-done.63 = f32[768,768]{1,0:T(8,128)} collective-permute-done((f32[768,768]{1,0:T(8,128)}, f32[768,768]{1,0:T(8,128)}, u32[]{:S(2)}, u32[]{:S(2)}) %collective-permute-start.63) | collective-permute-done | bytes 2359328 | tf_op jit(solution)/shard_map/ppermute | solution.py:179
  774.0 4.9 broadcast_select_fusion
  778.9 32.2 %collective-permute-done.33 = f32[4,2,24,16]{2,3,1,0:T(8,128)S(1)} collective-permute-done((f32[4,2,24,16]{2,3,1,0:T(8,128)S(1)}, f32[4,2,24,16]{2,3,1,0:T(8,128)S(1)}, u32[]{:S(2)}, u32[]{:S(2)}) %collective-permute-start.33) | collective-permute-done | bytes 12320 | tf_op jit(solution)/shard_map/ppermute | solution.py:179
  813.3 3.6 collective-permute-start.35
  818.7 3.7 collective-permute-start.45
  823.5 6.3 collective-permute-done.47
  831.1 13.3 %collective-permute-done.46 = f32[48,1536]{1,0:T(8,128)S(1)} collective-permute-done((f32[48,1536]{1,0:T(8,128)S(1)}, f32[48,1536]{1,0:T(8,128)S(1)}, u32[]{:S(2)}, u32[]{:S(2)}) %collective-permute-start.46) | collective-permute-done | bytes 294944 | tf_op jit(solution)/shard_map/ppermute | solution.py:183
  845.6 3.3 collective-permute-start.40
  849.0 7.1 collective-permute-done.42
  857.4 11.8 %collective-permute-done.41 = f32[48,1536]{1,0:T(8,128)S(1)} collective-permute-done((f32[48,1536]{1,0:T(8,128)S(1)}, f32[48,1536]{1,0:T(8,128)S(1)}, u32[]{:S(2)}, u32[]{:S(2)}) %collective-permute-start.41) | collective-permute-done | bytes 294944 | tf_op jit(solution)/shard_map/ppermute | solution.py:183
  871.5 17.0 %collective-permute-done.52 = f32[1,48,1536]{2,1,0:T(8,128)S(1)} collective-permute-done((f32[1,48,1536]{2,1,0:T(8,128)S(1)}, f32[1,48,1536]{2,1,0:T(8,128)S(1)}, u32[]{:S(2)}, u32[]{:S(2)}) %collective-permute-start.52) | collective-permute-done | bytes 294944 | tf_op jit(solution)/shard_map/ppermute | solution.py:179
  906.5 42.4 %collective-permute-done.25 = f32[2,48,1536]{2,1,0:T(8,128)} collective-permute-done((f32[2,48,1536]{2,1,0:T(8,128)S(1)}, f32[2,48,1536]{2,1,0:T(8,128)}, u32[]{:S(2)}, u32[]{:S(2)}) %collective-permute-start.25) | collective-permute-done | bytes 589856 | tf_op jit(solution)/shard_map/ppermute | solution.py:179
  954.2 10.5 %collective-permute-start.29 = (f32[48,1536]{1,0:T(8,128)S(1)}, f32[48,1536]{1,0:T(8,128)S(1)}, u32[]{:S(2)}, u32[]{:S(2)}) collective-permute-start(f32[48,1536]{1,0:T(8,128)S(1)} %get-tuple-element.251), channel_id=1, source_target_pairs={{0,16},{8,24},{16,0},{24,8},{1,17},{9,25},{17,1},{25,9},{2,18},{10... | collective-permute-start | bytes 884744 | tf_op jit(solution)/shard_map/ppermute | solution.py:183
  964.9 14.8 %collective-permute-done.29 = f32[48,1536]{1,0:T(8,128)S(1)} collective-permute-done((f32[48,1536]{1,0:T(8,128)S(1)}, f32[48,1536]{1,0:T(8,128)S(1)}, u32[]{:S(2)}, u32[]{:S(2)}) %collective-permute-start.29) | collective-permute-done | bytes 294944 | tf_op jit(solution)/shard_map/ppermute | solution.py:183
  986.9 6.6 add_bitcast_fusion
  993.5 4.1 reshape.279
  997.6 6.2 constant_dynamic-slice_fusion
  1003.8 4.7 copy.215
  1008.5 4.7 copy.194
  (440 shorter events, 221.3 us)
Async XLA Ops:
  100.9 82.6 %all-to-all-start = ((bf16[8,128,768]{1,2,0:T(8,128)(2,1)}), bf16[8,128,768]{1,2,0:T(8,128)(2,1)}, u32[]{:S(2)}, u32[]{:S(2)}) async-start(bf16[8,128,768]{1,2,0:T(8,128)(2,1)} %copy.167), calls=%async_computation | async-start | bytes 3145728 | tf_op jit(solution)/shard_map/all_to_all | solution.py:548
  113.2 13.8 %collective-permute-start.5 = (bf16[384,768]{1,0:T(8,128)(2,1)}, bf16[384,768]{1,0:T(8,128)(2,1)}, u32[]{:S(2)}, u32[]{:S(2)}) collective-permute-start(bf16[384,768]{1,0:T(8,128)(2,1)} %dynamic-slice_bitcast_fusion.2), channel_id=1, source_target_pairs={{0,1},{1,0},{2,3},{3,2},{4,5},{5,4},{6,7},{7,6},{8,9},{9,8},{10,11... | collective-permute-start | bytes 1769480 | tf_op jit(solution)/shard_map/ppermute | solution.py:179
  119.3 76.4 %collective-permute-start.1 = (bf16[2,192,3072]{2,1,0:T(8,128)(2,1)}, bf16[2,192,3072]{2,1,0:T(8,128)(2,1)}, u32[]{:S(2)}, u32[]{:S(2)}) collective-permute-start(bf16[2,192,3072]{2,1,0:T(8,128)(2,1)} %pad_maximum_fusion.2.refs_5_.refs_9_), channel_id=1, source_target_pairs={{0,2},{2,0},{1,3},{3,1},{4,6},{6,4},{5,7},{7,5},{8,10},{10,8},{9,1... | collective-permute-start | bytes 7077896 | tf_op jit(solution)/shard_map/ppermute | solution.py:179
  120.8 74.9 %collective-permute-start.2 = (bf16[2,192,3072]{2,1,0:T(8,128)(2,1)}, bf16[2,192,3072]{2,1,0:T(8,128)(2,1)}, u32[]{:S(2)}, u32[]{:S(2)}) collective-permute-start(bf16[2,192,3072]{2,1,0:T(8,128)(2,1)} %pad_maximum_fusion.2.refs_5_.refs_9_), channel_id=1, source_target_pairs={{0,4},{4,0},{1,5},{5,1},{2,6},{6,2},{3,7},{7,3},{8,12},{12,8},{9,1... | collective-permute-start | bytes 7077896 | tf_op jit(solution)/shard_map/ppermute | solution.py:179
  122.1 26.2 %collective-permute-start.15 = (bf16[48,4608]{1,0:T(8,128)(2,1)}, bf16[48,4608]{1,0:T(8,128)(2,1)}, u32[]{:S(2)}, u32[]{:S(2)}) collective-permute-start(bf16[48,4608]{1,0:T(8,128)(2,1)} %pad_maximum_fusion.11), channel_id=1, source_target_pairs={{0,24},{8,16},{16,8},{24,0},{1,25},{9,17},{17,9},{25,1},{2,26},{10... | collective-permute-start | bytes 1327112 | tf_op jit(solution)/shard_map/ppermute | solution.py:183
  127.0 56.6 %collective-permute-start.14 = (bf16[48,4608]{1,0:T(8,128)(2,1)}, bf16[48,4608]{1,0:T(8,128)(2,1)}, u32[]{:S(2)}, u32[]{:S(2)}) collective-permute-start(bf16[48,4608]{1,0:T(8,128)(2,1)} %pad_maximum_fusion.11), channel_id=1, source_target_pairs={{0,16},{8,24},{16,0},{24,8},{1,17},{9,25},{17,1},{25,9},{2,18},{10... | collective-permute-start | bytes 1327112 | tf_op jit(solution)/shard_map/ppermute | solution.py:183
  127.1 56.5 %collective-permute-start.13 = (bf16[48,4608]{1,0:T(8,128)(2,1)}, bf16[48,4608]{1,0:T(8,128)(2,1)}, u32[]{:S(2)}, u32[]{:S(2)}) collective-permute-start(bf16[48,4608]{1,0:T(8,128)(2,1)} %pad_maximum_fusion.11), channel_id=1, source_target_pairs={{0,8},{8,0},{16,24},{24,16},{1,9},{9,1},{17,25},{25,17},{2,10},{10... | collective-permute-start | bytes 1327112 | tf_op jit(solution)/shard_map/ppermute | solution.py:183
  148.3 45.9 %collective-permute-start.10 = (bf16[512,768]{0,1:T(8,128)(2,1)S(1)}, bf16[512,768]{0,1:T(8,128)(2,1)}, u32[]{:S(2)}, u32[]{:S(2)}) collective-permute-start(bf16[512,768]{0,1:T(8,128)(2,1)S(1)} %fusion.16), channel_id=1, source_target_pairs={{0,1},{1,0},{2,3},{3,2},{4,5},{5,4},{6,7},{7,6},{8,9},{9,8},{10,11... | collective-permute-start | bytes 2359304 | tf_op jit(solution)/shard_map/ppermute | solution.py:179
  183.6 104.3 %all-to-all-start.1 = ((bf16[8,128,768]{1,2,0:T(8,128)(2,1)}), bf16[8,128,768]{1,2,0:T(8,128)(2,1)}, u32[]{:S(2)}, u32[]{:S(2)}) async-start(bf16[8,128,768]{1,2,0:T(8,128)(2,1)} %copy.170), calls=%async_computation.1 | async-start | bytes 3145728 | tf_op jit(solution)/shard_map/all_to_all | solution.py:548
  191.1 84.3 %collective-permute-start.16 = (bf16[4,48,4608]{2,1,0:T(8,128)(2,1)}, bf16[4,48,4608]{2,1,0:T(8,128)(2,1)}, u32[]{:S(2)}, u32[]{:S(2)}) collective-permute-start(bf16[4,48,4608]{2,1,0:T(8,128)(2,1)} %pad_maximum_fusion.6.refs_0_.refs_5_.refs_10_), channel_id=1, source_target_pairs={{0,2},{2,0},{1,3},{3,1},{4,6},{6,4},{5,7},{7,5},{8,10},{10,8},{9,1... | collective-permute-start | bytes 5308424 | tf_op jit(solution)/shard_map/ppermute | solution.py:179
  192.6 84.4 %collective-permute-start.17 = (bf16[4,48,4608]{2,1,0:T(8,128)(2,1)}, bf16[4,48,4608]{2,1,0:T(8,128)(2,1)}, u32[]{:S(2)}, u32[]{:S(2)}) collective-permute-start(bf16[4,48,4608]{2,1,0:T(8,128)(2,1)} %pad_maximum_fusion.6.refs_0_.refs_5_.refs_10_), channel_id=1, source_target_pairs={{0,4},{4,0},{1,5},{5,1},{2,6},{6,2},{3,7},{7,3},{8,12},{12,8},{9,1... | collective-permute-start | bytes 5308424 | tf_op jit(solution)/shard_map/ppermute | solution.py:179
  194.2 64.0 %collective-permute-start.6 = (bf16[2,384,768]{2,1,0:T(8,128)(2,1)}, bf16[2,384,768]{2,1,0:T(8,128)(2,1)}, u32[]{:S(2)}, u32[]{:S(2)}) collective-permute-start(bf16[2,384,768]{2,1,0:T(8,128)(2,1)} %bitcast.25.refs_13_), channel_id=1, source_target_pairs={{0,2},{2,0},{1,3},{3,1},{4,6},{6,4},{5,7},{7,5},{8,10},{10,8},{9,1... | collective-permute-start | bytes 3538952 | tf_op jit(solution)/shard_map/ppermute | solution.py:179
  195.7 6.0 collective-permute-start.11
  195.7 76.1 %collective-permute-start.7 = (bf16[2,384,768]{2,1,0:T(8,128)(2,1)}, bf16[2,384,768]{2,1,0:T(8,128)(2,1)}, u32[]{:S(2)}, u32[]{:S(2)}) collective-permute-start(bf16[2,384,768]{2,1,0:T(8,128)(2,1)} %bitcast.25.refs_13_), channel_id=1, source_target_pairs={{0,4},{4,0},{1,5},{5,1},{2,6},{6,2},{3,7},{7,3},{8,12},{12,8},{9,1... | collective-permute-start | bytes 3538952 | tf_op jit(solution)/shard_map/ppermute | solution.py:179
  201.7 96.3 %collective-permute-start.3 = (bf16[1,192,3072]{2,1,0:T(8,128)(2,1)}, bf16[1,192,3072]{2,1,0:T(8,128)(2,1)}, u32[]{:S(2)}, u32[]{:S(2)}) collective-permute-start(bf16[1,192,3072]{2,1,0:T(8,128)(2,1)} %slice.184), channel_id=1, source_target_pairs={{0,2},{2,0},{1,3},{3,1},{4,6},{6,4},{5,7},{7,5},{8,10},{10,8},{9,1... | collective-permute-start | bytes 3538952 | tf_op jit(solution)/shard_map/ppermute | solution.py:179
  258.1 39.9 %collective-permute-start.4 = (bf16[1,192,3072]{2,1,0:T(8,128)(2,1)}, bf16[1,192,3072]{2,1,0:T(8,128)(2,1)}, u32[]{:S(2)}, u32[]{:S(2)}) collective-permute-start(bf16[1,192,3072]{2,1,0:T(8,128)(2,1)} %slice.185), channel_id=1, source_target_pairs={{0,4},{4,0},{1,5},{5,1},{2,6},{6,2},{3,7},{7,3},{8,12},{12,8},{9,1... | collective-permute-start | bytes 3538952 | tf_op jit(solution)/shard_map/ppermute | solution.py:179
  273.7 22.3 %collective-permute-start.8 = (bf16[1,384,768]{2,1,0:T(8,128)(2,1)}, bf16[1,384,768]{2,1,0:T(8,128)(2,1)}, u32[]{:S(2)}, u32[]{:S(2)}) collective-permute-start(bf16[1,384,768]{2,1,0:T(8,128)(2,1)} %slice.186), channel_id=1, source_target_pairs={{0,2},{2,0},{1,3},{3,1},{4,6},{6,4},{5,7},{7,5},{8,10},{10,8},{9,1... | collective-permute-start | bytes 1769480 | tf_op jit(solution)/shard_map/ppermute | solution.py:179
  275.4 22.7 %collective-permute-start.9 = (bf16[1,384,768]{2,1,0:T(8,128)(2,1)S(1)}, bf16[1,384,768]{2,1,0:T(8,128)(2,1)}, u32[]{:S(2)}, u32[]{:S(2)}) collective-permute-start(bf16[1,384,768]{2,1,0:T(8,128)(2,1)S(1)} %slice.187), channel_id=1, source_target_pairs={{0,4},{4,0},{1,5},{5,1},{2,6},{6,2},{3,7},{7,3},{8,12},{12,8},{9,1... | collective-permute-start | bytes 1769480 | tf_op jit(solution)/shard_map/ppermute | solution.py:179
  279.1 104.5 %collective-permute-start.18 = (bf16[2,48,4608]{2,1,0:T(8,128)(2,1)}, bf16[2,48,4608]{2,1,0:T(8,128)(2,1)}, u32[]{:S(2)}, u32[]{:S(2)}) collective-permute-start(bf16[2,48,4608]{2,1,0:T(8,128)(2,1)} %slice.188), channel_id=1, source_target_pairs={{0,2},{2,0},{1,3},{3,1},{4,6},{6,4},{5,7},{7,5},{8,10},{10,8},{9,1... | collective-permute-start | bytes 2654216 | tf_op jit(solution)/shard_map/ppermute | solution.py:179
  296.1 87.6 %collective-permute-start.19 = (bf16[2,48,4608]{2,1,0:T(8,128)(2,1)}, bf16[2,48,4608]{2,1,0:T(8,128)(2,1)}, u32[]{:S(2)}, u32[]{:S(2)}) collective-permute-start(bf16[2,48,4608]{2,1,0:T(8,128)(2,1)} %slice.189), channel_id=1, source_target_pairs={{0,4},{4,0},{1,5},{5,1},{2,6},{6,2},{3,7},{7,3},{8,12},{12,8},{9,1... | collective-permute-start | bytes 2654216 | tf_op jit(solution)/shard_map/ppermute | solution.py:179
  378.8 42.7 %all-to-all-start.3 = ((bf16[8,128,768]{2,1,0:T(8,128)(2,1)}), bf16[8,128,768]{2,1,0:T(8,128)(2,1)}, u32[]{:S(2)}, u32[]{:S(2)}) async-start(bf16[8,128,768]{2,1,0:T(8,128)(2,1)} %bitcast.308), calls=%async_computation.3 | async-start | bytes 3145728 | tf_op jit(solution)/shard_map/all_to_all | solution.py:548
  415.6 54.0 %collective-permute-start.43 = (f32[2,192,1536]{2,1,0:T(8,128)}, f32[2,192,1536]{2,1,0:T(8,128)}, u32[]{:S(2)}, u32[]{:S(2)}) collective-permute-start(f32[2,192,1536]{2,1,0:T(8,128)} %get-tuple-element.115), channel_id=1, source_target_pairs={{0,4},{4,0},{1,5},{5,1},{2,6},{6,2},{3,7},{7,3},{8,12},{12,8},{9,1... | collective-permute-start | bytes 7077896 | tf_op jit(solution)/shard_map/ppermute | solution.py:179
  417.0 55.2 %collective-permute-start.38 = (f32[2,192,1536]{2,1,0:T(8,128)}, f32[2,192,1536]{2,1,0:T(8,128)}, u32[]{:S(2)}, u32[]{:S(2)}) collective-permute-start(f32[2,192,1536]{2,1,0:T(8,128)} %get-tuple-element.111), channel_id=1, source_target_pairs={{0,2},{2,0},{1,3},{3,1},{4,6},{6,4},{5,7},{7,5},{8,10},{10,8},{9,1... | collective-permute-start | bytes 7077896 | tf_op jit(solution)/shard_map/ppermute | solution.py:179
  421.5 93.4 %all-to-all-start.2 = ((bf16[8,128,768]{2,1,0:T(8,128)(2,1)}), bf16[8,128,768]{2,1,0:T(8,128)(2,1)}, u32[]{:S(2)}, u32[]{:S(2)}) async-start(bf16[8,128,768]{2,1,0:T(8,128)(2,1)} %bitcast.307), calls=%async_computation.2 | async-start | bytes 3145728 | tf_op jit(solution)/shard_map/all_to_all | solution.py:548
  432.2 53.3 %collective-permute-start.21 = (f32[512,768]{0,1:T(8,128)}, f32[512,768]{0,1:T(8,128)}, u32[]{:S(2)}, u32[]{:S(2)}) collective-permute-start(f32[512,768]{0,1:T(8,128)} %slice.237), channel_id=1, source_target_pairs={{0,1},{1,0},{2,3},{3,2},{4,5},{5,4},{6,7},{7,6},{8,9},{9,8},{10,11... | collective-permute-start | bytes 4718600 | tf_op jit(solution)/shard_map/ppermute | solution.py:179
  439.7 77.9 %collective-permute-start.20 = (f32[512,768]{0,1:T(8,128)}, f32[512,768]{0,1:T(8,128)}, u32[]{:S(2)}, u32[]{:S(2)}) collective-permute-start(f32[512,768]{0,1:T(8,128)} %slice.235), channel_id=1, source_target_pairs={{0,1},{1,0},{2,3},{3,2},{4,5},{5,4},{6,7},{7,6},{8,9},{9,8},{10,11... | collective-permute-start | bytes 4718600 | tf_op jit(solution)/shard_map/ppermute | solution.py:179
  439.8 157.2 %collective-permute-start.50 = (f32[192,1536]{1,0:T(8,128)}, f32[192,1536]{1,0:T(8,128)}, u32[]{:S(2)}, u32[]{:S(2)}) collective-permute-start(f32[192,1536]{1,0:T(8,128)} %get-tuple-element.123), channel_id=1, source_target_pairs={{0,24},{8,16},{16,8},{24,0},{1,25},{9,17},{17,9},{25,1},{2,26},{10... | collective-permute-start | bytes 3538952 | tf_op jit(solution)/shard_map/ppermute | solution.py:183
  469.6 130.8 %collective-permute-start.49 = (f32[192,1536]{1,0:T(8,128)}, f32[192,1536]{1,0:T(8,128)}, u32[]{:S(2)}, u32[]{:S(2)}) collective-permute-start(f32[192,1536]{1,0:T(8,128)} %get-tuple-element.121), channel_id=1, source_target_pairs={{0,16},{8,24},{16,0},{24,8},{1,17},{9,25},{17,1},{25,9},{2,18},{10... | collective-permute-start | bytes 3538952 | tf_op jit(solution)/shard_map/ppermute | solution.py:183
  472.2 94.1 %collective-permute-start.54 = (f32[2,192,1536]{2,1,0:T(8,128)}, f32[2,192,1536]{2,1,0:T(8,128)}, u32[]{:S(2)}, u32[]{:S(2)}) collective-permute-start(f32[2,192,1536]{2,1,0:T(8,128)} %get-tuple-element.126), channel_id=1, source_target_pairs={{0,2},{2,0},{1,3},{3,1},{4,6},{6,4},{5,7},{7,5},{8,10},{10,8},{9,1... | collective-permute-start | bytes 7077896 | tf_op jit(solution)/shard_map/ppermute | solution.py:179
  485.5 82.2 %collective-permute-start.58 = (f32[2,192,1536]{2,1,0:T(8,128)}, f32[2,192,1536]{2,1,0:T(8,128)}, u32[]{:S(2)}, u32[]{:S(2)}) collective-permute-start(f32[2,192,1536]{2,1,0:T(8,128)} %get-tuple-element.134), channel_id=1, source_target_pairs={{0,4},{4,0},{1,5},{5,1},{2,6},{6,2},{3,7},{7,3},{8,12},{12,8},{9,1... | collective-permute-start | bytes 7077896 | tf_op jit(solution)/shard_map/ppermute | solution.py:179
  565.1 27.2 %collective-permute-start.22 = (f32[768,1152]{1,0:T(8,128)}, f32[768,1152]{1,0:T(8,128)}, u32[]{:S(2)}, u32[]{:S(2)}) collective-permute-start(f32[768,1152]{1,0:T(8,128)} %fusion.53), channel_id=1, source_target_pairs={{0,1},{1,0},{2,3},{3,2},{4,5},{5,4},{6,7},{7,6},{8,9},{9,8},{10,11... | collective-permute-start | bytes 10616840 | tf_op jit(solution)/shard_map/ppermute | solution.py:179
  566.2 80.9 %collective-permute-start.56 = (f32[2,192,1536]{2,1,0:T(8,128)}, f32[2,192,1536]{2,1,0:T(8,128)}, u32[]{:S(2)}, u32[]{:S(2)}) collective-permute-start(f32[2,192,1536]{2,1,0:T(8,128)} %get-tuple-element.130), channel_id=1, source_target_pairs={{0,2},{2,0},{1,3},{3,1},{4,6},{6,4},{5,7},{7,5},{8,10},{10,8},{9,1... | collective-permute-start | bytes 7077896 | tf_op jit(solution)/shard_map/ppermute | solution.py:179
  577.5 12.7 %collective-permute-start.23 = (f32[768,384]{1,0:T(8,128)}, f32[768,384]{1,0:T(8,128)}, u32[]{:S(2)}, u32[]{:S(2)}) collective-permute-start(f32[768,384]{1,0:T(8,128)} %fusion.72), channel_id=1, source_target_pairs={{0,1},{1,0},{2,3},{3,2},{4,5},{5,4},{6,7},{7,6},{8,9},{9,8},{10,11... | collective-permute-start | bytes 3538952 | tf_op jit(solution)/shard_map/ppermute | solution.py:179
  590.2 28.4 %collective-permute-start.48 = (f32[192,1536]{1,0:T(8,128)}, f32[192,1536]{1,0:T(8,128)S(1)}, u32[]{:S(2)}, u32[]{:S(2)}) collective-permute-start(f32[192,1536]{1,0:T(8,128)} %get-tuple-element.119), channel_id=1, source_target_pairs={{0,8},{8,0},{16,24},{24,16},{1,9},{9,1},{17,25},{25,17},{2,10},{10... | collective-permute-start | bytes 3538952 | tf_op jit(solution)/shard_map/ppermute | solution.py:183
  592.3 53.6 %collective-permute-start.44 = (f32[192,1536]{1,0:T(8,128)S(1)}, f32[192,1536]{1,0:T(8,128)S(1)}, u32[]{:S(2)}, u32[]{:S(2)}) collective-permute-start(f32[192,1536]{1,0:T(8,128)S(1)} %copy-done.43), channel_id=1, source_target_pairs={{0,2},{2,0},{1,3},{3,1},{4,6},{6,4},{5,7},{7,5},{8,10},{10,8},{9,1... | collective-permute-start | bytes 3538952 | tf_op jit(solution)/shard_map/ppermute | solution.py:179
  597.0 105.4 %collective-permute-start.60 = (f32[2,192,1536]{2,1,0:T(8,128)}, f32[2,192,1536]{2,1,0:T(8,128)}, u32[]{:S(2)}, u32[]{:S(2)}) collective-permute-start(f32[2,192,1536]{2,1,0:T(8,128)} %get-tuple-element.138), channel_id=1, source_target_pairs={{0,4},{4,0},{1,5},{5,1},{2,6},{6,2},{3,7},{7,3},{8,12},{12,8},{9,1... | collective-permute-start | bytes 7077896 | tf_op jit(solution)/shard_map/ppermute | solution.py:179
  600.5 135.3 %collective-permute-start.64 = (f32[768,768]{1,0:T(8,128)}, f32[768,768]{1,0:T(8,128)}, u32[]{:S(2)}, u32[]{:S(2)}) collective-permute-start(f32[768,768]{1,0:T(8,128)} %get-tuple-element.145), channel_id=1, source_target_pairs={{0,2},{2,0},{1,3},{3,1},{4,6},{6,4},{5,7},{7,5},{8,10},{10,8},{9,1... | collective-permute-start | bytes 7077896 | tf_op jit(solution)/shard_map/ppermute | solution.py:179
  618.6 58.2 %collective-permute-start.39 = (f32[192,1536]{1,0:T(8,128)S(1)}, f32[192,1536]{1,0:T(8,128)}, u32[]{:S(2)}, u32[]{:S(2)}) collective-permute-start(f32[192,1536]{1,0:T(8,128)S(1)} %copy-done.44), channel_id=1, source_target_pairs={{0,4},{4,0},{1,5},{5,1},{2,6},{6,2},{3,7},{7,3},{8,12},{12,8},{9,1... | collective-permute-start | bytes 3538952 | tf_op jit(solution)/shard_map/ppermute | solution.py:179
  645.8 55.5 %collective-permute-start.55 = (f32[192,1536]{1,0:T(8,128)}, f32[192,1536]{1,0:T(8,128)}, u32[]{:S(2)}, u32[]{:S(2)}) collective-permute-start(f32[192,1536]{1,0:T(8,128)} %slice_bitcast_fusion.6), channel_id=1, source_target_pairs={{0,4},{4,0},{1,5},{5,1},{2,6},{6,2},{3,7},{7,3},{8,12},{12,8},{9,1... | collective-permute-start | bytes 3538952 | tf_op jit(solution)/shard_map/ppermute | solution.py:179
  647.2 74.6 %collective-permute-start.59 = (f32[192,1536]{1,0:T(8,128)}, f32[192,1536]{1,0:T(8,128)}, u32[]{:S(2)}, u32[]{:S(2)}) collective-permute-start(f32[192,1536]{1,0:T(8,128)} %slice_bitcast_fusion.2), channel_id=1, source_target_pairs={{0,2},{2,0},{1,3},{3,1},{4,6},{6,4},{5,7},{7,5},{8,10},{10,8},{9,1... | collective-permute-start | bytes 3538952 | tf_op jit(solution)/shard_map/ppermute | solution.py:179
  676.8 95.5 %collective-permute-start.63 = (f32[768,768]{1,0:T(8,128)}, f32[768,768]{1,0:T(8,128)}, u32[]{:S(2)}, u32[]{:S(2)}) collective-permute-start(f32[768,768]{1,0:T(8,128)} %get-tuple-element.142), channel_id=1, source_target_pairs={{0,2},{2,0},{1,3},{3,1},{4,6},{6,4},{5,7},{7,5},{8,10},{10,8},{9,1... | collective-permute-start | bytes 7077896 | tf_op jit(solution)/shard_map/ppermute | solution.py:179
  701.4 190.5 %collective-permute-start.24 = (f32[2,2,48,1536]{3,2,1,0:T(8,128)}, f32[2,2,48,1536]{3,2,1,0:T(8,128)}, u32[]{:S(2)}, u32[]{:S(2)}) collective-permute-start(f32[2,2,48,1536]{3,2,1,0:T(8,128)} %dynamic-slice_bitcast_fusion.1), channel_id=1, source_target_pairs={{0,2},{2,0},{1,3},{3,1},{4,6},{6,4},{5,7},{7,5},{8,10},{10,8},{9,1... | collective-permute-start | bytes 3538952 | tf_op jit(solution)/shard_map/ppermute | solution.py:179
  702.4 69.9 %collective-permute-start.32 = (f32[4,2,2,24,16]{3,4,2,1,0:T(8,128)S(1)}, f32[4,2,2,24,16]{3,4,2,1,0:T(8,128)S(1)}, u32[]{:S(2)}, u32[]{:S(2)}) collective-permute-start(f32[4,2,2,24,16]{3,4,2,1,0:T(8,128)S(1)} %bitcast.336), channel_id=1, source_target_pairs={{0,4},{4,0},{1,5},{5,1},{2,6},{6,2},{3,7},{7,3},{8,12},{12,8},{9,1... | collective-permute-start | bytes 73736 | tf_op jit(solution)/shard_map/ppermute | solution.py:179
  721.8 123.8 %collective-permute-start.51 = (f32[2,1,48,1536]{3,2,1,0:T(8,128)S(1)}, f32[2,1,48,1536]{3,2,1,0:T(8,128)S(1)}, u32[]{:S(2)}, u32[]{:S(2)}) collective-permute-start(f32[2,1,48,1536]{3,2,1,0:T(8,128)S(1)} %split.11), channel_id=1, source_target_pairs={{0,2},{2,0},{1,3},{3,1},{4,6},{6,4},{5,7},{7,5},{8,10},{10,8},{9,1... | collective-permute-start | bytes 1769480 | tf_op jit(solution)/shard_map/ppermute | solution.py:179
  772.4 38.7 %collective-permute-start.33 = (f32[4,2,24,16]{2,3,1,0:T(8,128)S(1)}, f32[4,2,24,16]{2,3,1,0:T(8,128)S(1)}, u32[]{:S(2)}, u32[]{:S(2)}) collective-permute-start(f32[4,2,24,16]{2,3,1,0:T(8,128)S(1)} %dynamic-slice_bitcast_fusion.7), channel_id=1, source_target_pairs={{0,2},{2,0},{1,3},{3,1},{4,6},{6,4},{5,7},{7,5},{8,10},{10,8},{9,1... | collective-permute-start | bytes 36872 | tf_op jit(solution)/shard_map/ppermute | solution.py:179
  818.0 11.8 %collective-permute-start.47 = (f32[48,1536]{1,0:T(8,128)S(1)}, f32[48,1536]{1,0:T(8,128)S(1)}, u32[]{:S(2)}, u32[]{:S(2)}) collective-permute-start(f32[48,1536]{1,0:T(8,128)S(1)} %get-tuple-element.248), channel_id=1, source_target_pairs={{0,24},{8,16},{16,8},{24,0},{1,25},{9,17},{17,9},{25,1},{2,26},{10... | collective-permute-start | bytes 884744 | tf_op jit(solution)/shard_map/ppermute | solution.py:183
  818.7 25.6 %collective-permute-start.46 = (f32[48,1536]{1,0:T(8,128)S(1)}, f32[48,1536]{1,0:T(8,128)S(1)}, u32[]{:S(2)}, u32[]{:S(2)}) collective-permute-start(f32[48,1536]{1,0:T(8,128)S(1)} %get-tuple-element.249), channel_id=1, source_target_pairs={{0,16},{8,24},{16,0},{24,8},{1,17},{9,25},{17,1},{25,9},{2,18},{10... | collective-permute-start | bytes 884744 | tf_op jit(solution)/shard_map/ppermute | solution.py:183
  818.7 26.8 %collective-permute-start.45 = (f32[48,1536]{1,0:T(8,128)S(1)}, f32[48,1536]{1,0:T(8,128)S(1)}, u32[]{:S(2)}, u32[]{:S(2)}) collective-permute-start(f32[48,1536]{1,0:T(8,128)S(1)} %get-tuple-element.247), channel_id=1, source_target_pairs={{0,8},{8,0},{16,24},{24,16},{1,9},{9,1},{17,25},{25,17},{2,10},{10... | collective-permute-start | bytes 884744 | tf_op jit(solution)/shard_map/ppermute | solution.py:183
  829.8 63.4 %collective-permute-start.26 = (f32[2,2,48,1536]{3,2,1,0:T(8,128)}, f32[2,2,48,1536]{3,2,1,0:T(8,128)}, u32[]{:S(2)}, u32[]{:S(2)}) collective-permute-start(f32[2,2,48,1536]{3,2,1,0:T(8,128)} %dynamic-slice_bitcast_fusion), channel_id=1, source_target_pairs={{0,4},{4,0},{1,5},{5,1},{2,6},{6,2},{3,7},{7,3},{8,12},{12,8},{9,1... | collective-permute-start | bytes 3538952 | tf_op jit(solution)/shard_map/ppermute | solution.py:179
  844.3 11.8 %collective-permute-start.42 = (f32[48,1536]{1,0:T(8,128)S(1)}, f32[48,1536]{1,0:T(8,128)S(1)}, u32[]{:S(2)}, u32[]{:S(2)}) collective-permute-start(f32[48,1536]{1,0:T(8,128)S(1)} %get-tuple-element.245), channel_id=1, source_target_pairs={{0,24},{8,16},{16,8},{24,0},{1,25},{9,17},{17,9},{25,1},{2,26},{10... | collective-permute-start | bytes 884744 | tf_op jit(solution)/shard_map/ppermute | solution.py:183
  845.5 23.7 %collective-permute-start.41 = (f32[48,1536]{1,0:T(8,128)S(1)}, f32[48,1536]{1,0:T(8,128)S(1)}, u32[]{:S(2)}, u32[]{:S(2)}) collective-permute-start(f32[48,1536]{1,0:T(8,128)S(1)} %get-tuple-element.246), channel_id=1, source_target_pairs={{0,16},{8,24},{16,0},{24,8},{1,17},{9,25},{17,1},{25,9},{2,18},{10... | collective-permute-start | bytes 884744 | tf_op jit(solution)/shard_map/ppermute | solution.py:183
  845.6 25.1 %collective-permute-start.40 = (f32[48,1536]{1,0:T(8,128)S(1)}, f32[48,1536]{1,0:T(8,128)S(1)}, u32[]{:S(2)}, u32[]{:S(2)}) collective-permute-start(f32[48,1536]{1,0:T(8,128)S(1)} %get-tuple-element.244), channel_id=1, source_target_pairs={{0,8},{8,0},{16,24},{24,16},{1,9},{9,1},{17,25},{25,17},{2,10},{10... | collective-permute-start | bytes 884744 | tf_op jit(solution)/shard_map/ppermute | solution.py:183
  856.1 40.0 %collective-permute-start.57 = (f32[192,1536]{1,0:T(8,128)}, f32[192,1536]{1,0:T(8,128)}, u32[]{:S(2)}, u32[]{:S(2)}) collective-permute-start(f32[192,1536]{1,0:T(8,128)} %slice_bitcast_fusion.4), channel_id=1, source_target_pairs={{0,4},{4,0},{1,5},{5,1},{2,6},{6,2},{3,7},{7,3},{8,12},{12,8},{9,1... | collective-permute-start | bytes 3538952 | tf_op jit(solution)/shard_map/ppermute | solution.py:179
  869.2 29.9 %collective-permute-start.61 = (f32[192,1536]{1,0:T(8,128)}, f32[192,1536]{1,0:T(8,128)}, u32[]{:S(2)}, u32[]{:S(2)}) collective-permute-start(f32[192,1536]{1,0:T(8,128)} %slice_bitcast_fusion), channel_id=1, source_target_pairs={{0,2},{2,0},{1,3},{3,1},{4,6},{6,4},{5,7},{7,5},{8,10},{10,8},{9,1... | collective-permute-start | bytes 3538952 | tf_op jit(solution)/shard_map/ppermute | solution.py:179
  870.7 17.8 %collective-permute-start.52 = (f32[1,48,1536]{2,1,0:T(8,128)S(1)}, f32[1,48,1536]{2,1,0:T(8,128)S(1)}, u32[]{:S(2)}, u32[]{:S(2)}) collective-permute-start(f32[1,48,1536]{2,1,0:T(8,128)S(1)} %slice_bitcast_fusion.12), channel_id=1, source_target_pairs={{0,4},{4,0},{1,5},{5,1},{2,6},{6,2},{3,7},{7,3},{8,12},{12,8},{9,1... | collective-permute-start | bytes 884744 | tf_op jit(solution)/shard_map/ppermute | solution.py:179
  888.5 98.4 %collective-permute-start.65 = (f32[768,768]{1,0:T(8,128)}, f32[768,768]{1,0:T(8,128)}, u32[]{:S(2)}, u32[]{:S(2)}) collective-permute-start(f32[768,768]{1,0:T(8,128)} %broadcast_select_fusion), channel_id=1, source_target_pairs={{0,4},{4,0},{1,5},{5,1},{2,6},{6,2},{3,7},{7,3},{8,12},{12,8},{9,1... | collective-permute-start | bytes 7077896 | tf_op jit(solution)/shard_map/ppermute | solution.py:179
  891.9 12.5 %collective-permute-start.53 = (f32[24,4608]{1,0:T(8,128)}, f32[24,4608]{1,0:T(8,128)}, u32[]{:S(2)}, u32[]{:S(2)}) collective-permute-start(f32[24,4608]{1,0:T(8,128)} %get-tuple-element.254), channel_id=1, source_target_pairs={{0,1},{1,0},{2,3},{3,2},{4,5},{5,4},{6,7},{7,6},{8,9},{9,8},{10,11... | collective-permute-start | bytes 1327112 | tf_op jit(solution)/shard_map/ppermute | solution.py:179
  893.2 55.7 %collective-permute-start.25 = (f32[2,48,1536]{2,1,0:T(8,128)S(1)}, f32[2,48,1536]{2,1,0:T(8,128)}, u32[]{:S(2)}, u32[]{:S(2)}) collective-permute-start(f32[2,48,1536]{2,1,0:T(8,128)S(1)} %bitcast_add_fusion.2), channel_id=1, source_target_pairs={{0,4},{4,0},{1,5},{5,1},{2,6},{6,2},{3,7},{7,3},{8,12},{12,8},{9,1... | collective-permute-start | bytes 1769480 | tf_op jit(solution)/shard_map/ppermute | solution.py:179
  896.2 54.2 %collective-permute-start.27 = (f32[2,48,1536]{2,1,0:T(8,128)}, f32[2,48,1536]{2,1,0:T(8,128)}, u32[]{:S(2)}, u32[]{:S(2)}) collective-permute-start(f32[2,48,1536]{2,1,0:T(8,128)} %bitcast_add_fusion), channel_id=1, source_target_pairs={{0,2},{2,0},{1,3},{3,1},{4,6},{6,4},{5,7},{7,5},{8,10},{10,8},{9,1... | collective-permute-start | bytes 1769480 | tf_op jit(solution)/shard_map/ppermute | solution.py:179
  904.4 109.3 %collective-permute-start.62 = (f32[2,96,3072]{2,1,0:T(8,128)}, f32[2,96,3072]{2,1,0:T(8,128)}, u32[]{:S(2)}, u32[]{:S(2)}) collective-permute-start(f32[2,96,3072]{2,1,0:T(8,128)} %fusion.4), channel_id=1, source_target_pairs={{0,1},{1,0},{2,3},{3,2},{4,5},{5,4},{6,7},{7,6},{8,9},{9,8},{10,11... | collective-permute-start | bytes 7077896 | tf_op jit(solution)/shard_map/ppermute | solution.py:179
  952.2 12.8 %collective-permute-start.30 = (f32[48,1536]{1,0:T(8,128)S(1)}, f32[48,1536]{1,0:T(8,128)S(1)}, u32[]{:S(2)}, u32[]{:S(2)}) collective-permute-start(f32[48,1536]{1,0:T(8,128)S(1)} %get-tuple-element.252), channel_id=1, source_target_pairs={{0,24},{8,16},{16,8},{24,0},{1,25},{9,17},{17,9},{25,1},{2,26},{10... | collective-permute-start | bytes 884744 | tf_op jit(solution)/shard_map/ppermute | solution.py:183
  954.2 25.5 %collective-permute-start.29 = (f32[48,1536]{1,0:T(8,128)S(1)}, f32[48,1536]{1,0:T(8,128)S(1)}, u32[]{:S(2)}, u32[]{:S(2)}) collective-permute-start(f32[48,1536]{1,0:T(8,128)S(1)} %get-tuple-element.251), channel_id=1, source_target_pairs={{0,16},{8,24},{16,0},{24,8},{1,17},{9,25},{17,1},{25,9},{2,18},{10... | collective-permute-start | bytes 884744 | tf_op jit(solution)/shard_map/ppermute | solution.py:183
  964.7 15.0 %collective-permute-start.28 = (f32[48,1536]{1,0:T(8,128)S(1)}, f32[48,1536]{1,0:T(8,128)S(1)}, u32[]{:S(2)}, u32[]{:S(2)}) collective-permute-start(f32[48,1536]{1,0:T(8,128)S(1)} %get-tuple-element.250), channel_id=1, source_target_pairs={{0,8},{8,0},{16,24},{24,16},{1,9},{9,1},{17,25},{25,17},{2,10},{10... | collective-permute-start | bytes 884744 | tf_op jit(solution)/shard_map/ppermute | solution.py:183
  1013.2 5.7 collective-permute-start.66
  (85 other events, 723.6 us)
where the time goes:
time: 1030 us; the launch traced here: 1020 us
  waiting for transfers between devices  448 us (43%)
  Pallas kernels  207 us (20%)
  local copies, waits for them, and re-layouts  115 us (11%)
  other arithmetic  105 us (10%)
  starting transfers between devices  99.5 us (10%)
  matrix products  43.8 us (4%)
    ppermute x49, waiting for transfers between devices, hop(): return lax.ppermute(block, axis, SWAP)  301 us
    ppermute x18, waiting for transfers between devices, z_hop(): lax.ppermute(block, 'z', [(z_idx, z_idx ^ step) for z_idx in range(4)])  119 us
    pallas_call x2, Pallas kernels, expert_half(): pl.pallas_call(lambda *refs: expert_kernel(half, *refs), grid_spec=pltpu....  80.7 us
    ppermute x49, starting transfers between devices, hop(): return lax.ppermute(block, axis, SWAP)  42.2 us
    pallas_call x1, Pallas kernels, gather_weights(): pl.pallas_call(weight_kernel, in_specs=[any_spec] * 2, out_specs=[any_spe...  39.6 us
    ppermute x18, starting transfers between devices, z_hop(): lax.ppermute(block, 'z', [(z_idx, z_idx ^ step) for z_idx in range(4)])  36.7 us
    pallas_call x2, Pallas kernels, attn_bwd(): pl.pallas_call(attn_bwd_kernel, grid=(width // 128,), in_specs=head_specs...  33.4 us
    pallas_call x1, Pallas kernels, shared_ffn(): pl.pallas_call(shared_kernel, grid_spec=pltpu.PrefetchScalarGridSpec(num_...  31.9 us
  transfers between devices with their start and end apart: 71, of which 25 were waited for; matrix products, arithmetic and copies ran while one was open for 21% of the time, Pallas kernels for 14%

commit v1 on v0

--- a/solution.py
+++ b/solution.py
@@ -6,6 +6,9 @@
 from jax.experimental.pallas import tpu as pltpu
 from jax.sharding import Mesh, PartitionSpec as P
 
+LANES = 128
+ROWS = 48
+QUAD = 4
 EPS_NORM = 1e-5
 EPS_QK = 1e-6
 ROPE_BASE = 500000.0
@@ -26,14 +29,15 @@
 
 def rope_tables(seq_len, head_dim):
     half_dim = head_dim // 2
-    inv_freq = ROPE_BASE ** (-(jnp.arange(half_dim, dtype=F32) * 2.0 / head_dim))
-    angles = jnp.arange(seq_len, dtype=F32)[:, None] * inv_freq[None, :]
-    cos_tab, sin_tab = jnp.cos(angles), jnp.sin(angles)
-    return jnp.concatenate([cos_tab] * 4, axis=1), jnp.concatenate([-sin_tab, sin_tab] * 2, axis=1)
+    steps = np.arange(half_dim, dtype=np.float32) * np.float32(2.0 / head_dim)
+    inv_freq = np.power(np.float32(ROPE_BASE), -steps)
+    angles = np.arange(seq_len, dtype=np.float32)[:, None] * inv_freq[None, :]
+    cos_tab, sin_tab = np.cos(angles), np.sin(angles)
+    return jnp.asarray(np.tile(cos_tab, (1, 4))), jnp.asarray(np.tile(np.concatenate([-sin_tab, sin_tab], axis=1), (1, 2)))
 
 
 def lane_masks(rows):
-    lane = lax.broadcasted_iota(jnp.int32, (rows, 128), 1)
+    lane = lax.broadcasted_iota(jnp.int32, (rows, LANES), 1)
     return lane % 64 < 32, lane < 64
 
 
@@ -95,7 +99,7 @@
         o_ref[start:keys, :] = jnp.where(head_a[:QUERY_BLOCK], outs[0], outs[1]).astype(BF16)
 
 
-def attn_bwd_kernel(q_ref, k_ref, v_ref, do_ref, cos_ref, sin_ref, dq_ref, dk_ref, dv_ref):
+def attn_bwd_kernel(q_ref, k_ref, v_ref, do_ref, cos_ref, sin_ref, d_ref):
     seq = q_ref.shape[0]
     low_half, head_a = lane_masks(seq)
     cos_tab, sin_tab = cos_ref[:], sin_ref[:]
@@ -120,15 +124,40 @@
             dk_part = dot_tn(d_scores, q_head[start:keys])
             dv_part = dot_tn(probs.astype(BF16), do_head[start:keys])
             if keys < seq:
-                pad = jnp.zeros((seq - keys, 128), F32)
+                pad = jnp.zeros((seq - keys, LANES), F32)
                 dk_part, dv_part = jnp.concatenate([dk_part, pad]), jnp.concatenate([dv_part, pad])
             dk_sum = dk_part if dk_sum is None else dk_sum + dk_part
             dv_sum = dv_part if dv_sum is None else dv_sum + dv_part
         grads.append((jnp.concatenate(dq_rows), dk_sum, dv_sum))
     d_q, d_k, d_v = (jnp.where(head_a, part_a, part_b) for part_a, part_b in zip(*grads))
-    dq_ref[:] = rope_norm_back(d_q, q_raw, q_inv, cos_tab, sin_tab, low_half, head_a)
-    dk_ref[:] = rope_norm_back(d_k, k_raw, k_inv, cos_tab, sin_tab, low_half, head_a)
-    dv_ref[:] = d_v.astype(BF16)
+    rotary = (cos_tab, sin_tab, low_half, head_a)
+    parts = rope_norm_back(d_q, q_raw, q_inv, *rotary), rope_norm_back(d_k, k_raw, k_inv, *rotary), d_v.astype(BF16)
+    for part, value in enumerate(parts):
+        block = column_block(pl.program_id(0), part)
+        d_ref[:, pl.ds(pl.multiple_of(block * LANES, LANES), LANES)] = value
+
+
+def column_block(pair, part):
+    return pair // 3 * 9 + part * 3 + pair % 3
+
+
+def qkv_kernel(x_ref, gamma_ref, w_ref, qkv_ref, n_ref):
+    @pl.when(pl.program_id(0) == 0)
+    def _():
+        n_ref[:] = rms_norm(x_ref[:], gamma_ref[:])
+
+    qkv_ref[:] = dot_nn(n_ref[:], w_ref[:]).astype(BF16)
+
+
+def norm_qkv(tokens, gamma, weights):
+    (tok, dim), width = tokens.shape, weights.shape[1] // 8
+    return pl.pallas_call(
+        qkv_kernel, grid=(6,), in_specs=[fixed(tok, dim), fixed(1, dim), pl.BlockSpec((dim, width), lambda step: (0, step + step // 3))],
+        out_specs=[pl.BlockSpec((tok, width), lambda step: (0, step)), fixed(tok, dim)],
+        out_shape=[jax.ShapeDtypeStruct((tok, 6 * width), BF16), jax.ShapeDtypeStruct((tok, dim), BF16)],
+        compiler_params=pltpu.CompilerParams(vmem_limit_bytes=VMEM_LIMIT),
+        cost_estimate=kernel_cost(12 * tok * dim * width, dim * width),
+    )(tokens, gamma, weights)
 
 
 def fixed(*shape):
@@ -139,39 +168,27 @@
     return pl.CostEstimate(flops=flops, bytes_accessed=moved, transcendentals=0)
 
 
-def attn_specs(seq, pairs):
-    head_specs = [pl.BlockSpec((seq, 128), lambda pair, part=part: (0, part * pairs + pair)) for part in range(3)]
-    one = pl.BlockSpec((seq, 128), lambda pair: (0, pair))
-    table = fixed(seq, 128)
-    return head_specs, one, table
-
-
-def attn_fwd(qkv, cos_tab, sin_tab):
-    seq, width = qkv.shape[0], qkv.shape[1] // 3
-    head_specs, one, table = attn_specs(seq, width // 128)
+def attn_call(kernel, name_cost, qkv, d_o, cos_tab, sin_tab, out_spec, out_width):
+    seq = qkv.shape[0]
+    head_specs = [pl.BlockSpec((seq, LANES), lambda pair, part=part: (0, column_block(pair, part))) for part in range(3)]
+    table = fixed(seq, LANES)
+    extra = [] if d_o is None else [pair_spec(seq)]
     return pl.pallas_call(
-        attn_fwd_kernel, grid=(width // 128,), in_specs=head_specs + [table, table], out_specs=one,
-        out_shape=jax.ShapeDtypeStruct((seq, width), BF16),
-        compiler_params=pltpu.CompilerParams(vmem_limit_bytes=VMEM_LIMIT),
-        cost_estimate=kernel_cost(40 * seq * seq * width, seq * width),
-    )(qkv, qkv, qkv, cos_tab, sin_tab)
-
-
-def attn_bwd(qkv, d_o, cos_tab, sin_tab):
-    seq, width = qkv.shape[0], qkv.shape[1] // 3
-    head_specs, one, table = attn_specs(seq, width // 128)
-    return pl.pallas_call(
-        attn_bwd_kernel, grid=(width // 128,), in_specs=head_specs + [one, table, table], out_specs=[one] * 3,
-        out_shape=[jax.ShapeDtypeStruct((seq, width), BF16)] * 3,
-        compiler_params=pltpu.CompilerParams(vmem_limit_bytes=VMEM_LIMIT),
-        cost_estimate=kernel_cost(80 * seq * seq * width, seq * width),
-    )(qkv, qkv, qkv, d_o, cos_tab, sin_tab)
+        kernel, grid=(6,), in_specs=head_specs + extra + [table, table], out_specs=out_spec, out_shape=jax.ShapeDtypeStruct((seq, out_width), BF16),
+        compiler_params=pltpu.CompilerParams(vmem_limit_bytes=VMEM_LIMIT), cost_estimate=kernel_cost(name_cost * seq * seq * seq, qkv.size),
+    )(qkv, qkv, qkv, *([] if d_o is None else [d_o]), cos_tab, sin_tab)
+
+
+def pair_spec(seq):
+    return pl.BlockSpec((seq, LANES), lambda pair: (0, pair))
 
 
 def route_slots(flat_ids, n_experts, capacity):
     onehot = flat_ids[:, None] == jnp.arange(n_experts)[None, :]
-    running = jnp.cumsum(onehot.astype(jnp.int32), axis=0)
-    slot_idx = jnp.sum(jnp.where(onehot, running, 0), axis=1) - 1
+    token = jnp.arange(flat_ids.size)
+    before = (token[:, None] > token[None, :]).astype(BF16)
+    running = jnp.dot(before, onehot.astype(BF16), preferred_element_type=F32)
+    slot_idx = jnp.sum(jnp.where(onehot, running, 0.0), axis=1).astype(jnp.int32)
     return onehot, flat_ids * capacity + slot_idx
 
 
@@ -180,7 +197,7 @@
 
 
 def z_hop(block, step):
-    return lax.ppermute(block, 'z', [(z_idx, z_idx ^ step) for z_idx in range(4)])
+    return lax.ppermute(block, 'z', [(z_idx, z_idx ^ step) for z_idx in range(QUAD)])
 
 
 def pick(array, idx, axis):
@@ -190,6 +207,12 @@
 def in_core_order(mine, other, axis):
     first = lax.axis_index('c') == 0
     return jnp.concatenate([jnp.where(first, mine, other), jnp.where(first, other, mine)], axis=axis)
+
+
+def core_halves(array, axis):
+    low, high = jnp.split(array, 2, axis=axis)
+    first = lax.axis_index('c') == 0
+    return jnp.where(first, low, high), jnp.where(first, high, low)
 
 
 def plane_first(block):
@@ -206,14 +229,14 @@
     return lax.optimization_barrier((value,) + anchors)[0]
 
 
-def z_stack(parts):
+def z_stack(parts, gate):
     half = parts[0].shape[1] // 2
     c_me = lax.axis_index('c')
 
     def side(core):
-        return jnp.concatenate([lax.dynamic_slice_in_dim(part, core * half, half, 1) for part in parts], axis=1)
-
-    chip = in_core_order(side(c_me), hop(side(1 - c_me), 'c'), 0)
+        return jnp.concatenate([lax.dynamic_slice_in_dim(part, core * half, half, axis=1) for part in parts], axis=1)
+
+    chip = after(in_core_order(side(c_me), hop(side(1 - c_me), 'c'), 0), gate)
     return [chip] + [z_hop(chip, step) for step in Z_STEPS]
 
 
@@ -251,30 +274,30 @@
     z_sem, x_sem, y_sem, far_sem, c_sem = range(0, 20, 4)
     for step, peer in zip(Z_STEPS, peers):
         send(0, 0, peer, z_sem + step, own=True)
-    for back in range(4):
+    for back in range(QUAD):
         if back:
             landed(back, 0, z_sem + back)
         send(back, 0, peer_x, x_sem + back, own=not back)
         send(back, 0, peer_y, y_sem + back, own=not back)
-        send(back, 0, peer_c, c_sem + 4 * back, own=not back)
-    for back in range(4):
+        send(back, 0, peer_c, c_sem + QUAD * back, own=not back)
+    for back in range(QUAD):
         landed(back, 1, x_sem + back)
         if back >= 2:
             send(back, 1, peer_y, far_sem + back)
-        send(back, 1, peer_c, c_sem + 4 * back + 1)
+        send(back, 1, peer_c, c_sem + QUAD * back + 1)
         landed(back, 2, y_sem + back)
         if back < 2:
             send(back, 2, peer_x, far_sem + back)
-        send(back, 2, peer_c, c_sem + 4 * back + 2)
-    for back in range(4):
+        send(back, 2, peer_c, c_sem + QUAD * back + 2)
+    for back in range(QUAD):
         landed(back, 3, far_sem + back)
-        send(back, 3, peer_c, c_sem + 4 * back + 3)
+        send(back, 3, peer_c, c_sem + QUAD * back + 3)
     local = [pltpu.make_async_copy(src, out.at[slot(0, 0, c_me)], local_sems.at[kind]) for kind, (src, out) in enumerate(pairs)]
     for copy in local:
         copy.start()
-    for back in range(4):
-        for rel in range(4):
-            landed(back, rel, c_sem + 4 * back + rel, 1 - c_me)
+    for back in range(QUAD):
+        for rel in range(QUAD):
+            landed(back, rel, c_sem + QUAD * back + rel, 1 - c_me)
     for copy in local:
         copy.wait()
     for copy in started:
@@ -330,10 +353,10 @@
     lax.fori_loop(0, rows_ref.shape[0] // chunk, step, 0)
 
 
-def up_grads(lhs_s, dg_s, dl_s, g1_away, g1_near, g3_away, g3_near):
+def row_grads(lhs_s, grad, away, near, x_first):
     for slot in range(2):
-        for ref, rel, grad in ((g1_away, 2 * slot + 1, dg_s), (g1_near, 2 * slot, dg_s), (g3_away, slot + 2, dl_s), (g3_near, slot, dl_s)):
-            ref[slot] = dot_nn(lhs_s[rel], grad[:])
+        away[slot] = dot_nn(lhs_s[2 * slot + 1 if x_first else slot + 2], grad[:])
+        near[slot] = dot_nn(lhs_s[2 * slot if x_first else slot], grad[:])
 
 
 def expert_kernel(half, info, rows_ref, dd_ref, rows_t_ref, dd_t_ref, *refs):
@@ -360,10 +383,10 @@
         else:
             out_acc[:] = jnp.zeros_like(out_acc)
             back_acc[:] = jnp.zeros_like(back_acc)
-        for rel in range(4):
+        for rel in range(QUAD):
             lhs_s[rel] = rows_t_ref[pl.ds(pl.multiple_of((me ^ rel) * 192, 64), 192), :]
 
-    for rel in range(4):
+    for rel in range(QUAD):
         at = pl.ds(pl.multiple_of((me ^ rel) * 192, 64), 192)
         w1[at, :] = up_refs[rel][0]
         w3[at, :] = up_refs[4 + rel][0]
@@ -375,7 +398,8 @@
                 pltpu.make_async_copy(src, w2_halves[part], sems.at[part]).wait()
 
     ffn_rows(rows_ref, dd_ref, w1, w3, w2, False, wait_w2, act_s, dg_s, dl_s, out_acc, back_acc)
-    up_grads(lhs_s, dg_s, dl_s, g1_away, g1_near, g3_away, g3_near)
+    row_grads(lhs_s, dg_s, g1_away, g1_near, True)
+    row_grads(lhs_s, dl_s, g3_away, g3_near, False)
 
     for near in range(2):
         @pl.when(step == near)
@@ -397,24 +421,24 @@
     whole, turned = fixed(tok, dim), fixed(dim, tok)
 
     def up_spec(mat):
-        return pl.BlockSpec((1, dim // 4, dim), lambda step, info_ref, mat=mat: (mat, 0, info_ref[1 + step]))
+        return pl.BlockSpec((1, dim // QUAD, dim), lambda step, info_ref, mat=mat: (mat, 0, info_ref[1 + step]))
 
     own, from_x, from_y, low, high = up
     up_args = (own, from_x, from_y, low, own, from_x, from_y, high)
-    up_specs = [up_spec(0)] * 4 + [up_spec(1)] * 3 + [up_spec(0)]
+    up_specs = [up_spec(0)] * QUAD + [up_spec(1)] * 3 + [up_spec(0)]
     any_spec = pl.BlockSpec(memory_space=pl.ANY)
-    row_out = pl.BlockSpec((2, dim // 4, dim), lambda step, info_ref: (0, 0, info_ref[1 + step] - 2 * half))
+    row_out = pl.BlockSpec((2, dim // QUAD, dim), lambda step, info_ref: (0, 0, info_ref[1 + step] - 2 * half))
     square = fixed(dim, dim)
     acc_type = F32 if half == 0 else BF16
-    row_shape, square_shape = jax.ShapeDtypeStruct((2, dim // 4, 2 * dim), F32), jax.ShapeDtypeStruct((dim, dim), F32)
+    row_shape, square_shape = jax.ShapeDtypeStruct((2, dim // QUAD, 2 * dim), F32), jax.ShapeDtypeStruct((dim, dim), F32)
     return pl.pallas_call(
         lambda *refs: expert_kernel(half, *refs),
         grid_spec=pltpu.PrefetchScalarGridSpec(
             num_scalar_prefetch=1, grid=(2,),
             in_specs=[whole, whole, turned, turned] + up_specs + [any_spec] * 5 + [whole] * len(acc),
-            out_specs=[whole, whole] + [row_out] * 4 + [square] * 2,
-            scratch_shapes=[pltpu.VMEM((dim, dim), BF16)] * 3 + [pltpu.VMEM((tok, dim), BF16)] * 3 + [pltpu.VMEM((tok, dim), F32)] * 2 + [pltpu.VMEM((4, dim // 4, tok), BF16), pltpu.SemaphoreType.DMA((2,))]),
-        out_shape=[jax.ShapeDtypeStruct((tok, dim), acc_type)] * 2 + [row_shape] * 4 + [square_shape] * 2,
+            out_specs=[whole, whole] + [row_out] * QUAD + [square] * 2,
+            scratch_shapes=[pltpu.VMEM((dim, dim), BF16)] * 3 + [pltpu.VMEM((tok, dim), BF16)] * 3 + [pltpu.VMEM((tok, dim), F32)] * 2 + [pltpu.VMEM((QUAD, dim // QUAD, tok), BF16), pltpu.SemaphoreType.DMA((2,))]),
+        out_shape=[jax.ShapeDtypeStruct((tok, dim), acc_type)] * 2 + [row_shape] * QUAD + [square_shape] * 2,
         compiler_params=pltpu.CompilerParams(vmem_limit_bytes=VMEM_LIMIT),
         cost_estimate=kernel_cost(36 * tok * dim * dim, dim * dim),
     )(info, rows, dd, rows_t, dd_t, *up_args, *down, *acc)
@@ -422,54 +446,64 @@
 
 def shared_kernel(info, rows_ref, dd_ref, rows_t_ref, dd_t_ref, *refs):
     pieces, refs = [refs[5 * mat:5 * mat + 5] for mat in range(3)], refs[15:]
-    out_ref, back_ref, g1_away, g1_near, g3_away, g3_near = refs[:6]
-    g2_refs = refs[6:10]
-    w1, w3, w2, act_s, dg_s, dl_s, lhs_s, dd_s = refs[10:]
+    out_refs, back_refs, g3_away, g3_near, g1_refs, g2_refs = refs[:2], refs[2:4], refs[4], refs[5], refs[6:10], refs[10:14]
+    w1, w3, w2, act_s, dg_s, dl_s, out_acc, back_acc, lhs_s, lhs_z, dd_z = refs[14:]
     step, me, z_me = pl.program_id(0), info[0], info[1]
 
     def spot(rel, turn_z):
-        return pl.ds(pl.multiple_of(((z_me ^ turn_z) * 4 + (me ^ rel)) * 48, 16), 48)
+        return pl.ds(pl.multiple_of(((z_me ^ turn_z) * QUAD + (me ^ rel)) * ROWS, 16), ROWS)
 
     @pl.when(step == 0)
     def _():
-        out_ref[:] = jnp.zeros_like(out_ref)
-        back_ref[:] = jnp.zeros_like(back_ref)
-        for rel in range(4):
-            for turn_z in range(4):
-                lhs_s[rel, turn_z * 48:(turn_z + 1) * 48, :] = rows_t_ref[spot(rel, turn_z), :]
-                dd_s[turn_z, rel * 48:(rel + 1) * 48, :] = dd_t_ref[spot(rel, turn_z), :]
+        out_acc[:] = jnp.zeros_like(out_acc)
+        back_acc[:] = jnp.zeros_like(back_acc)
+        for rel in range(QUAD):
+            for turn_z in range(QUAD):
+                inner = slice(rel * ROWS, rel * ROWS + ROWS)
+                lhs_s[rel, turn_z * ROWS:turn_z * ROWS + ROWS, :] = rows_t_ref[spot(rel, turn_z), :]
+                lhs_z[turn_z, inner, :] = rows_t_ref[spot(rel, turn_z), :]
+                dd_z[turn_z, inner, :] = dd_t_ref[spot(rel, turn_z), :]
 
     for w_ref, (own, from_x, from_y, low, high) in zip((w1, w3, w2), pieces):
-        for turn_z in range(4):
-            for rel, src in ((0, own.at[turn_z]), (1, from_x.at[turn_z]), (2, from_y.at[turn_z]), (3, low.at[turn_z] if turn_z < 2 else high.at[turn_z - 2])):
+        for turn_z in range(QUAD):
+            for rel, src in enumerate((own.at[turn_z], from_x.at[turn_z], from_y.at[turn_z], low.at[turn_z] if turn_z < 2 else high.at[turn_z - 2])):
                 w_ref[spot(rel, turn_z), :] = src[:]
 
-    ffn_rows(rows_ref, dd_ref, w1, w3, w2, True, None, act_s, dg_s, dl_s, out_ref, back_ref)
-    up_grads(lhs_s, dg_s, dl_s, g1_away, g1_near, g3_away, g3_near)
-    for turn_z in range(4):
-        g2_refs[turn_z][:] = dot_nn(dd_s[turn_z], act_s[:])
-
-
-def shared_ffn(rows, dd, rows_t, dd_t, pieces):
+    ffn_rows(rows_ref, dd_ref, w1, w3, w2, True, None, act_s, dg_s, dl_s, out_acc, back_acc)
+    row_grads(lhs_s, dl_s, g3_away, g3_near, False)
+    for turn_z in range(QUAD):
+        g1_refs[turn_z][:] = dot_nn(lhs_z[turn_z], dg_s[:])
+        g2_refs[turn_z][:] = dot_nn(dd_z[turn_z], act_s[:])
+
+    @pl.when(step == pl.num_programs(0) - 1)
+    def _():
+        for acc, halves in ((out_acc, out_refs), (back_acc, back_refs)):
+            for ref, value in zip(halves, jnp.split(acc[:], 2, axis=0)):
+                ref[:] = value
+
+
+def shared_ffn(gate, rows, dd, rows_t, dd_t, pieces):
     tok, dim = rows.shape
     width = pieces[0].shape[2] // 3
     steps = width // dim
-    info = jnp.stack([2 * lax.axis_index('y') + lax.axis_index('x'), lax.axis_index('z')]).astype(jnp.int32)
-    whole, turned = fixed(tok, dim), fixed(dim, tok)
-    piece_specs = [pl.BlockSpec((piece.shape[0], 48, dim), lambda step, info_ref, mat=mat: (0, 0, mat * steps + step)) for mat in range(3) for piece in pieces]
-    row_out = pl.BlockSpec((2, dim // 4, dim), lambda step, info_ref: (0, 0, step))
-    z_out = pl.BlockSpec((dim // 4, dim), lambda step, info_ref: (0, step))
-    return pl.pallas_call(
+    info = after(jnp.stack([2 * lax.axis_index('y') + lax.axis_index('x'), lax.axis_index('z')]).astype(jnp.int32), gate)
+    whole, turned, half = fixed(tok, dim), fixed(dim, tok), fixed(tok // 2, dim)
+    piece_specs = [pl.BlockSpec((piece.shape[0], ROWS, dim), lambda step, info_ref, mat=mat: (0, 0, mat * steps + step)) for mat in range(3) for piece in pieces]
+    row_out = pl.BlockSpec((2, dim // QUAD, dim), lambda step, info_ref: (0, 0, step))
+    z_out = pl.BlockSpec((dim // QUAD, dim), lambda step, info_ref: (0, step))
+    shapes = ((tok // 2, dim),) * QUAD + ((2, dim // QUAD, width),) * 2 + ((dim // QUAD, width),) * 8
+    outs = pl.pallas_call(
         shared_kernel,
         grid_spec=pltpu.PrefetchScalarGridSpec(
             num_scalar_prefetch=1, grid=(steps,),
             in_specs=[whole, whole, turned, turned] + piece_specs,
-            out_specs=[whole, whole] + [row_out] * 4 + [z_out] * 4,
-            scratch_shapes=[pltpu.VMEM((dim, dim), BF16)] * 3 + [pltpu.VMEM((tok, dim), BF16)] * 3 + [pltpu.VMEM((4, dim // 4, tok), BF16)] * 2),
-        out_shape=[jax.ShapeDtypeStruct((tok, dim), F32)] * 2 + [jax.ShapeDtypeStruct((2, dim // 4, width), F32)] * 4 + [jax.ShapeDtypeStruct((dim // 4, width), F32)] * 4,
+            out_specs=[half] * QUAD + [row_out] * 2 + [z_out] * 8,
+            scratch_shapes=[pltpu.VMEM((dim, dim), BF16)] * 3 + [pltpu.VMEM((tok, dim), BF16)] * 3 + [pltpu.VMEM((tok, dim), F32)] * 2 + [pltpu.VMEM((QUAD, dim // QUAD, tok), BF16)] * 3),
+        out_shape=[jax.ShapeDtypeStruct(shape, F32) for shape in shapes],
         compiler_params=pltpu.CompilerParams(vmem_limit_bytes=VMEM_LIMIT),
         cost_estimate=kernel_cost(18 * tok * dim * width, dim * width),
     )(info, rows, dd, rows_t, dd_t, *(list(pieces) * 3))
+    return outs[:2], outs[2:4], outs[4:6], outs[6:10], outs[10:]
 
 
 def z_sum(plane):
@@ -503,18 +537,6 @@
 
 def swap_experts(summed):
     return in_core_order(*(part[None] for part in swap_rows(summed)), 0)
-
-
-def scatter_small(grad):
-    sums = grad.reshape(4, 2, 2, 2, 24, -1)
-    for axis, name in ((1, 'y'), (1, 'x'), (1, 'c')):
-        me = lax.axis_index(name)
-        sums = pick(sums, me, axis) + hop(pick(sums, 1 - me, axis), name)
-    z_me = lax.axis_index('z')
-    total = pick(sums, z_me, 0)
-    for step in (1, 2, 3):
-        total = total + z_hop(pick(sums, z_me ^ step, 0), step)
-    return total
 
 
 def layer_step(x_in, grad_y, w_q, w_k, w_v, w_o, gamma_attn, gamma_mlp, w_router, w1_shared, w3_shared, w2_shared, w1_expert, w3_expert, w2_expert, expert_ids):
@@ -530,15 +552,14 @@
     att_parts = (w_q.reshape(-1, att_dim), w_k.reshape(-1, att_dim), w_v.reshape(-1, att_dim), w_o.reshape(att_dim, -1).T)
     att_block = jnp.concatenate([part[:, :att_half] for part in att_parts] + [part[:, att_half:] for part in att_parts], axis=1)
     small = jnp.concatenate([gamma_attn.astype(F32)[:, None], gamma_mlp.astype(F32)[:, None], w_router], axis=1)
-    small = jnp.pad(small, ((0, 0), (0, 128 - small.shape[1])))
+    small = jnp.pad(small, ((0, 0), (0, LANES - small.shape[1])))
     up_chip, down_chip = expert_chips(w1_expert, w3_expert, w2_expert)
     att_all, small_all = gather_weights(att_block, small)
     att_all, small_all = att_all.reshape(model_dim, -1), small_all.reshape(model_dim, -1)
-    att_w = jnp.split(att_all, 2, axis=1)
     ga_all, gm_all, wr_all = small_all[:, 0], small_all[:, 1], small_all[:, 2:2 + n_experts]
     down_first = plane_first(down_chip)
     up_first = plane_first(up_chip)
-    sh_parts = z_stack((w1_shared, w3_shared, w2_shared.T))
+    sh_parts = z_stack((w1_shared, w3_shared, w2_shared.T), small_all)
 
     d_out = grad_y.reshape(n_tok, model_dim)
     onehot, dest_row = route_slots(expert_ids.reshape(n_tok), n_experts, capacity)
@@ -548,38 +569,45 @@
         return lax.all_to_all(values.reshape(n_experts, capacity, model_dim), ('z', 'c'), 0, 0, tiled=True).reshape(n_slots, model_dim)
 
     def dispatch(values):
-        return exchange(jnp.einsum('ts,td->sd', place, values, preferred_element_type=F32).astype(BF16))
+        return jnp.einsum('ts,td->sd', place, values, preferred_element_type=F32).astype(BF16)
 
     d_out_both = jnp.concatenate([d_out, hop(d_out, 'c')], axis=0)
     d_out_t = d_out_both.T
-    cos_tab, sin_tab = rope_tables(seq_len, head_dim)
+    tables = rope_tables(seq_len, head_dim)
 
     tokens = x_in.reshape(n_tok, model_dim)
-    normed1, norm1_pull = jax.vjp(rms_norm, tokens, ga_all)
-    qkv = [dot32(normed1, w_half[:, :3 * att_half]).astype(BF16) for w_half in att_w]
-    attn_parts = [attn_fwd(half, cos_tab, sin_tab) for half in qkv]
-    wot = [w_half[:, 3 * att_half:] for w_half in att_w]
-    attn_out = sum(jnp.einsum('tk,dk->td', part, w_half, preferred_element_type=F32) for part, w_half in zip(attn_parts, wot))
+    qkv, normed1 = norm_qkv(tokens, ga_all[None, :], att_all)
+    norm1_pull = jax.vjp(rms_norm, tokens, ga_all)[1]
+    heads = attn_call(attn_fwd_kernel, 8, qkv, None, *tables, pair_spec(n_tok), att_dim)
+    half_cols = [slice(start, start + att_half) for start in (0, att_half)]
+    wot = [att_all[:, start + 3 * att_half:start + QUAD * att_half] for start in (0, QUAD * att_half)]
+    attn_out = sum(jnp.einsum('tk,dk->td', heads[:, cols], w_half, preferred_element_type=F32) for cols, w_half in zip(half_cols, wot))
     hidden = (tokens.astype(F32) + attn_out).astype(BF16)
     normed2, norm2_pull = jax.vjp(rms_norm, hidden, gm_all)
     normed2_f = normed2.astype(F32)
     logits = jnp.dot(normed2, wr_all, preferred_element_type=F32, precision=lax.Precision.HIGHEST)
     gate_val = jax.nn.sigmoid(jnp.sum(jnp.where(onehot, logits, 0.0), axis=1))
     routed_in = (gate_val[:, None] * normed2_f).astype(BF16)
-    rows = dispatch(routed_in)
-    d_down = dispatch(after(d_out, routed_in))
-    d_down_t = d_down.T
+    give_r = dispatch(routed_in)
+    give_d = dispatch(after(d_out, give_r))
+    rows = exchange(give_r)
+    d_down = exchange(after(give_d, rows))
+    rows_t, d_down_t = rows.T, d_down.T
 
     normed2_both = jnp.concatenate([normed2, hop(normed2, 'c')], axis=0)
-    sh_first = plane_first(jnp.stack([after(part, attn_parts[1]) for part in sh_parts]))
-    sh_pieces = plane_pieces([after(piece, routed_in) for piece in sh_first])
-    down_pieces = plane_pieces([after(piece, routed_in) for piece in down_first])
-    up_pieces = plane_pieces([after(piece, routed_in) for piece in up_first])
-    shared_part, d_part, s1_away, s1_near, s3_away, s3_near, *s2 = shared_ffn(normed2_both, d_out_both, normed2_both.T, d_out_t, sh_pieces)
-    shared_out = shared_part[:n_tok] + hop(shared_part[n_tok:], 'c')
-    d_normed2 = d_part[:n_tok] + hop(d_part[n_tok:], 'c')
-
-    rows_t = rows.T
+    normed2_t = normed2_both.T
+    sh_first = plane_first(jnp.stack([after(part, heads) for part in sh_parts]))
+
+    def settle(pieces):
+        return [after(piece, give_r, give_d, normed2_t, d_out_t) for piece in pieces]
+
+    sh_pieces = plane_pieces(settle(sh_first))
+    down_pieces = plane_pieces(settle(down_first))
+    up_pieces = plane_pieces(settle(up_first))
+    shared_part, d_part, (s3_away, s3_near), s1, s2 = shared_ffn(rows_t, normed2_both, d_out_both, normed2_t, d_out_t, sh_pieces)
+    shared_out = shared_part[0] + hop(shared_part[1], 'c')
+    d_normed2 = d_part[0] + hop(d_part[1], 'c')
+
     *acc, a1_away, a1_near, a3_away, a3_near, a2_away, a2_near = expert_half(0, rows, d_down, rows_t, d_down_t, up_pieces, down_pieces, ())
     down_rows, d_rows, b1_away, b1_near, b3_away, b3_near, b2_away, b2_near = expert_half(1, rows, d_down, rows_t, d_down_t, up_pieces, down_pieces, acc)
     d_back = exchange(d_rows)
@@ -588,11 +616,8 @@
         keep, give = near + after(hop(away, axis), *gate)
         return keep, hop(give, 'y' if axis == 'x' else 'x')
 
-    s1, s3 = first_sum(s1_away, s1_near, 'x', [d_rows]), first_sum(s3_away, s3_near, 'y', [d_rows])
+    s3 = first_sum(s3_away, s3_near, 'y', [d_rows])
     a1, a3 = first_sum(a1_away, a1_near, 'x', [d_rows]), first_sum(a3_away, a3_near, 'y', [d_rows])
-    routed = jnp.einsum('ts,sd->td', place, exchange(down_rows), preferred_element_type=F32)
-    layer_out = (hidden.astype(F32) + routed + shared_out).astype(BF16)
-
     d_routed_in = jnp.einsum('ts,sd->td', place, d_back, preferred_element_type=F32)
     d_normed2 = d_normed2 + gate_val[:, None] * d_routed_in
     d_gate_val = jnp.sum(d_routed_in * normed2_f, axis=1) * gate_val * (1.0 - gate_val)
@@ -603,53 +628,67 @@
     d_hidden = (d_out.astype(F32) + d_hid_norm.astype(F32)).astype(BF16)
 
     d_hidden_t, normed1_t = d_hidden.T, normed1.T
-    d_qkv = [jnp.concatenate(attn_bwd(half, dot32(d_hidden, w_half).astype(BF16), cos_tab, sin_tab), axis=1) for half, w_half in zip(qkv, wot)]
-    c_me = lax.axis_index('c')
-    core_0 = c_me == 0
+    d_heads = jnp.concatenate([dot32(d_hidden, w_half).astype(BF16) for w_half in wot], axis=1)
+    d_qkv = attn_call(attn_bwd_kernel, 16, qkv, d_heads, *tables, fixed(n_tok, 3 * att_dim), 3 * att_dim)
+    d_halves = jnp.split(d_qkv, 2, axis=1)
+    d_normed1 = sum(jnp.einsum('tk,dk->td', half, att_all[:, start:start + 3 * att_half], preferred_element_type=F32) for half, start in zip(d_halves, (0, QUAD * att_half)))
+    d_tok_norm, g_ga = norm1_pull(d_normed1.astype(BF16))
+    g_small = jnp.concatenate([g_ga[:, None], g_gm[:, None], g_wr, jnp.zeros((model_dim, 6), F32)], axis=1)
+    core_0 = lax.axis_index('c') == 0
 
     def core_pick(pair):
         first, second = pair
         return jnp.where(core_0, first, second), jnp.where(core_0, second, first)
 
     g_att = []
-    for lhs_t, pair in ((normed1_t, d_qkv), (d_hidden_t, attn_parts)):
+    for lhs_t, pair in ((normed1_t, d_halves), (d_hidden_t, [heads[:, cols] for cols in half_cols])):
         mine, other = core_pick(pair)
         g_att.append(dot32(lhs_t, mine) + hop(dot32(lhs_t, other), 'c'))
-    att_gives, att_rest = plane_sum_values(jnp.concatenate(g_att, axis=1).reshape(4, 2, 2, 48, -1))
+    mine, other = (jnp.pad(half, ((0, 0), (0, LANES - half.shape[1]))) for half in core_pick(jnp.split(g_small, 2, axis=1)))
+    g_att.append(mine + hop(other, 'c'))
+    att_gives, att_rest = plane_sum_values(jnp.concatenate(g_att, axis=1).reshape(QUAD, 2, 2, ROWS, -1))
 
     def later(value):
         return after(value, *att_gives)
 
-    s2_total = s2[0]
-    for step in Z_STEPS:
-        s2_total = s2_total + later(z_hop(s2[step], step))
-    b1, b3 = first_sum(b1_away, b1_near, 'x', att_gives), first_sum(b3_away, b3_near, 'y', att_gives)
     low_y = lax.axis_index('y') == 0
-    g2_sums = a2_near + later(hop(a2_away, 'x')), b2_near + later(hop(b2_away, 'x'))
-    g2_low, g2_high = g2_sums
+    g2_low, g2_high = a2_near + later(hop(a2_away, 'x')), b2_near + later(hop(b2_away, 'x'))
     g2_keep, g2_give = jnp.where(low_y, g2_low, g2_high), jnp.where(low_y, g2_high, g2_low)
+
+    def z_first(parts):
+        total = parts[0]
+        for step in Z_STEPS:
+            total = total + after(z_hop(parts[step], step), g2_give)
+        return jnp.split(total.reshape(2, 2, ROWS, -1), 2, axis=1)
+
+    def z_last(pair):
+        keep, give = pair
+        keep, give = keep + hop(give, 'x')
+        return (keep + hop(give, 'y')).reshape(ROWS, -1)
+
+    s1, s2 = z_first(s1), z_first(s2)
+    b_gates = [s1[1], s2[1]]
+    routed = jnp.einsum('ts,sd->td', place, exchange(later(down_rows)), preferred_element_type=F32)
+    layer_out = (hidden.astype(F32) + routed + shared_out).astype(BF16)
+    b1, b3 = first_sum(b1_away, b1_near, 'x', b_gates), first_sum(b3_away, b3_near, 'y', b_gates)
 
     def finish(pairs):
         return jnp.concatenate([mine + later(got) for mine, got in pairs], axis=1)
 
     g_w1, g_w3 = finish((a1, b1)), finish((a3, b3))
-    g_w2 = (g2_keep + hop(g2_give, 'y')).T
-    s2_keep, s2_give = jnp.split(s2_total.reshape(2, 2, 48, -1), 2, axis=1)
-    s2_keep, s2_give = s2_keep + hop(s2_give, 'x')
-    g_s2 = (s2_keep + hop(s2_give, 'y')).reshape(48, -1)
-    g_sh = jnp.concatenate([z_sum(finish((pair,)).reshape(4, 48, -1)) for pair in (s1, s3)] + [g_s2], axis=1)
+    g2_mine, g2_other = core_halves(g2_keep + hop(g2_give, 'y'), 1)
+    g_w2e = in_core_order(g2_mine.T[None], hop(g2_other, 'c').T[None], 0)
+    g_sh = jnp.concatenate([z_last(s1), z_sum(finish((s3,)).reshape(QUAD, ROWS, -1)), z_last(s2)], axis=1)
     g_sh_mine, g_sh_other = swap_rows(g_sh)
-    g_w2e = swap_experts(g_w2)
     g_up = swap_experts(jnp.stack([g_w1, g_w3]))
     z_me = lax.axis_index('z')
     att_plane = att_rest()
-    g_att_mine, g_att_other = swap_rows(z_sum([pick(att_plane, z_me ^ step, 0) for step in range(4)]))
-    d_normed1 = sum(jnp.einsum('tk,dk->td', half, w_half[:, :3 * att_half], preferred_element_type=F32) for half, w_half in zip(d_qkv, att_w))
-    d_tok_norm, g_ga = norm1_pull(d_normed1.astype(BF16))
+    g_att_mine, g_att_other = swap_rows(z_sum([pick(att_plane, z_me ^ step, 0) for step in range(QUAD)]))
     d_x = (d_hidden.astype(F32) + d_tok_norm.astype(F32)).astype(BF16).reshape(n_batch, seq_len, model_dim)
 
-    g_small = scatter_small(later(jnp.concatenate([g_ga[:, None], g_gm[:, None], g_wr, jnp.zeros((model_dim, 6), F32)], axis=1)))
-    g_att = in_core_order(g_att_mine.reshape(-1, 4, att_half), g_att_other.reshape(-1, 4, att_half), 2)
+    g_small = in_core_order(*(part[:, QUAD * att_half:QUAD * att_half + 8] for part in (g_att_mine, g_att_other)), 1)
+    g_att_mine, g_att_other = g_att_mine[:, :QUAD * att_half], g_att_other[:, :QUAD * att_half]
+    g_att = in_core_order(g_att_mine.reshape(-1, QUAD, att_half), g_att_other.reshape(-1, QUAD, att_half), 2)
     g_q, g_k, g_v = (g_att[:, part].reshape(-1, n_heads, head_dim) for part in range(3))
     g_wo = g_att[:, 3].T.reshape(n_heads, head_dim, -1)
     g_sh = in_core_order(g_sh_mine.reshape(-1, 3, ff_half), g_sh_other.reshape(-1, 3, ff_half), 2)

time: 1030 us -> 1120 us (1.087)
  waiting for transfers between devices: 448 us -> 525 us
  starting transfers between devices: 99.5 us -> 144 us
  other arithmetic: 105 us -> 84 us
  local copies, waits for them, and re-layouts: 115 us -> 98.7 us
    ppermute x18 -> x15, waiting for transfers between devices: 119 us -> 230 us  [z_hop(): lax.ppermute(block, 'z', [(z_idx, z_idx ^ step) for z_idx in range(QUAD)])]
    ppermute x18 -> x15, starting transfers between devices: 36.7 us -> 71.3 us  [z_hop(): lax.ppermute(block, 'z', [(z_idx, z_idx ^ step) for z_idx in range(QUAD)])]
    all_to_all x4, waiting for transfers between devices: 28.5 us -> 0.01 us  [exchange(): lax.all_to_all(values.reshape(n_experts, capacity, model_dim), ('z', 'c')...]
    all_to_all x4, starting transfers between devices: 20.6 us -> 36.7 us  [exchange(): lax.all_to_all(values.reshape(n_experts, capacity, model_dim), ('z', 'c')...]
    dot_general x8 -> x6, matrix products: 22.6 us -> 15.4 us  [dot32(): return jnp.dot(lhs, rhs, preferred_element_type=F32)]
    ppermute x49 -> x47, starting transfers between devices: 42.2 us -> 35.9 us  [hop(): return lax.ppermute(block, axis, SWAP)]
    ppermute x49 -> x47, waiting for transfers between devices: 301 us -> 295 us  [hop(): return lax.ppermute(block, axis, SWAP)]
    pallas_call x4 -> x3, Pallas kernels: 54.9 us -> 58.4 us  [the longest x2 51.1 us: attn_call(): pl.pallas_call(kernel, grid=(6,), in_specs=head_specs + extra + [table, t...]
  transfers between devices with their start and end apart: 71 -> 66, of which waited for: 25 -> 24; matrix products, arithmetic and copies ran while one was open for 21% -> 17% of each run, Pallas kernels for 14% -> 13%
where the time goes in v1:
time: 1120 us; the launch traced here: 1100 us
  waiting for transfers between devices  525 us (47%)
  Pallas kernels  214 us (19%)
  starting transfers between devices  144 us (13%)
  local copies, waits for them, and re-layouts  98.7 us (9%)
  other arithmetic  84 us (8%)
  matrix products  36.1 us (3%)
    ppermute x47, waiting for transfers between devices, hop(): return lax.ppermute(block, axis, SWAP)  295 us
    ppermute x15, waiting for transfers between devices, z_hop(): lax.ppermute(block, 'z', [(z_idx, z_idx ^ step) for z_idx in range(QUAD)])  230 us
    pallas_call x2, Pallas kernels, expert_half(): pl.pallas_call(lambda *refs: expert_kernel(half, *refs), grid_spec=pltpu....  80.5 us
    ppermute x15, starting transfers between devices, z_hop(): lax.ppermute(block, 'z', [(z_idx, z_idx ^ step) for z_idx in range(QUAD)])  71.3 us
    pallas_call x2, Pallas kernels, attn_call(): pl.pallas_call(kernel, grid=(6,), in_specs=head_specs + extra + [table, t...  51.1 us
    pallas_call x1, Pallas kernels, gather_weights(): pl.pallas_call(weight_kernel, in_specs=[any_spec] * 2, out_specs=[any_spe...  39.6 us
    all_to_all x4, starting transfers between devices, exchange(): lax.all_to_all(values.reshape(n_experts, capacity, model_dim), ('z', 'c')...  36.7 us
    ppermute x47, starting transfers between devices, hop(): return lax.ppermute(block, axis, SWAP)  35.9 us
  transfers between devices with their start and end apart: 66, of which 24 were waited for; matrix products, arithmetic and copies ran while one was open for 17% of the time, Pallas kernels for 13%

profile of v1, /device:TPU:0, one launch (start us, length us, event | category | flops | bytes accessed | tf_op | source)
XLA Modules:
  0.0 1103.1 jit_solution(13783076565982458893)
XLA Ops:
  7.8 39.6 %shard_map.289 = (bf16[32,24,3072]{2,1,0:T(8,128)(2,1)}, f32[32,24,128]{2,1,0:T(8,128)}) custom-call(bf16[24,3072]{1,0:T(8,128)(2,1)} %copy-done.65, f32[24,128]{1,0:T(8,128)} %select_maximum_fusion.small_ref), custom_call_target="tpu_custom_call" | custom-call | flops 7372800000 | bytes 73728 | tf_op jit(solution)/shard_map/pallas_call | solution.py:310
  50.7 7.3 shard_map.290
  57.9 19.4 %shard_map.291 = bf16[512,768]{1,0:T(8,128)(2,1)} custom-call(bf16[512,2304]{1,0:T(8,128)(2,1)} %get-tuple-element.87.q_ref.k_ref.v_ref, bf16[512,2304]{1,0:T(8,128)(2,1)} %get-tuple-element.87.q_ref.k_ref.v_ref, bf16[512,2304]{1,0:T(8,128)(2,1)} %get-tuple-element.87.q_ref.k_ref.v_ref, f32[512,128]{1,0:T(8,128)} %constant.218.clone.cos_ref, ...), custom_call_target="tpu_custom_call" | custom-call | flops 1073741824 | bytes 1179648 | tf_op jit(solution)/shard_map/pallas_call | solution.py:176
  81.4 2.5 fusion.36
  91.2 2.6 copy.238
  93.7 6.6 all-to-all-start
  113.7 2.4 collective-permute-start.14
  118.8 21.2 %collective-permute-done.13 = bf16[48,4608]{1,0:T(8,128)(2,1)} collective-permute-done((bf16[48,4608]{1,0:T(8,128)(2,1)}, bf16[48,4608]{1,0:T(8,128)(2,1)}, u32[]{:S(2)}, u32[]{:S(2)}) %collective-permute-start.13) | collective-permute-done | bytes 442400 | tf_op jit(solution)/shard_map/ppermute | solution.py:200
  142.0 3.5 copy_bitcast_fusion.1
  145.5 2.6 copy.241
  148.1 4.5 all-to-all-start.1
  153.9 20.9 %collective-permute-done.14 = bf16[48,4608]{1,0:T(8,128)(2,1)} collective-permute-done((bf16[48,4608]{1,0:T(8,128)(2,1)}, bf16[48,4608]{1,0:T(8,128)(2,1)}, u32[]{:S(2)}, u32[]{:S(2)}) %collective-permute-start.14) | collective-permute-done | bytes 442400 | tf_op jit(solution)/shard_map/ppermute | solution.py:200
  174.8 2.9 pad_maximum_fusion.6.refs_0_.refs_5_.refs_10_
  181.7 3.2 fusion.120
  190.9 2.4 slice.165
  193.3 50.9 %collective-permute-done.9.refs_15_ = bf16[2,384,768]{2,1,0:T(8,128)(2,1)S(1)} collective-permute-done((bf16[2,384,768]{2,1,0:T(8,128)(2,1)S(1)}, bf16[2,384,768]{2,1,0:T(8,128)(2,1)S(1)}, u32[]{:S(2)}, u32[]{:S(2)}) %collective-permute-start.9) | collective-permute-done | bytes 1179680 | tf_op jit(solution)/shard_map/ppermute | solution.py:196
  250.8 2.6 copy.247.rows_ref
  253.4 2.6 copy.248.dd_ref
  261.8 2.6 copy.245.refs_1_
  264.4 3.5 fusion.118
  267.9 2.6 copy.246.refs_2_
  270.4 14.2 %collective-permute-done.10.refs_16_ = bf16[1,384,768]{2,1,0:T(8,128)(2,1)} collective-permute-done((bf16[1,384,768]{2,1,0:T(8,128)(2,1)S(1)}, bf16[1,384,768]{2,1,0:T(8,128)(2,1)}, u32[]{:S(2)}, u32[]{:S(2)}) %collective-permute-start.10) | collective-permute-done | bytes 589856 | tf_op jit(solution)/shard_map/ppermute | solution.py:196
  286.2 39.8 %shard_map.292 = (f32[1024,768]{1,0:T(8,128)}, f32[1024,768]{1,0:T(8,128)}, f32[2,192,1536]{2,1,0:T(8,128)}, f32[2,192,1536]{2,1,0:T(8,128)}, f32[2,192,1536]{2,...) custom-call(s32[3]{0:T(128)} %get-tuple-element.299.refs_0_, ...), custom_call_target="tpu_custom_call" | custom-call | flops 21743271936 | bytes 589824 | tf_op jit(solution)/shard_map/pallas_call | solution.py:434
  325.9 40.7 %shard_map.293 = (bf16[1024,768]{1,0:T(8,128)(2,1)}, bf16[1024,768]{1,0:T(8,128)(2,1)}, f32[2,192,1536]{2,1,0:T(8,128)}, f32[2,192,1536]{2,1,0:T(8,128)}, f32[2,...) custom-call(s32[3]{0:T(128)} %get-tuple-element.298.refs_0_, ...), custom_call_target="tpu_custom_call" | custom-call | flops 21743271936 | bytes 589824 | tf_op jit(solution)/shard_map/pallas_call | solution.py:434
  366.7 21.3 %all-to-all-start.2 = ((bf16[8,128,768]{2,1,0:T(8,128)(2,1)}), bf16[8,128,768]{2,1,0:T(8,128)(2,1)}, u32[]{:S(2)}, u32[]{:S(2)}) async-start(bf16[8,128,768]{2,1,0:T(8,128)(2,1)} %bitcast.273), calls=%async_computation.2 | async-start | bytes 3145728 | tf_op jit(solution)/shard_map/all_to_all | solution.py:569
  387.9 35.2 %shard_map.294 = (f32[512,768]{1,0:T(8,128)}, f32[512,768]{1,0:T(8,128)}, f32[512,768]{1,0:T(8,128)}, f32[512,768]{1,0:T(8,128)}, f32[2,192,1536]{2,1,0:T(8,128)...) custom-call(s32[2]{0:T(128)} %pad_add_fusion.3.info, ...), custom_call_target="tpu_custom_call" | custom-call | flops 21743271936 | bytes 1179648 | tf_op jit(solution)/shard_map/pallas_call | solution.py:495
  423.7 3.0 copy.249
  427.8 3.1 copy.250
  430.9 3.0 copy.262
  433.9 3.0 copy.263
  440.4 37.2 %collective-permute-done.40 = f32[2,192,1536]{2,1,0:T(8,128)} collective-permute-done((f32[2,192,1536]{2,1,0:T(8,128)}, f32[2,192,1536]{2,1,0:T(8,128)}, u32[]{:S(2)}, u32[]{:S(2)}) %collective-permute-start.40) | collective-permute-done | bytes 2359328 | tf_op jit(solution)/shard_map/ppermute | solution.py:196
  478.2 4.2 add.330
  482.4 2.6 fusion.19
  493.7 31.7 %shard_map.295 = bf16[512,2304]{1,0:T(8,128)(2,1)} custom-call(bf16[512,2304]{1,0:T(8,128)(2,1)} %get-tuple-element.87.q_ref.k_ref.v_ref, bf16[512,2304]{1,0:T(8,128)(2,1)} %get-tuple-element.87.q_ref.k_ref.v_ref, bf16[512,2304]{1,0:T(8,128)(2,1)} %get-tuple-element.87.q_ref.k_ref.v_ref, bf16[512,768]{1,0:T(8,128)(2,1)} %pad_maximum_fusion.11.do_ref, ...), custom_call_target="tpu_custom_call" | custom-call | flops 2147483648 | bytes 1179648 | tf_op jit(solution)/shard_map/pallas_call | solution.py:176
  525.4 5.1 fusion.44
  531.6 60.2 %collective-permute-done.51 = f32[2,192,1536]{2,1,0:T(8,128)} collective-permute-done((f32[2,192,1536]{2,1,0:T(8,128)}, f32[2,192,1536]{2,1,0:T(8,128)}, u32[]{:S(2)}, u32[]{:S(2)}) %collective-permute-start.51) | collective-permute-done | bytes 2359328 | tf_op jit(solution)/shard_map/ppermute | solution.py:196
  594.2 3.1 add.340
  603.2 2.9 fusion.26
  610.4 2.9 collective-permute-start.33
  618.9 3.3 convolution_add_fusion
  622.6 41.4 %collective-permute-done.33 = f32[192,1536]{1,0:T(8,128)S(1)} collective-permute-done((f32[192,1536]{1,0:T(8,128)}, f32[192,1536]{1,0:T(8,128)S(1)}, u32[]{:S(2)}, u32[]{:S(2)}) %collective-permute-start.33) | collective-permute-done | bytes 1179680 | tf_op jit(solution)/shard_map/ppermute | solution.py:200
  664.0 29.9 %collective-permute-done.36 = f32[192,1536]{1,0:T(8,128)S(1)} collective-permute-done((f32[192,1536]{1,0:T(8,128)}, f32[192,1536]{1,0:T(8,128)S(1)}, u32[]{:S(2)}, u32[]{:S(2)}) %collective-permute-start.36) | collective-permute-done | bytes 1179680 | tf_op jit(solution)/shard_map/ppermute | solution.py:200
  701.5 4.6 broadcast_select_fusion
  706.2 11.4 %collective-permute-done.45 = f32[192,1536]{1,0:T(8,128)S(1)} collective-permute-done((f32[192,1536]{1,0:T(8,128)S(1)}, f32[192,1536]{1,0:T(8,128)S(1)}, u32[]{:S(2)}, u32[]{:S(2)}) %collective-permute-start.45) | collective-permute-done | bytes 1179680 | tf_op jit(solution)/shard_map/ppermute | solution.py:200
  719.1 75.8 %collective-permute-done.46 = f32[192,1536]{1,0:T(8,128)S(1)} collective-permute-done((f32[192,1536]{1,0:T(8,128)S(1)}, f32[192,1536]{1,0:T(8,128)S(1)}, u32[]{:S(2)}, u32[]{:S(2)}) %collective-permute-start.46) | collective-permute-done | bytes 1179680 | tf_op jit(solution)/shard_map/ppermute | solution.py:200
  803.8 17.1 %collective-permute-done.52 = f32[192,1536]{1,0:T(8,128)S(1)} collective-permute-done((f32[192,1536]{1,0:T(8,128)S(1)}, f32[192,1536]{1,0:T(8,128)S(1)}, u32[]{:S(2)}, u32[]{:S(2)}) %collective-permute-start.52) | collective-permute-done | bytes 1179680 | tf_op jit(solution)/shard_map/ppermute | solution.py:196
  823.3 5.5 collective-permute-done.41
  829.9 51.3 %collective-permute-start.42 = (f32[48,1536]{1,0:T(8,128)}, f32[48,1536]{1,0:T(8,128)}, u32[]{:S(2)}, u32[]{:S(2)}) collective-permute-start(f32[48,1536]{1,0:T(8,128)} %get-tuple-element.267), channel_id=1, source_target_pairs={{0,8},{8,0},{16,24},{24,16},{1,9},{9,1},{17,25},{25,17},{2,10},{10... | collective-permute-start | bytes 884744 | tf_op jit(solution)/shard_map/ppermute | solution.py:200
  886.5 4.3 all-to-all-start.3
  891.8 9.1 collective-permute-done.43
  906.1 11.3 %collective-permute-done.48 = f32[2,1,48,1536]{3,2,1,0:T(8,128)S(1)} collective-permute-done((f32[2,1,48,1536]{3,2,1,0:T(8,128)}, f32[2,1,48,1536]{3,2,1,0:T(8,128)S(1)}, u32[]{:S(2)}, u32[]{:S(2)}) %collective-permute-start.48) | collective-permute-done | bytes 589856 | tf_op jit(solution)/shard_map/ppermute | solution.py:196
  918.0 60.3 %collective-permute-done.39 = f32[1,48,1536]{2,1,0:T(8,128)S(1)} collective-permute-done((f32[1,48,1536]{2,1,0:T(8,128)S(1)}, f32[1,48,1536]{2,1,0:T(8,128)S(1)}, u32[]{:S(2)}, u32[]{:S(2)}) %collective-permute-start.39) | collective-permute-done | bytes 294944 | tf_op jit(solution)/shard_map/ppermute | solution.py:196
  978.9 7.4 collective-permute-done.49
  993.1 19.6 %collective-permute-done.54 = f32[192,1536]{1,0:T(8,128)} collective-permute-done((f32[192,1536]{1,0:T(8,128)}, f32[192,1536]{1,0:T(8,128)}, u32[]{:S(2)}, u32[]{:S(2)}) %collective-permute-start.54) | collective-permute-done | bytes 1179680 | tf_op jit(solution)/shard_map/ppermute | solution.py:196
  1029.0 8.1 collective-permute-done.28
  1044.1 2.4 collective-permute-start.30
  1049.5 7.2 collective-permute-done.29
  1056.8 12.3 %collective-permute-done.30 = f32[48,1664]{1,0:T(8,128)S(1)} collective-permute-done((f32[48,1664]{1,0:T(8,128)S(1)}, f32[48,1664]{1,0:T(8,128)S(1)}, u32[]{:S(2)}, u32[]{:S(2)}) %collective-permute-start.30) | collective-permute-done | bytes 319520 | tf_op jit(solution)/shard_map/ppermute | solution.py:200
  1069.4 3.9 select_add_fusion
  1082.7 2.7 fusion.8
  1085.4 3.0 fusion.62
  1094.4 3.0 copy.275
  1097.5 2.7 select_bitcast_fusion
  1100.2 2.5 fusion.6
  (408 shorter events, 181.2 us)
Async XLA Ops:
  81.3 97.8 %collective-permute-start.1 = (bf16[512,768]{0,1:T(8,128)(2,1)S(1)}, bf16[512,768]{0,1:T(8,128)(2,1)}, u32[]{:S(2)}, u32[]{:S(2)}) collective-permute-start(bf16[512,768]{0,1:T(8,128)(2,1)S(1)} %fusion.17), channel_id=1, source_target_pairs={{0,1},{1,0},{2,3},{3,2},{4,5},{5,4},{6,7},{7,6},{8,9},{9,8},{10,11... | collective-permute-start | bytes 2359304 | tf_op jit(solution)/shard_map/ppermute | solution.py:196
  83.9 19.3 %collective-permute-start = (bf16[2,96,3072]{2,1,0:T(8,128)(2,1)}, bf16[2,96,3072]{2,1,0:T(8,128)(2,1)}, u32[]{:S(2)}, u32[]{:S(2)}) collective-permute-start(bf16[2,96,3072]{2,1,0:T(8,128)(2,1)} %fusion.36), channel_id=1, source_target_pairs={{0,1},{1,0},{2,3},{3,2},{4,5},{5,4},{6,7},{7,6},{8,9},{9,8},{10,11... | collective-permute-start | bytes 3538952 | tf_op jit(solution)/shard_map/ppermute | solution.py:196
  85.3 30.8 %collective-permute-start.7 = (bf16[384,768]{1,0:T(8,128)(2,1)}, bf16[384,768]{1,0:T(8,128)(2,1)}, u32[]{:S(2)}, u32[]{:S(2)}) collective-permute-start(bf16[384,768]{1,0:T(8,128)(2,1)} %dynamic-slice_bitcast_fusion.2), channel_id=1, source_target_pairs={{0,1},{1,0},{2,3},{3,2},{4,5},{5,4},{6,7},{7,6},{8,9},{9,8},{10,11... | collective-permute-start | bytes 1769480 | tf_op jit(solution)/shard_map/ppermute | solution.py:196
  87.4 14.4 %collective-permute-start.12 = (bf16[24,4608]{1,0:T(8,128)(2,1)}, bf16[24,4608]{1,0:T(8,128)(2,1)}, u32[]{:S(2)}, u32[]{:S(2)}) collective-permute-start(bf16[24,4608]{1,0:T(8,128)(2,1)} %pad_maximum_fusion.17), channel_id=1, source_target_pairs={{0,1},{1,0},{2,3},{3,2},{4,5},{5,4},{6,7},{7,6},{8,9},{9,8},{10,11... | collective-permute-start | bytes 663560 | tf_op jit(solution)/shard_map/ppermute | solution.py:196
  93.7 48.2 %all-to-all-start = ((bf16[8,128,768]{1,2,0:T(8,128)(2,1)}), bf16[8,128,768]{1,2,0:T(8,128)(2,1)}, u32[]{:S(2)}, u32[]{:S(2)}) async-start(bf16[8,128,768]{1,2,0:T(8,128)(2,1)} %copy.238), calls=%async_computation | async-start | bytes 3145728 | tf_op jit(solution)/shard_map/all_to_all | solution.py:569
  107.1 74.1 %collective-permute-start.4 = (bf16[2,192,3072]{2,1,0:T(8,128)(2,1)}, bf16[2,192,3072]{2,1,0:T(8,128)(2,1)}, u32[]{:S(2)}, u32[]{:S(2)}) collective-permute-start(bf16[2,192,3072]{2,1,0:T(8,128)(2,1)} %pad_maximum_fusion.2.refs_5_.refs_9_), channel_id=1, source_target_pairs={{0,4},{4,0},{1,5},{5,1},{2,6},{6,2},{3,7},{7,3},{8,12},{12,8},{9,1... | collective-permute-start | bytes 7077896 | tf_op jit(solution)/shard_map/ppermute | solution.py:196
  109.3 30.6 %collective-permute-start.13 = (bf16[48,4608]{1,0:T(8,128)(2,1)}, bf16[48,4608]{1,0:T(8,128)(2,1)}, u32[]{:S(2)}, u32[]{:S(2)}) collective-permute-start(bf16[48,4608]{1,0:T(8,128)(2,1)} %pad_maximum_fusion.12), channel_id=1, source_target_pairs={{0,8},{8,0},{16,24},{24,16},{1,9},{9,1},{17,25},{25,17},{2,10},{10... | collective-permute-start | bytes 1327112 | tf_op jit(solution)/shard_map/ppermute | solution.py:200
  113.7 61.0 %collective-permute-start.14 = (bf16[48,4608]{1,0:T(8,128)(2,1)}, bf16[48,4608]{1,0:T(8,128)(2,1)}, u32[]{:S(2)}, u32[]{:S(2)}) collective-permute-start(bf16[48,4608]{1,0:T(8,128)(2,1)} %pad_maximum_fusion.12), channel_id=1, source_target_pairs={{0,16},{8,24},{16,0},{24,8},{1,17},{9,25},{17,1},{25,9},{2,18},{10... | collective-permute-start | bytes 1327112 | tf_op jit(solution)/shard_map/ppermute | solution.py:200
  116.1 73.3 %collective-permute-start.3 = (bf16[2,192,3072]{2,1,0:T(8,128)(2,1)}, bf16[2,192,3072]{2,1,0:T(8,128)(2,1)}, u32[]{:S(2)}, u32[]{:S(2)}) collective-permute-start(bf16[2,192,3072]{2,1,0:T(8,128)(2,1)} %pad_maximum_fusion.2.refs_5_.refs_9_), channel_id=1, source_target_pairs={{0,2},{2,0},{1,3},{3,1},{4,6},{6,4},{5,7},{7,5},{8,10},{10,8},{9,1... | collective-permute-start | bytes 7077896 | tf_op jit(solution)/shard_map/ppermute | solution.py:196
  140.0 34.8 %collective-permute-start.15 = (bf16[48,4608]{1,0:T(8,128)(2,1)}, bf16[48,4608]{1,0:T(8,128)(2,1)}, u32[]{:S(2)}, u32[]{:S(2)}) collective-permute-start(bf16[48,4608]{1,0:T(8,128)(2,1)} %pad_maximum_fusion.12), channel_id=1, source_target_pairs={{0,24},{8,16},{16,8},{24,0},{1,25},{9,17},{17,9},{25,1},{2,26},{10... | collective-permute-start | bytes 1327112 | tf_op jit(solution)/shard_map/ppermute | solution.py:200
  148.1 116.3 %all-to-all-start.1 = ((bf16[8,128,768]{1,2,0:T(8,128)(2,1)}), bf16[8,128,768]{1,2,0:T(8,128)(2,1)}, u32[]{:S(2)}, u32[]{:S(2)}) async-start(bf16[8,128,768]{1,2,0:T(8,128)(2,1)} %copy.241), calls=%async_computation.1 | async-start | bytes 3145728 | tf_op jit(solution)/shard_map/all_to_all | solution.py:569
  177.6 71.4 %collective-permute-start.17 = (bf16[4,48,4608]{2,1,0:T(8,128)(2,1)}, bf16[4,48,4608]{2,1,0:T(8,128)(2,1)}, u32[]{:S(2)}, u32[]{:S(2)}) collective-permute-start(bf16[4,48,4608]{2,1,0:T(8,128)(2,1)} %pad_maximum_fusion.6.refs_0_.refs_5_.refs_10_), channel_id=1, source_target_pairs={{0,4},{4,0},{1,5},{5,1},{2,6},{6,2},{3,7},{7,3},{8,12},{12,8},{9,1... | collective-permute-start | bytes 5308424 | tf_op jit(solution)/shard_map/ppermute | solution.py:196
  179.1 65.0 %collective-permute-start.9 = (bf16[2,384,768]{2,1,0:T(8,128)(2,1)S(1)}, bf16[2,384,768]{2,1,0:T(8,128)(2,1)S(1)}, u32[]{:S(2)}, u32[]{:S(2)}) collective-permute-start(bf16[2,384,768]{2,1,0:T(8,128)(2,1)S(1)} %bitcast.279), channel_id=1, source_target_pairs={{0,4},{4,0},{1,5},{5,1},{2,6},{6,2},{3,7},{7,3},{8,12},{12,8},{9,1... | collective-permute-start | bytes 3538952 | tf_op jit(solution)/shard_map/ppermute | solution.py:196
  179.7 78.5 %collective-permute-start.16 = (bf16[4,48,4608]{2,1,0:T(8,128)(2,1)}, bf16[4,48,4608]{2,1,0:T(8,128)(2,1)}, u32[]{:S(2)}, u32[]{:S(2)}) collective-permute-start(bf16[4,48,4608]{2,1,0:T(8,128)(2,1)} %pad_maximum_fusion.6.refs_0_.refs_5_.refs_10_), channel_id=1, source_target_pairs={{0,2},{2,0},{1,3},{3,1},{4,6},{6,4},{5,7},{7,5},{8,10},{10,8},{9,1... | collective-permute-start | bytes 5308424 | tf_op jit(solution)/shard_map/ppermute | solution.py:196
  181.2 65.5 %collective-permute-start.8 = (bf16[2,384,768]{2,1,0:T(8,128)(2,1)S(1)}, bf16[2,384,768]{2,1,0:T(8,128)(2,1)S(1)}, u32[]{:S(2)}, u32[]{:S(2)}) collective-permute-start(bf16[2,384,768]{2,1,0:T(8,128)(2,1)S(1)} %bitcast.280), channel_id=1, source_target_pairs={{0,2},{2,0},{1,3},{3,1},{4,6},{6,4},{5,7},{7,5},{8,10},{10,8},{9,1... | collective-permute-start | bytes 3538952 | tf_op jit(solution)/shard_map/ppermute | solution.py:196
  189.4 96.8 %collective-permute-start.5 = (bf16[1,192,3072]{2,1,0:T(8,128)(2,1)}, bf16[1,192,3072]{2,1,0:T(8,128)(2,1)}, u32[]{:S(2)}, u32[]{:S(2)}) collective-permute-start(bf16[1,192,3072]{2,1,0:T(8,128)(2,1)} %slice.164), channel_id=1, source_target_pairs={{0,2},{2,0},{1,3},{3,1},{4,6},{6,4},{5,7},{7,5},{8,10},{10,8},{9,1... | collective-permute-start | bytes 3538952 | tf_op jit(solution)/shard_map/ppermute | solution.py:196
  244.2 42.0 %collective-permute-start.6 = (bf16[1,192,3072]{2,1,0:T(8,128)(2,1)}, bf16[1,192,3072]{2,1,0:T(8,128)(2,1)}, u32[]{:S(2)}, u32[]{:S(2)}) collective-permute-start(bf16[1,192,3072]{2,1,0:T(8,128)(2,1)} %slice.165), channel_id=1, source_target_pairs={{0,4},{4,0},{1,5},{5,1},{2,6},{6,2},{3,7},{7,3},{8,12},{12,8},{9,1... | collective-permute-start | bytes 3538952 | tf_op jit(solution)/shard_map/ppermute | solution.py:196
  246.7 38.0 %collective-permute-start.10 = (bf16[1,384,768]{2,1,0:T(8,128)(2,1)S(1)}, bf16[1,384,768]{2,1,0:T(8,128)(2,1)}, u32[]{:S(2)}, u32[]{:S(2)}) collective-permute-start(bf16[1,384,768]{2,1,0:T(8,128)(2,1)S(1)} %slice.166), channel_id=1, source_target_pairs={{0,2},{2,0},{1,3},{3,1},{4,6},{6,4},{5,7},{7,5},{8,10},{10,8},{9,1... | collective-permute-start | bytes 1769480 | tf_op jit(solution)/shard_map/ppermute | solution.py:196
  249.0 37.1 %collective-permute-start.11 = (bf16[1,384,768]{2,1,0:T(8,128)(2,1)}, bf16[1,384,768]{2,1,0:T(8,128)(2,1)}, u32[]{:S(2)}, u32[]{:S(2)}) collective-permute-start(bf16[1,384,768]{2,1,0:T(8,128)(2,1)} %slice.167), channel_id=1, source_target_pairs={{0,4},{4,0},{1,5},{5,1},{2,6},{6,2},{3,7},{7,3},{8,12},{12,8},{9,1... | collective-permute-start | bytes 1769480 | tf_op jit(solution)/shard_map/ppermute | solution.py:196
  258.2 129.8 %collective-permute-start.18 = (bf16[2,48,4608]{2,1,0:T(8,128)(2,1)}, bf16[2,48,4608]{2,1,0:T(8,128)(2,1)}, u32[]{:S(2)}, u32[]{:S(2)}) collective-permute-start(bf16[2,48,4608]{2,1,0:T(8,128)(2,1)} %slice.168), channel_id=1, source_target_pairs={{0,2},{2,0},{1,3},{3,1},{4,6},{6,4},{5,7},{7,5},{8,10},{10,8},{9,1... | collective-permute-start | bytes 2654216 | tf_op jit(solution)/shard_map/ppermute | solution.py:196
  284.7 103.3 %collective-permute-start.19 = (bf16[2,48,4608]{2,1,0:T(8,128)(2,1)}, bf16[2,48,4608]{2,1,0:T(8,128)(2,1)}, u32[]{:S(2)}, u32[]{:S(2)}) collective-permute-start(bf16[2,48,4608]{2,1,0:T(8,128)(2,1)} %slice.169), channel_id=1, source_target_pairs={{0,4},{4,0},{1,5},{5,1},{2,6},{6,2},{3,7},{7,3},{8,12},{12,8},{9,1... | collective-permute-start | bytes 2654216 | tf_op jit(solution)/shard_map/ppermute | solution.py:196
  366.7 115.7 %all-to-all-start.2 = ((bf16[8,128,768]{2,1,0:T(8,128)(2,1)}), bf16[8,128,768]{2,1,0:T(8,128)(2,1)}, u32[]{:S(2)}, u32[]{:S(2)}) async-start(bf16[8,128,768]{2,1,0:T(8,128)(2,1)} %bitcast.273), calls=%async_computation.2 | async-start | bytes 3145728 | tf_op jit(solution)/shard_map/all_to_all | solution.py:569
  423.1 54.5 %collective-permute-start.40 = (f32[2,192,1536]{2,1,0:T(8,128)}, f32[2,192,1536]{2,1,0:T(8,128)}, u32[]{:S(2)}, u32[]{:S(2)}) collective-permute-start(f32[2,192,1536]{2,1,0:T(8,128)} %get-tuple-element.129), channel_id=1, source_target_pairs={{0,4},{4,0},{1,5},{5,1},{2,6},{6,2},{3,7},{7,3},{8,12},{12,8},{9,1... | collective-permute-start | bytes 7077896 | tf_op jit(solution)/shard_map/ppermute | solution.py:196
  426.8 59.7 %collective-permute-start.20 = (f32[512,768]{0,1:T(8,128)}, f32[512,768]{0,1:T(8,128)}, u32[]{:S(2)}, u32[]{:S(2)}) collective-permute-start(f32[512,768]{0,1:T(8,128)} %copy.249), channel_id=1, source_target_pairs={{0,1},{1,0},{2,3},{3,2},{4,5},{5,4},{6,7},{7,6},{8,9},{9,8},{10,11... | collective-permute-start | bytes 4718600 | tf_op jit(solution)/shard_map/ppermute | solution.py:196
  436.9 260.0 %collective-permute-start.34 = (f32[768,768]{1,0:T(8,128)}, f32[768,768]{1,0:T(8,128)}, u32[]{:S(2)}, u32[]{:S(2)}) collective-permute-start(f32[768,768]{1,0:T(8,128)} %get-tuple-element.118), channel_id=1, source_target_pairs={{0,2},{2,0},{1,3},{3,1},{4,6},{6,4},{5,7},{7,5},{8,10},{10,8},{9,1... | collective-permute-start | bytes 7077896 | tf_op jit(solution)/shard_map/ppermute | solution.py:196
  438.5 260.0 %collective-permute-start.35 = (f32[768,768]{1,0:T(8,128)}, f32[768,768]{1,0:T(8,128)}, u32[]{:S(2)}, u32[]{:S(2)}) collective-permute-start(f32[768,768]{1,0:T(8,128)} %get-tuple-element.121), channel_id=1, source_target_pairs={{0,2},{2,0},{1,3},{3,1},{4,6},{6,4},{5,7},{7,5},{8,10},{10,8},{9,1... | collective-permute-start | bytes 7077896 | tf_op jit(solution)/shard_map/ppermute | solution.py:196
  438.9 92.7 %collective-permute-start.55 = (f32[2,192,1536]{2,1,0:T(8,128)}, f32[2,192,1536]{2,1,0:T(8,128)}, u32[]{:S(2)}, u32[]{:S(2)}) collective-permute-start(f32[2,192,1536]{2,1,0:T(8,128)} %get-tuple-element.148), channel_id=1, source_target_pairs={{0,4},{4,0},{1,5},{5,1},{2,6},{6,2},{3,7},{7,3},{8,12},{12,8},{9,1... | collective-permute-start | bytes 7077896 | tf_op jit(solution)/shard_map/ppermute | solution.py:196
  477.6 114.2 %collective-permute-start.51 = (f32[2,192,1536]{2,1,0:T(8,128)}, f32[2,192,1536]{2,1,0:T(8,128)}, u32[]{:S(2)}, u32[]{:S(2)}) collective-permute-start(f32[2,192,1536]{2,1,0:T(8,128)} %get-tuple-element.140), channel_id=1, source_target_pairs={{0,2},{2,0},{1,3},{3,1},{4,6},{6,4},{5,7},{7,5},{8,10},{10,8},{9,1... | collective-permute-start | bytes 7077896 | tf_op jit(solution)/shard_map/ppermute | solution.py:196
  530.5 84.3 %collective-permute-start.21 = (f32[768,1152]{1,0:T(8,128)}, f32[768,1152]{1,0:T(8,128)}, u32[]{:S(2)}, u32[]{:S(2)}) collective-permute-start(f32[768,1152]{1,0:T(8,128)} %fusion.44), channel_id=1, source_target_pairs={{0,1},{1,0},{2,3},{3,2},{4,5},{5,4},{6,7},{7,6},{8,9},{9,8},{10,11... | collective-permute-start | bytes 10616840 | tf_op jit(solution)/shard_map/ppermute | solution.py:196
  601.7 11.6 %collective-permute-start.22 = (f32[768,384]{1,0:T(8,128)}, f32[768,384]{1,0:T(8,128)}, u32[]{:S(2)}, u32[]{:S(2)}) collective-permute-start(f32[768,384]{1,0:T(8,128)} %fusion.72), channel_id=1, source_target_pairs={{0,1},{1,0},{2,3},{3,2},{4,5},{5,4},{6,7},{7,6},{8,9},{9,8},{10,11... | collective-permute-start | bytes 3538952 | tf_op jit(solution)/shard_map/ppermute | solution.py:196
  610.4 53.6 %collective-permute-start.33 = (f32[192,1536]{1,0:T(8,128)}, f32[192,1536]{1,0:T(8,128)S(1)}, u32[]{:S(2)}, u32[]{:S(2)}) collective-permute-start(f32[192,1536]{1,0:T(8,128)} %get-tuple-element.116), channel_id=1, source_target_pairs={{0,8},{8,0},{16,24},{24,16},{1,9},{9,1},{17,25},{25,17},{2,10},{10... | collective-permute-start | bytes 3538952 | tf_op jit(solution)/shard_map/ppermute | solution.py:200
  613.3 80.6 %collective-permute-start.36 = (f32[192,1536]{1,0:T(8,128)}, f32[192,1536]{1,0:T(8,128)S(1)}, u32[]{:S(2)}, u32[]{:S(2)}) collective-permute-start(f32[192,1536]{1,0:T(8,128)} %get-tuple-element.124), channel_id=1, source_target_pairs={{0,16},{8,24},{16,0},{24,8},{1,17},{9,25},{17,1},{25,9},{2,18},{10... | collective-permute-start | bytes 3538952 | tf_op jit(solution)/shard_map/ppermute | solution.py:200
  614.8 79.1 %collective-permute-start.37 = (f32[192,1536]{1,0:T(8,128)}, f32[192,1536]{1,0:T(8,128)S(1)}, u32[]{:S(2)}, u32[]{:S(2)}) collective-permute-start(f32[192,1536]{1,0:T(8,128)} %get-tuple-element.126), channel_id=1, source_target_pairs={{0,24},{8,16},{16,8},{24,0},{1,25},{9,17},{17,9},{25,1},{2,26},{10... | collective-permute-start | bytes 3538952 | tf_op jit(solution)/shard_map/ppermute | solution.py:200
  664.0 53.6 %collective-permute-start.45 = (f32[192,1536]{1,0:T(8,128)S(1)}, f32[192,1536]{1,0:T(8,128)S(1)}, u32[]{:S(2)}, u32[]{:S(2)}) collective-permute-start(f32[192,1536]{1,0:T(8,128)S(1)} %copy-done.75), channel_id=1, source_target_pairs={{0,8},{8,0},{16,24},{24,16},{1,9},{9,1},{17,25},{25,17},{2,10},{10... | collective-permute-start | bytes 3538952 | tf_op jit(solution)/shard_map/ppermute | solution.py:200
  693.9 101.1 %collective-permute-start.46 = (f32[192,1536]{1,0:T(8,128)S(1)}, f32[192,1536]{1,0:T(8,128)S(1)}, u32[]{:S(2)}, u32[]{:S(2)}) collective-permute-start(f32[192,1536]{1,0:T(8,128)S(1)} %copy-done.74), channel_id=1, source_target_pairs={{0,16},{8,24},{16,0},{24,8},{1,17},{9,25},{17,1},{25,9},{2,18},{10... | collective-permute-start | bytes 3538952 | tf_op jit(solution)/shard_map/ppermute | solution.py:200
  693.9 106.2 %collective-permute-start.57 = (f32[2,192,1536]{2,1,0:T(8,128)S(1)}, f32[2,192,1536]{2,1,0:T(8,128)S(1)}, u32[]{:S(2)}, u32[]{:S(2)}) collective-permute-start(f32[2,192,1536]{2,1,0:T(8,128)S(1)} %copy-done.72), channel_id=1, source_target_pairs={{0,4},{4,0},{1,5},{5,1},{2,6},{6,2},{3,7},{7,3},{8,12},{12,8},{9,1... | collective-permute-start | bytes 7077896 | tf_op jit(solution)/shard_map/ppermute | solution.py:196
  696.9 100.8 %collective-permute-start.47 = (f32[192,1536]{1,0:T(8,128)S(1)}, f32[192,1536]{1,0:T(8,128)S(1)}, u32[]{:S(2)}, u32[]{:S(2)}) collective-permute-start(f32[192,1536]{1,0:T(8,128)S(1)} %copy-done.73), channel_id=1, source_target_pairs={{0,24},{8,16},{16,8},{24,0},{1,25},{9,17},{17,9},{25,1},{2,26},{10... | collective-permute-start | bytes 3538952 | tf_op jit(solution)/shard_map/ppermute | solution.py:200
  699.2 121.8 %collective-permute-start.53 = (f32[2,192,1536]{2,1,0:T(8,128)S(1)}, f32[2,192,1536]{2,1,0:T(8,128)S(1)}, u32[]{:S(2)}, u32[]{:S(2)}) collective-permute-start(f32[2,192,1536]{2,1,0:T(8,128)S(1)} %copy-done.71), channel_id=1, source_target_pairs={{0,2},{2,0},{1,3},{3,1},{4,6},{6,4},{5,7},{7,5},{8,10},{10,8},{9,1... | collective-permute-start | bytes 7077896 | tf_op jit(solution)/shard_map/ppermute | solution.py:196
  717.6 85.6 %collective-permute-start.56 = (f32[192,1536]{1,0:T(8,128)S(1)}, f32[192,1536]{1,0:T(8,128)S(1)}, u32[]{:S(2)}, u32[]{:S(2)}) collective-permute-start(f32[192,1536]{1,0:T(8,128)S(1)} %copy-done.42), channel_id=1, source_target_pairs={{0,2},{2,0},{1,3},{3,1},{4,6},{6,4},{5,7},{7,5},{8,10},{10,8},{9,1... | collective-permute-start | bytes 3538952 | tf_op jit(solution)/shard_map/ppermute | solution.py:196
  795.0 26.0 %collective-permute-start.52 = (f32[192,1536]{1,0:T(8,128)S(1)}, f32[192,1536]{1,0:T(8,128)S(1)}, u32[]{:S(2)}, u32[]{:S(2)}) collective-permute-start(f32[192,1536]{1,0:T(8,128)S(1)} %copy-done.41), channel_id=1, source_target_pairs={{0,4},{4,0},{1,5},{5,1},{2,6},{6,2},{3,7},{7,3},{8,12},{12,8},{9,1... | collective-permute-start | bytes 3538952 | tf_op jit(solution)/shard_map/ppermute | solution.py:196
  797.7 287.7 %collective-permute-start.24 = (f32[512,768]{0,1:T(8,128)}, f32[512,768]{0,1:T(8,128)}, u32[]{:S(2)}, u32[]{:S(2)}) collective-permute-start(f32[512,768]{0,1:T(8,128)} %copy.262), channel_id=1, source_target_pairs={{0,1},{1,0},{2,3},{3,2},{4,5},{5,4},{6,7},{7,6},{8,9},{9,8},{10,11... | collective-permute-start | bytes 4718600 | tf_op jit(solution)/shard_map/ppermute | solution.py:196
  800.0 28.8 %collective-permute-start.41 = (f32[192,1536]{1,0:T(8,128)S(1)}, f32[192,1536]{1,0:T(8,128)S(1)}, u32[]{:S(2)}, u32[]{:S(2)}) collective-permute-start(f32[192,1536]{1,0:T(8,128)S(1)} %copy-done.40), channel_id=1, source_target_pairs={{0,2},{2,0},{1,3},{3,1},{4,6},{6,4},{5,7},{7,5},{8,10},{10,8},{9,1... | collective-permute-start | bytes 3538952 | tf_op jit(solution)/shard_map/ppermute | solution.py:196
  803.2 101.2 %collective-permute-start.38 = (f32[2,1,48,1536]{3,2,1,0:T(8,128)}, f32[2,1,48,1536]{3,2,1,0:T(8,128)}, u32[]{:S(2)}, u32[]{:S(2)}) collective-permute-start(f32[2,1,48,1536]{3,2,1,0:T(8,128)} %split.43), channel_id=1, source_target_pairs={{0,2},{2,0},{1,3},{3,1},{4,6},{6,4},{5,7},{7,5},{8,10},{10,8},{9,1... | collective-permute-start | bytes 1769480 | tf_op jit(solution)/shard_map/ppermute | solution.py:196
  829.9 61.3 %collective-permute-start.42 = (f32[48,1536]{1,0:T(8,128)}, f32[48,1536]{1,0:T(8,128)}, u32[]{:S(2)}, u32[]{:S(2)}) collective-permute-start(f32[48,1536]{1,0:T(8,128)} %get-tuple-element.267), channel_id=1, source_target_pairs={{0,8},{8,0},{16,24},{24,16},{1,9},{9,1},{17,25},{25,17},{2,10},{10... | collective-permute-start | bytes 884744 | tf_op jit(solution)/shard_map/ppermute | solution.py:200
  881.2 19.7 %collective-permute-start.43 = (f32[48,1536]{1,0:T(8,128)}, f32[48,1536]{1,0:T(8,128)}, u32[]{:S(2)}, u32[]{:S(2)}) collective-permute-start(f32[48,1536]{1,0:T(8,128)} %get-tuple-element.269), channel_id=1, source_target_pairs={{0,16},{8,24},{16,0},{24,8},{1,17},{9,25},{17,1},{25,9},{2,18},{10... | collective-permute-start | bytes 884744 | tf_op jit(solution)/shard_map/ppermute | solution.py:200
  881.2 20.3 %collective-permute-start.44 = (f32[48,1536]{1,0:T(8,128)S(1)}, f32[48,1536]{1,0:T(8,128)}, u32[]{:S(2)}, u32[]{:S(2)}) collective-permute-start(f32[48,1536]{1,0:T(8,128)S(1)} %get-tuple-element.268), channel_id=1, source_target_pairs={{0,24},{8,16},{16,8},{24,0},{1,25},{9,17},{17,9},{25,1},{2,26},{10... | collective-permute-start | bytes 884744 | tf_op jit(solution)/shard_map/ppermute | solution.py:200
  886.5 196.2 %all-to-all-start.3 = ((bf16[8,128,768]{2,1,0:T(8,128)(2,1)}), bf16[8,128,768]{2,1,0:T(8,128)(2,1)}, u32[]{:S(2)}, u32[]{:S(2)}) async-start(bf16[8,128,768]{2,1,0:T(8,128)(2,1)} %bitcast.272), calls=%async_computation.3 | async-start | bytes 3145728 | tf_op jit(solution)/shard_map/all_to_all | solution.py:569
  891.2 178.1 %collective-permute-start.60 = (f32[768,768]{1,0:T(8,128)}, f32[768,768]{1,0:T(8,128)}, u32[]{:S(2)}, u32[]{:S(2)}) collective-permute-start(f32[768,768]{1,0:T(8,128)} %broadcast_select_fusion), channel_id=1, source_target_pairs={{0,4},{4,0},{1,5},{5,1},{2,6},{6,2},{3,7},{7,3},{8,12},{12,8},{9,1... | collective-permute-start | bytes 7077896 | tf_op jit(solution)/shard_map/ppermute | solution.py:196
  900.9 16.4 %collective-permute-start.48 = (f32[2,1,48,1536]{3,2,1,0:T(8,128)}, f32[2,1,48,1536]{3,2,1,0:T(8,128)S(1)}, u32[]{:S(2)}, u32[]{:S(2)}) collective-permute-start(f32[2,1,48,1536]{3,2,1,0:T(8,128)} %split.45), channel_id=1, source_target_pairs={{0,2},{2,0},{1,3},{3,1},{4,6},{6,4},{5,7},{7,5},{8,10},{10,8},{9,1... | collective-permute-start | bytes 1769480 | tf_op jit(solution)/shard_map/ppermute | solution.py:196
  901.5 116.5 %collective-permute-start.27 = (f32[2,2,48,1664]{3,2,1,0:T(8,128)}, f32[2,2,48,1664]{3,2,1,0:T(8,128)}, u32[]{:S(2)}, u32[]{:S(2)}) collective-permute-start(f32[2,2,48,1664]{3,2,1,0:T(8,128)} %dynamic-slice_bitcast_fusion), channel_id=1, source_target_pairs={{0,4},{4,0},{1,5},{5,1},{2,6},{6,2},{3,7},{7,3},{8,12},{12,8},{9,1... | collective-permute-start | bytes 3833864 | tf_op jit(solution)/shard_map/ppermute | solution.py:196
  904.3 85.8 %collective-permute-start.58 = (f32[192,1536]{1,0:T(8,128)}, f32[192,1536]{1,0:T(8,128)}, u32[]{:S(2)}, u32[]{:S(2)}) collective-permute-start(f32[192,1536]{1,0:T(8,128)} %slice_bitcast_fusion), channel_id=1, source_target_pairs={{0,2},{2,0},{1,3},{3,1},{4,6},{6,4},{5,7},{7,5},{8,10},{10,8},{9,1... | collective-permute-start | bytes 3538952 | tf_op jit(solution)/shard_map/ppermute | solution.py:196
  917.3 60.9 %collective-permute-start.39 = (f32[1,48,1536]{2,1,0:T(8,128)S(1)}, f32[1,48,1536]{2,1,0:T(8,128)S(1)}, u32[]{:S(2)}, u32[]{:S(2)}) collective-permute-start(f32[1,48,1536]{2,1,0:T(8,128)S(1)} %slice_bitcast_fusion.12), channel_id=1, source_target_pairs={{0,4},{4,0},{1,5},{5,1},{2,6},{6,2},{3,7},{7,3},{8,12},{12,8},{9,1... | collective-permute-start | bytes 884744 | tf_op jit(solution)/shard_map/ppermute | solution.py:196
  978.3 8.0 collective-permute-start.49
  986.3 26.4 %collective-permute-start.54 = (f32[192,1536]{1,0:T(8,128)}, f32[192,1536]{1,0:T(8,128)}, u32[]{:S(2)}, u32[]{:S(2)}) collective-permute-start(f32[192,1536]{1,0:T(8,128)} %slice_bitcast_fusion.4), channel_id=1, source_target_pairs={{0,4},{4,0},{1,5},{5,1},{2,6},{6,2},{3,7},{7,3},{8,12},{12,8},{9,1... | collective-permute-start | bytes 3538952 | tf_op jit(solution)/shard_map/ppermute | solution.py:196
  990.1 30.7 %collective-permute-start.25 = (f32[2,2,48,1664]{3,2,1,0:T(8,128)}, f32[2,2,48,1664]{3,2,1,0:T(8,128)S(1)}, u32[]{:S(2)}, u32[]{:S(2)}) collective-permute-start(f32[2,2,48,1664]{3,2,1,0:T(8,128)} %dynamic-slice_bitcast_fusion.1), channel_id=1, source_target_pairs={{0,2},{2,0},{1,3},{3,1},{4,6},{6,4},{5,7},{7,5},{8,10},{10,8},{9,1... | collective-permute-start | bytes 3833864 | tf_op jit(solution)/shard_map/ppermute | solution.py:196
  1012.8 12.6 %collective-permute-start.50 = (f32[24,4608]{1,0:T(8,128)S(1)}, f32[24,4608]{1,0:T(8,128)}, u32[]{:S(2)}, u32[]{:S(2)}) collective-permute-start(f32[24,4608]{1,0:T(8,128)S(1)} %copy-done.50), channel_id=1, source_target_pairs={{0,1},{1,0},{2,3},{3,2},{4,5},{5,4},{6,7},{7,6},{8,9},{9,8},{10,11... | collective-permute-start | bytes 1327112 | tf_op jit(solution)/shard_map/ppermute | solution.py:196
  1020.2 16.9 %collective-permute-start.28 = (f32[2,48,1664]{2,1,0:T(8,128)}, f32[2,48,1664]{2,1,0:T(8,128)}, u32[]{:S(2)}, u32[]{:S(2)}) collective-permute-start(f32[2,48,1664]{2,1,0:T(8,128)} %bitcast_add_fusion), channel_id=1, source_target_pairs={{0,2},{2,0},{1,3},{3,1},{4,6},{6,4},{5,7},{7,5},{8,10},{10,8},{9,1... | collective-permute-start | bytes 1916936 | tf_op jit(solution)/shard_map/ppermute | solution.py:196
  1023.8 16.7 %collective-permute-start.26 = (f32[2,48,1664]{2,1,0:T(8,128)}, f32[2,48,1664]{2,1,0:T(8,128)}, u32[]{:S(2)}, u32[]{:S(2)}) collective-permute-start(f32[2,48,1664]{2,1,0:T(8,128)} %bitcast_add_fusion.2), channel_id=1, source_target_pairs={{0,4},{4,0},{1,5},{5,1},{2,6},{6,2},{3,7},{7,3},{8,12},{12,8},{9,1... | collective-permute-start | bytes 1916936 | tf_op jit(solution)/shard_map/ppermute | solution.py:196
  1042.1 14.7 %collective-permute-start.29 = (f32[48,1664]{1,0:T(8,128)S(1)}, f32[48,1664]{1,0:T(8,128)S(1)}, u32[]{:S(2)}, u32[]{:S(2)}) collective-permute-start(f32[48,1664]{1,0:T(8,128)S(1)} %get-tuple-element.259), channel_id=1, source_target_pairs={{0,8},{8,0},{16,24},{24,16},{1,9},{9,1},{17,25},{25,17},{2,10},{10... | collective-permute-start | bytes 958472 | tf_op jit(solution)/shard_map/ppermute | solution.py:200
  1044.1 25.0 %collective-permute-start.30 = (f32[48,1664]{1,0:T(8,128)S(1)}, f32[48,1664]{1,0:T(8,128)S(1)}, u32[]{:S(2)}, u32[]{:S(2)}) collective-permute-start(f32[48,1664]{1,0:T(8,128)S(1)} %get-tuple-element.260), channel_id=1, source_target_pairs={{0,16},{8,24},{16,0},{24,8},{1,17},{9,25},{17,1},{25,9},{2,18},{10... | collective-permute-start | bytes 958472 | tf_op jit(solution)/shard_map/ppermute | solution.py:200
  1046.5 22.6 %collective-permute-start.31 = (f32[48,1664]{1,0:T(8,128)S(1)}, f32[48,1664]{1,0:T(8,128)S(1)}, u32[]{:S(2)}, u32[]{:S(2)}) collective-permute-start(f32[48,1664]{1,0:T(8,128)S(1)} %get-tuple-element.261), channel_id=1, source_target_pairs={{0,24},{8,16},{16,8},{24,0},{1,25},{9,17},{17,9},{25,1},{2,26},{10... | collective-permute-start | bytes 958472 | tf_op jit(solution)/shard_map/ppermute | solution.py:200
  1056.8 40.7 %collective-permute-start.59 = (f32[2,96,3072]{2,1,0:T(8,128)}, f32[2,96,3072]{2,1,0:T(8,128)}, u32[]{:S(2)}, u32[]{:S(2)}) collective-permute-start(f32[2,96,3072]{2,1,0:T(8,128)} %fusion.3), channel_id=1, source_target_pairs={{0,1},{1,0},{2,3},{3,2},{4,5},{5,4},{6,7},{7,6},{8,9},{9,8},{10,11... | collective-permute-start | bytes 7077896 | tf_op jit(solution)/shard_map/ppermute | solution.py:196
  1069.3 6.3 collective-permute-start.32
  1075.0 15.6 %collective-permute-start.61 = (f32[768,384]{1,0:T(8,128)}, f32[768,384]{1,0:T(8,128)}, u32[]{:S(2)}, u32[]{:S(2)}) collective-permute-start(f32[768,384]{1,0:T(8,128)} %slice_select_fusion), channel_id=1, source_target_pairs={{0,1},{1,0},{2,3},{3,2},{4,5},{5,4},{6,7},{7,6},{8,9},{9,8},{10,11... | collective-permute-start | bytes 3538952 | tf_op jit(solution)/shard_map/ppermute | solution.py:196
  (80 other events, 1038.7 us)

commit v2 on v1

--- a/solution.py
+++ b/solution.py
@@ -204,9 +204,13 @@
     return lax.dynamic_index_in_dim(array, idx, axis, keepdims=False)
 
 
+def core_sorted(mine, other):
+    first = lax.axis_index('c') == 0
+    return jnp.where(first, mine, other), jnp.where(first, other, mine)
+
+
 def in_core_order(mine, other, axis):
-    first = lax.axis_index('c') == 0
-    return jnp.concatenate([jnp.where(first, mine, other), jnp.where(first, other, mine)], axis=axis)
+    return jnp.concatenate(core_sorted(mine, other), axis=axis)
 
 
 def core_halves(array, axis):
@@ -215,28 +219,22 @@
     return jnp.where(first, low, high), jnp.where(first, high, low)
 
 
-def plane_first(block):
-    return block, hop(block, 'x'), hop(block, 'y')
-
-
-def plane_pieces(first):
-    block, from_x, from_y = first
-    half = block.shape[0] // 2
-    return block, from_x, from_y, hop(from_y[:half], 'x'), hop(from_x[half:], 'y')
+def plane_near(halves):
+    return [hop(half, 'x') for half in halves], [hop(half, 'y') for half in halves]
 
 
 def after(value, *anchors):
     return lax.optimization_barrier((value,) + anchors)[0]
 
 
-def z_stack(parts, gate):
+def z_parts(parts):
     half = parts[0].shape[1] // 2
     c_me = lax.axis_index('c')
 
     def side(core):
         return jnp.concatenate([lax.dynamic_slice_in_dim(part, core * half, half, axis=1) for part in parts], axis=1)
 
-    chip = after(in_core_order(side(c_me), hop(side(1 - c_me), 'c'), 0), gate)
+    chip = in_core_order(side(c_me), hop(side(1 - c_me), 'c'), 0)
     return [chip] + [z_hop(chip, step) for step in Z_STEPS]
 
 
@@ -316,12 +314,10 @@
     )(*blocks)
 
 
-def expert_chips(w1_expert, w3_expert, w2_expert):
+def expert_halves(w1_expert, w3_expert, w2_expert):
     c_me = lax.axis_index('c')
-    up = jnp.stack([w1_expert, w3_expert])
-    up_chip = in_core_order(pick(up, c_me, 1), hop(pick(up, 1 - c_me, 1), 'c'), 1)
-    down_chip = in_core_order(pick(w2_expert, c_me, 0), hop(pick(w2_expert, 1 - c_me, 0), 'c'), 0)
-    return up_chip, down_chip.reshape(2, -1, down_chip.shape[1])
+    down = core_sorted(pick(w2_expert, c_me, 0), hop(pick(w2_expert, 1 - c_me, 0), 'c'))
+    return [in_core_order(pick(w, c_me, 0), hop(pick(w, 1 - c_me, 0), 'c'), 0) for w in (w1_expert, w3_expert)], down
 
 
 def dot32(lhs, rhs):
@@ -360,14 +356,14 @@
 
 
 def expert_kernel(half, info, rows_ref, dd_ref, rows_t_ref, dd_t_ref, *refs):
-    up_refs, down_refs, refs = refs[:8], refs[8:13], refs[13:]
+    up_refs, down_refs, refs = refs[:8], refs[8:16], refs[16:]
     if half == 1:
         acc_in, refs = refs[:2], refs[2:]
     out_ref, back_ref, g1_away, g1_near, g3_away, g3_near, g2_away, g2_near = refs[:8]
     w1, w3, w2, act_s, dg_s, dl_s, out_acc, back_acc, lhs_s, sems = refs[8:]
     step, me = pl.program_id(0), info[0]
     same_y = (me // 2) == half
-    pieces = [(ref.at[0], ref.at[1]) for ref in down_refs[:3]] + [[ref.at[0] for ref in down_refs[3:]]]
+    pieces = [down_refs[2 * rel:2 * rel + 2] for rel in range(QUAD)]
     w2_halves = [w2.at[pl.ds(part * 384, 384)] for part in range(2)]
     for rel, srcs in enumerate(pieces):
         @pl.when(jnp.logical_and(same_y == (rel < 2), (step == 0) == (rel % 2 == 1)))
@@ -388,8 +384,7 @@
 
     for rel in range(QUAD):
         at = pl.ds(pl.multiple_of((me ^ rel) * 192, 64), 192)
-        w1[at, :] = up_refs[rel][0]
-        w3[at, :] = up_refs[4 + rel][0]
+        w1[at, :], w3[at, :] = (ref[:] for ref in up_refs[2 * rel:2 * rel + 2])
 
     def wait_w2(idx):
         @pl.when(idx == 0)
@@ -420,12 +415,7 @@
     info = jnp.stack([2 * y_me + x_me, 2 * half + 1 - x_me, 2 * half + x_me]).astype(jnp.int32)
     whole, turned = fixed(tok, dim), fixed(dim, tok)
 
-    def up_spec(mat):
-        return pl.BlockSpec((1, dim // QUAD, dim), lambda step, info_ref, mat=mat: (mat, 0, info_ref[1 + step]))
-
-    own, from_x, from_y, low, high = up
-    up_args = (own, from_x, from_y, low, own, from_x, from_y, high)
-    up_specs = [up_spec(0)] * QUAD + [up_spec(1)] * 3 + [up_spec(0)]
+    up_spec = pl.BlockSpec((dim // QUAD, dim), lambda step, info_ref: (0, info_ref[1 + step]))
     any_spec = pl.BlockSpec(memory_space=pl.ANY)
     row_out = pl.BlockSpec((2, dim // QUAD, dim), lambda step, info_ref: (0, 0, info_ref[1 + step] - 2 * half))
     square = fixed(dim, dim)
@@ -435,17 +425,17 @@
         lambda *refs: expert_kernel(half, *refs),
         grid_spec=pltpu.PrefetchScalarGridSpec(
             num_scalar_prefetch=1, grid=(2,),
-            in_specs=[whole, whole, turned, turned] + up_specs + [any_spec] * 5 + [whole] * len(acc),
+            in_specs=[whole, whole, turned, turned] + [up_spec] * 8 + [any_spec] * 8 + [whole] * len(acc),
             out_specs=[whole, whole] + [row_out] * QUAD + [square] * 2,
             scratch_shapes=[pltpu.VMEM((dim, dim), BF16)] * 3 + [pltpu.VMEM((tok, dim), BF16)] * 3 + [pltpu.VMEM((tok, dim), F32)] * 2 + [pltpu.VMEM((QUAD, dim // QUAD, tok), BF16), pltpu.SemaphoreType.DMA((2,))]),
         out_shape=[jax.ShapeDtypeStruct((tok, dim), acc_type)] * 2 + [row_shape] * QUAD + [square_shape] * 2,
         compiler_params=pltpu.CompilerParams(vmem_limit_bytes=VMEM_LIMIT),
         cost_estimate=kernel_cost(36 * tok * dim * dim, dim * dim),
-    )(info, rows, dd, rows_t, dd_t, *up_args, *down, *acc)
+    )(info, rows, dd, rows_t, dd_t, *up, *down, *acc)
 
 
 def shared_kernel(info, rows_ref, dd_ref, rows_t_ref, dd_t_ref, *refs):
-    pieces, refs = [refs[5 * mat:5 * mat + 5] for mat in range(3)], refs[15:]
+    pieces, refs = [refs[8 * mat:8 * mat + 8] for mat in range(3)], refs[24:]
     out_refs, back_refs, g3_away, g3_near, g1_refs, g2_refs = refs[:2], refs[2:4], refs[4], refs[5], refs[6:10], refs[10:14]
     w1, w3, w2, act_s, dg_s, dl_s, out_acc, back_acc, lhs_s, lhs_z, dd_z = refs[14:]
     step, me, z_me = pl.program_id(0), info[0], info[1]
@@ -464,13 +454,13 @@
                 lhs_z[turn_z, inner, :] = rows_t_ref[spot(rel, turn_z), :]
                 dd_z[turn_z, inner, :] = dd_t_ref[spot(rel, turn_z), :]
 
-    for w_ref, (own, from_x, from_y, low, high) in zip((w1, w3, w2), pieces):
+    for w_ref, halves in zip((w1, w3, w2), pieces):
         for turn_z in range(QUAD):
-            for rel, src in enumerate((own.at[turn_z], from_x.at[turn_z], from_y.at[turn_z], low.at[turn_z] if turn_z < 2 else high.at[turn_z - 2])):
-                w_ref[spot(rel, turn_z), :] = src[:]
+            for rel in range(QUAD):
+                w_ref[spot(rel, turn_z), :] = halves[2 * rel + turn_z // 2][turn_z % 2]
 
     ffn_rows(rows_ref, dd_ref, w1, w3, w2, True, None, act_s, dg_s, dl_s, out_acc, back_acc)
-    row_grads(lhs_s, dl_s, g3_away, g3_near, False)
+    row_grads(lhs_s, dl_s, g3_away, g3_near, True)
     for turn_z in range(QUAD):
         g1_refs[turn_z][:] = dot_nn(lhs_z[turn_z], dg_s[:])
         g2_refs[turn_z][:] = dot_nn(dd_z[turn_z], act_s[:])
@@ -488,7 +478,7 @@
     steps = width // dim
     info = after(jnp.stack([2 * lax.axis_index('y') + lax.axis_index('x'), lax.axis_index('z')]).astype(jnp.int32), gate)
     whole, turned, half = fixed(tok, dim), fixed(dim, tok), fixed(tok // 2, dim)
-    piece_specs = [pl.BlockSpec((piece.shape[0], ROWS, dim), lambda step, info_ref, mat=mat: (0, 0, mat * steps + step)) for mat in range(3) for piece in pieces]
+    piece_specs = [pl.BlockSpec((2, ROWS, dim), lambda step, info_ref, mat=mat: (0, 0, mat * steps + step)) for mat in range(3) for _ in pieces]
     row_out = pl.BlockSpec((2, dim // QUAD, dim), lambda step, info_ref: (0, 0, step))
     z_out = pl.BlockSpec((dim // QUAD, dim), lambda step, info_ref: (0, step))
     shapes = ((tok // 2, dim),) * QUAD + ((2, dim // QUAD, width),) * 2 + ((dim // QUAD, width),) * 8
@@ -535,10 +525,6 @@
     return gives, rest
 
 
-def swap_experts(summed):
-    return in_core_order(*(part[None] for part in swap_rows(summed)), 0)
-
-
 def layer_step(x_in, grad_y, w_q, w_k, w_v, w_o, gamma_attn, gamma_mlp, w_router, w1_shared, w3_shared, w2_shared, w1_expert, w3_expert, w2_expert, expert_ids):
     n_batch, seq_len, model_dim = x_in.shape
     n_tok = n_batch * seq_len
@@ -549,17 +535,23 @@
     capacity = 2 * n_tok // n_experts
     n_slots = n_experts * capacity
 
+    up_own, down_own = expert_halves(w1_expert, w3_expert, w2_expert)
+    down_x, down_y = plane_near(down_own)
+    w_q, w_k, w_v, w_o = (after(weight, *down_own) for weight in (w_q, w_k, w_v, w_o))
     att_parts = (w_q.reshape(-1, att_dim), w_k.reshape(-1, att_dim), w_v.reshape(-1, att_dim), w_o.reshape(att_dim, -1).T)
     att_block = jnp.concatenate([part[:, :att_half] for part in att_parts] + [part[:, att_half:] for part in att_parts], axis=1)
     small = jnp.concatenate([gamma_attn.astype(F32)[:, None], gamma_mlp.astype(F32)[:, None], w_router], axis=1)
     small = jnp.pad(small, ((0, 0), (0, LANES - small.shape[1])))
-    up_chip, down_chip = expert_chips(w1_expert, w3_expert, w2_expert)
     att_all, small_all = gather_weights(att_block, small)
     att_all, small_all = att_all.reshape(model_dim, -1), small_all.reshape(model_dim, -1)
     ga_all, gm_all, wr_all = small_all[:, 0], small_all[:, 1], small_all[:, 2:2 + n_experts]
-    down_first = plane_first(down_chip)
-    up_first = plane_first(up_chip)
-    sh_parts = z_stack((w1_shared, w3_shared, w2_shared.T), small_all)
+
+    def far(from_x, from_y, *gates):
+        return [hop(after(from_y[0], *gates), 'x'), hop(after(from_x[1], *gates), 'y')]
+
+    down_far = far(down_x, down_y, small_all)
+    up_x, up_y = plane_near(up_own)
+    sh_parts = z_parts([after(weight, small_all) for weight in (w1_shared, w3_shared, w2_shared.T)])
 
     d_out = grad_y.reshape(n_tok, model_dim)
     onehot, dest_row = route_slots(expert_ids.reshape(n_tok), n_experts, capacity)
@@ -596,14 +588,13 @@
 
     normed2_both = jnp.concatenate([normed2, hop(normed2, 'c')], axis=0)
     normed2_t = normed2_both.T
-    sh_first = plane_first(jnp.stack([after(part, heads) for part in sh_parts]))
-
-    def settle(pieces):
-        return [after(piece, give_r, give_d, normed2_t, d_out_t) for piece in pieces]
-
-    sh_pieces = plane_pieces(settle(sh_first))
-    down_pieces = plane_pieces(settle(down_first))
-    up_pieces = plane_pieces(settle(up_first))
+    sh_parts = [after(part, heads) for part in sh_parts]
+    sh_own = jnp.stack(sh_parts[:2]), jnp.stack(sh_parts[2:])
+    sh_x, sh_y = plane_near(sh_own)
+
+    up_far = far(up_x, up_y, give_r)
+    sh_far = far(sh_x, sh_y, give_r, give_d, normed2_t, d_out_t)
+    sh_pieces, up_pieces, down_pieces = ([*own, *from_x, *from_y, *diag] for own, from_x, from_y, diag in ((sh_own, sh_x, sh_y, sh_far), (up_own, up_x, up_y, up_far), (down_own, down_x, down_y, down_far)))
     shared_part, d_part, (s3_away, s3_near), s1, s2 = shared_ffn(rows_t, normed2_both, d_out_both, normed2_t, d_out_t, sh_pieces)
     shared_out = shared_part[0] + hop(shared_part[1], 'c')
     d_normed2 = d_part[0] + hop(d_part[1], 'c')
@@ -616,8 +607,8 @@
         keep, give = near + after(hop(away, axis), *gate)
         return keep, hop(give, 'y' if axis == 'x' else 'x')
 
-    s3 = first_sum(s3_away, s3_near, 'y', [d_rows])
-    a1, a3 = first_sum(a1_away, a1_near, 'x', [d_rows]), first_sum(a3_away, a3_near, 'y', [d_rows])
+    s3 = first_sum(s3_away, s3_near, 'x', [d_rows])
+    a1 = first_sum(a1_away, a1_near, 'x', [d_rows])
     d_routed_in = jnp.einsum('ts,sd->td', place, d_back, preferred_element_type=F32)
     d_normed2 = d_normed2 + gate_val[:, None] * d_routed_in
     d_gate_val = jnp.sum(d_routed_in * normed2_f, axis=1) * gate_val * (1.0 - gate_val)
@@ -670,17 +661,21 @@
     b_gates = [s1[1], s2[1]]
     routed = jnp.einsum('ts,sd->td', place, exchange(later(down_rows)), preferred_element_type=F32)
     layer_out = (hidden.astype(F32) + routed + shared_out).astype(BF16)
+    a3 = first_sum(a3_away, a3_near, 'y', att_gives)
     b1, b3 = first_sum(b1_away, b1_near, 'x', b_gates), first_sum(b3_away, b3_near, 'y', b_gates)
 
-    def finish(pairs):
-        return jnp.concatenate([mine + later(got) for mine, got in pairs], axis=1)
-
-    g_w1, g_w3 = finish((a1, b1)), finish((a3, b3))
+    def finish(pair, *gates):
+        mine, got = pair
+        return mine + later(after(got, *gates) if gates else got)
+
+    def rows_by_expert(pairs, *gates):
+        return in_core_order(*(part[None] for part in swap_rows(jnp.stack([finish(pair, *gates) for pair in pairs]))), 0)
+
+    g_up = jnp.concatenate([rows_by_expert((a1, a3), b1[0], b3[0]), rows_by_expert((b1, b3))], axis=-1)
     g2_mine, g2_other = core_halves(g2_keep + hop(g2_give, 'y'), 1)
     g_w2e = in_core_order(g2_mine.T[None], hop(g2_other, 'c').T[None], 0)
-    g_sh = jnp.concatenate([z_last(s1), z_sum(finish((s3,)).reshape(QUAD, ROWS, -1)), z_last(s2)], axis=1)
+    g_sh = jnp.concatenate([z_last(s1), z_sum(finish(s3).reshape(QUAD, ROWS, -1)), z_last(s2)], axis=1)
     g_sh_mine, g_sh_other = swap_rows(g_sh)
-    g_up = swap_experts(jnp.stack([g_w1, g_w3]))
     z_me = lax.axis_index('z')
     att_plane = att_rest()
     g_att_mine, g_att_other = swap_rows(z_sum([pick(att_plane, z_me ^ step, 0) for step in range(QUAD)]))

time: 1120 us -> 1150 us (1.027)
  waiting for transfers between devices: 525 us -> 580 us
  other arithmetic: 84 us -> 72.5 us
    ppermute x47 -> x55, waiting for transfers between devices: 295 us -> 369 us  [hop(): return lax.ppermute(block, axis, SWAP)]
    ppermute x15, waiting for transfers between devices: 230 us -> 167 us  [z_hop(): lax.ppermute(block, 'z', [(z_idx, z_idx ^ step) for z_idx in range(QUAD)])]
    all_to_all x4, waiting for transfers between devices: 0.01 us -> 43.5 us  [exchange(): lax.all_to_all(values.reshape(n_experts, capacity, model_dim), ('z', 'c')...]
    ppermute x47 -> x55, starting transfers between devices: 35.9 us -> 49.2 us  [hop(): return lax.ppermute(block, axis, SWAP)]
    unnamed x184 -> x222, local copies, waits for them, and re-layouts: 28.3 us -> 26.2 us
  transfers between devices with their start and end apart: 66 -> 74, of which waited for: 24 -> 24; matrix products, arithmetic and copies ran while one was open for 17% -> 16% of each run, Pallas kernels for 13% -> 19%
where the time goes in v2:
time: 1150 us; the launch traced here: 1140 us
  waiting for transfers between devices  580 us (50%)
  Pallas kernels  215 us (19%)
  starting transfers between devices  140 us (12%)
  local copies, waits for them, and re-layouts  91.5 us (8%)
  other arithmetic  72.5 us (6%)
  matrix products  38.9 us (3%)
    ppermute x55, waiting for transfers between devices, hop(): return lax.ppermute(block, axis, SWAP)  369 us
    ppermute x15, waiting for transfers between devices, z_hop(): lax.ppermute(block, 'z', [(z_idx, z_idx ^ step) for z_idx in range(QUAD)])  167 us
    pallas_call x2, Pallas kernels, expert_half(): pl.pallas_call(lambda *refs: expert_kernel(half, *refs), grid_spec=pltpu....  80.5 us
    ppermute x15, starting transfers between devices, z_hop(): lax.ppermute(block, 'z', [(z_idx, z_idx ^ step) for z_idx in range(QUAD)])  62.5 us
    pallas_call x2, Pallas kernels, attn_call(): pl.pallas_call(kernel, grid=(6,), in_specs=head_specs + extra + [table, t...  51.1 us
    ppermute x55, starting transfers between devices, hop(): return lax.ppermute(block, axis, SWAP)  49.2 us
    all_to_all x4, waiting for transfers between devices, exchange(): lax.all_to_all(values.reshape(n_experts, capacity, model_dim), ('z', 'c')...  43.5 us
    pallas_call x1, Pallas kernels, gather_weights(): pl.pallas_call(weight_kernel, in_specs=[any_spec] * 2, out_specs=[any_spe...  40.7 us
  transfers between devices with their start and end apart: 74, of which 24 were waited for; matrix products, arithmetic and copies ran while one was open for 16% of the time, Pallas kernels for 19%

profile of v2, /device:TPU:0, one launch (start us, length us, event | category | flops | bytes accessed | tf_op | source)
XLA Modules:
  0.0 1140.0 jit_solution(11557331256299668022)
XLA Ops:
  12.5 2.5 collective-permute-start.11
  16.4 40.7 %shard_map.289 = (bf16[32,24,3072]{2,1,0:T(8,128)(2,1)}, f32[32,24,128]{2,1,0:T(8,128)}) custom-call(bf16[24,3072]{1,0:T(8,128)(2,1)} %copy-done.80, f32[24,128]{1,0:T(8,128)} %select_maximum_fusion.small_ref), custom_call_target="tpu_custom_call" | custom-call | flops 7372800000 | bytes 73728 | tf_op jit(solution)/shard_map/pallas_call | solution.py:308
  59.9 7.2 shard_map.290
  67.2 19.4 %shard_map.291 = bf16[512,768]{1,0:T(8,128)(2,1)} custom-call(bf16[512,2304]{1,0:T(8,128)(2,1)} %get-tuple-element.96.q_ref.k_ref.v_ref, bf16[512,2304]{1,0:T(8,128)(2,1)} %get-tuple-element.96.q_ref.k_ref.v_ref, bf16[512,2304]{1,0:T(8,128)(2,1)} %get-tuple-element.96.q_ref.k_ref.v_ref, f32[512,128]{1,0:T(8,128)} %constant.226.clone.cos_ref, ...), custom_call_target="tpu_custom_call" | custom-call | flops 1073741824 | bytes 1179648 | tf_op jit(solution)/shard_map/pallas_call | solution.py:176
  94.8 2.6 copy.238
  97.4 5.1 all-to-all-start
  112.3 2.7 collective-permute-start.19
  116.5 43.5 %all-to-all-done = bf16[8,128,768]{1,2,0:T(8,128)(2,1)} async-done(((bf16[8,128,768]{1,2,0:T(8,128)(2,1)}), bf16[8,128,768]{1,2,0:T(8,128)(2,1)}, u32[]{:S(2)}, u32[]{:S(2)}) %all-to-all-start) | async-done | bytes 1572896 | tf_op jit(solution)/shard_map/all_to_all | solution.py:561
  159.9 3.5 copy_bitcast_fusion.1
  163.4 2.6 copy.241
  166.0 13.6 %all-to-all-start.1 = ((bf16[8,128,768]{1,2,0:T(8,128)(2,1)}), bf16[8,128,768]{1,2,0:T(8,128)(2,1)}, u32[]{:S(2)}, u32[]{:S(2)}) async-start(bf16[8,128,768]{1,2,0:T(8,128)(2,1)} %copy.241), calls=%async_computation.1 | async-start | bytes 3145728 | tf_op jit(solution)/shard_map/all_to_all | solution.py:561
  188.6 35.4 %collective-permute-done.10.refs_16_ = bf16[384,768]{1,0:T(8,128)(2,1)} collective-permute-done((bf16[384,768]{1,0:T(8,128)(2,1)S(1)}, bf16[384,768]{1,0:T(8,128)(2,1)}, u32[]{:S(2)}, u32[]{:S(2)}) %collective-permute-start.10) | collective-permute-done | bytes 589856 | tf_op jit(solution)/shard_map/ppermute | solution.py:196
  230.0 6.5 collective-permute-done.9.refs_15_
  239.6 9.6 collective-permute-done.13.refs_19_
  250.7 17.5 %collective-permute-done.22.refs_3_.refs_11_.refs_19_ = bf16[2,48,4608]{2,1,0:T(8,128)(2,1)S(1)} collective-permute-done((bf16[2,48,4608]{2,1,0:T(8,128)(2,1)S(1)}, bf16[2,48,4608]{2,1,0:T(8,128)(2,1)S(1)}, u32[]{:S(2)}, u32[]{:S(2)}) %collective-permute-start.22) | collective-permute-done | bytes 884768 | tf_op jit(solution)/shard_map/ppermute | solution.py:196
  272.4 3.2 fusion.116
  275.6 2.7 copy.248.dd_ref
  280.4 2.6 copy.247.rows_ref
  283.0 2.6 copy.245.refs_1_
  285.5 3.5 fusion.115
  289.0 2.6 copy.246.refs_2_
  291.6 22.2 %collective-permute-done.14.refs_20_ = bf16[384,768]{1,0:T(8,128)(2,1)} collective-permute-done((bf16[384,768]{1,0:T(8,128)(2,1)}, bf16[384,768]{1,0:T(8,128)(2,1)}, u32[]{:S(2)}, u32[]{:S(2)}) %collective-permute-start.14) | collective-permute-done | bytes 589856 | tf_op jit(solution)/shard_map/ppermute | solution.py:196
  320.3 39.6 %shard_map.292 = (f32[1024,768]{1,0:T(8,128)}, f32[1024,768]{1,0:T(8,128)}, f32[2,192,1536]{2,1,0:T(8,128)}, f32[2,192,1536]{2,1,0:T(8,128)}, f32[2,192,1536]{2,...) custom-call(s32[3]{0:T(128)} %get-tuple-element.313.refs_0_, ...), custom_call_target="tpu_custom_call" | custom-call | flops 21743271936 | bytes 589824 | tf_op jit(solution)/shard_map/pallas_call | solution.py:424
  360.0 40.9 %shard_map.293 = (bf16[1024,768]{1,0:T(8,128)(2,1)}, bf16[1024,768]{1,0:T(8,128)(2,1)}, f32[2,192,1536]{2,1,0:T(8,128)}, f32[2,192,1536]{2,1,0:T(8,128)}, f32[2,...) custom-call(s32[3]{0:T(128)} %get-tuple-element.312.refs_0_, ...), custom_call_target="tpu_custom_call" | custom-call | flops 21743271936 | bytes 589824 | tf_op jit(solution)/shard_map/pallas_call | solution.py:424
  400.8 5.2 all-to-all-start.2
  406.1 35.3 %shard_map.294 = (f32[512,768]{1,0:T(8,128)}, f32[512,768]{1,0:T(8,128)}, f32[512,768]{1,0:T(8,128)}, f32[512,768]{1,0:T(8,128)}, f32[2,192,1536]{2,1,0:T(8,128)...) custom-call(s32[2]{0:T(128)} %pad_add_fusion.3.info, ...), custom_call_target="tpu_custom_call" | custom-call | flops 21743271936 | bytes 1179648 | tf_op jit(solution)/shard_map/pallas_call | solution.py:485
  442.1 3.0 copy.249
  446.2 3.0 copy.250
  449.2 3.1 copy.262
  452.3 3.0 copy.263
  458.7 37.2 %collective-permute-done.47 = f32[2,192,1536]{2,1,0:T(8,128)} collective-permute-done((f32[2,192,1536]{2,1,0:T(8,128)}, f32[2,192,1536]{2,1,0:T(8,128)}, u32[]{:S(2)}, u32[]{:S(2)}) %collective-permute-start.47) | collective-permute-done | bytes 2359328 | tf_op jit(solution)/shard_map/ppermute | solution.py:196
  495.9 4.2 add.334
  500.1 2.6 fusion.12
  511.4 31.7 %shard_map.295 = bf16[512,2304]{1,0:T(8,128)(2,1)} custom-call(bf16[512,2304]{1,0:T(8,128)(2,1)} %get-tuple-element.96.q_ref.k_ref.v_ref, bf16[512,2304]{1,0:T(8,128)(2,1)} %get-tuple-element.96.q_ref.k_ref.v_ref, bf16[512,2304]{1,0:T(8,128)(2,1)} %get-tuple-element.96.q_ref.k_ref.v_ref, bf16[512,768]{1,0:T(8,128)(2,1)} %pad_maximum_fusion.10.do_ref, ...), custom_call_target="tpu_custom_call" | custom-call | flops 2147483648 | bytes 1179648 | tf_op jit(solution)/shard_map/pallas_call | solution.py:176
  543.0 5.1 fusion.39
  549.3 97.8 %collective-permute-done.58 = f32[2,192,1536]{2,1,0:T(8,128)} collective-permute-done((f32[2,192,1536]{2,1,0:T(8,128)}, f32[2,192,1536]{2,1,0:T(8,128)}, u32[]{:S(2)}, u32[]{:S(2)}) %collective-permute-start.58) | collective-permute-done | bytes 2359328 | tf_op jit(solution)/shard_map/ppermute | solution.py:196
  652.8 2.7 fusion.6
  655.5 4.4 fusion.19
  671.8 3.3 convolution_add_fusion
  675.5 41.6 %collective-permute-done.40 = f32[192,1536]{1,0:T(8,128)S(1)} collective-permute-done((f32[192,1536]{1,0:T(8,128)}, f32[192,1536]{1,0:T(8,128)S(1)}, u32[]{:S(2)}, u32[]{:S(2)}) %collective-permute-start.40) | collective-permute-done | bytes 1179680 | tf_op jit(solution)/shard_map/ppermute | solution.py:200
  717.1 29.2 %collective-permute-done.43 = f32[192,1536]{1,0:T(8,128)S(1)} collective-permute-done((f32[192,1536]{1,0:T(8,128)}, f32[192,1536]{1,0:T(8,128)S(1)}, u32[]{:S(2)}, u32[]{:S(2)}) %collective-permute-start.43) | collective-permute-done | bytes 1179680 | tf_op jit(solution)/shard_map/ppermute | solution.py:200
  749.4 22.7 %collective-permute-start.53 = (f32[192,1536]{1,0:T(8,128)S(1)}, f32[192,1536]{1,0:T(8,128)S(1)}, u32[]{:S(2)}, u32[]{:S(2)}) collective-permute-start(f32[192,1536]{1,0:T(8,128)S(1)} %copy-done.90), channel_id=1, source_target_pairs={{0,16},{8,24},{16,0},{24,8},{1,17},{9,25},{17,1},{25,9},{2,18},{10... | collective-permute-start | bytes 3538952 | tf_op jit(solution)/shard_map/ppermute | solution.py:200
  775.4 4.6 broadcast_select_fusion
  782.9 66.3 %collective-permute-done.53 = f32[192,1536]{1,0:T(8,128)S(1)} collective-permute-done((f32[192,1536]{1,0:T(8,128)S(1)}, f32[192,1536]{1,0:T(8,128)S(1)}, u32[]{:S(2)}, u32[]{:S(2)}) %collective-permute-start.53) | collective-permute-done | bytes 1179680 | tf_op jit(solution)/shard_map/ppermute | solution.py:200
  857.8 45.0 %collective-permute-done.59 = f32[192,1536]{1,0:T(8,128)S(1)} collective-permute-done((f32[192,1536]{1,0:T(8,128)S(1)}, f32[192,1536]{1,0:T(8,128)S(1)}, u32[]{:S(2)}, u32[]{:S(2)}) %collective-permute-start.59) | collective-permute-done | bytes 1179680 | tf_op jit(solution)/shard_map/ppermute | solution.py:196
  907.0 22.9 %collective-permute-start.49 = (f32[48,1536]{1,0:T(8,128)}, f32[48,1536]{1,0:T(8,128)}, u32[]{:S(2)}, u32[]{:S(2)}) collective-permute-start(f32[48,1536]{1,0:T(8,128)} %get-tuple-element.281), channel_id=1, source_target_pairs={{0,8},{8,0},{16,24},{24,16},{1,9},{9,1},{17,25},{25,17},{2,10},{10... | collective-permute-start | bytes 884744 | tf_op jit(solution)/shard_map/ppermute | solution.py:200
  934.1 2.4 slice_bitcast_fusion.4
  936.5 4.3 all-to-all-start.3
  942.4 12.9 %collective-permute-done.50 = f32[48,1536]{1,0:T(8,128)} collective-permute-done((f32[48,1536]{1,0:T(8,128)}, f32[48,1536]{1,0:T(8,128)}, u32[]{:S(2)}, u32[]{:S(2)}) %collective-permute-start.50) | collective-permute-done | bytes 294944 | tf_op jit(solution)/shard_map/ppermute | solution.py:200
  960.4 11.3 collective-permute-done.55
  973.3 27.6 %collective-permute-done.46 = f32[1,48,1536]{2,1,0:T(8,128)S(1)} collective-permute-done((f32[1,48,1536]{2,1,0:T(8,128)S(1)}, f32[1,48,1536]{2,1,0:T(8,128)S(1)}, u32[]{:S(2)}, u32[]{:S(2)}) %collective-permute-start.46) | collective-permute-done | bytes 294944 | tf_op jit(solution)/shard_map/ppermute | solution.py:196
  1002.5 7.0 collective-permute-done.56
  1019.0 19.5 %collective-permute-done.65 = f32[192,1536]{1,0:T(8,128)} collective-permute-done((f32[192,1536]{1,0:T(8,128)}, f32[192,1536]{1,0:T(8,128)}, u32[]{:S(2)}, u32[]{:S(2)}) %collective-permute-start.65) | collective-permute-done | bytes 1179680 | tf_op jit(solution)/shard_map/ppermute | solution.py:196
  1043.6 20.2 %collective-permute-done.34 = f32[2,2,48,1664]{3,2,1,0:T(8,128)S(1)} collective-permute-done((f32[2,2,48,1664]{3,2,1,0:T(8,128)}, f32[2,2,48,1664]{3,2,1,0:T(8,128)S(1)}, u32[]{:S(2)}, u32[]{:S(2)}) %collective-permute-start.34) | collective-permute-done | bytes 1277984 | tf_op jit(solution)/shard_map/ppermute | solution.py:196
  1063.7 2.5 bitcast_add_fusion
  1066.9 2.5 bitcast_add_fusion.2
  1072.3 8.5 collective-permute-done.35
  1086.2 2.4 collective-permute-start.37
  1092.7 5.4 collective-permute-done.36
  1098.0 12.0 %collective-permute-done.37 = f32[48,1664]{1,0:T(8,128)S(1)} collective-permute-done((f32[48,1664]{1,0:T(8,128)S(1)}, f32[48,1664]{1,0:T(8,128)S(1)}, u32[]{:S(2)}, u32[]{:S(2)}) %collective-permute-start.37) | collective-permute-done | bytes 319520 | tf_op jit(solution)/shard_map/ppermute | solution.py:200
  1110.8 3.9 select_add_fusion
  1118.3 2.5 slice_bitcast_fusion
  1128.0 2.7 fusion.1
  1130.7 3.0 fusion.57
  (463 shorter events, 181.1 us)
Async XLA Ops:
  4.1 98.4 %collective-permute-start.1 = (bf16[96,3072]{1,0:T(8,128)(2,1)}, bf16[96,3072]{1,0:T(8,128)(2,1)}, u32[]{:S(2)}, u32[]{:S(2)}) collective-permute-start(bf16[96,3072]{1,0:T(8,128)(2,1)} %dynamic-slice_bitcast_fusion.3), channel_id=1, source_target_pairs={{0,1},{1,0},{2,3},{3,2},{4,5},{5,4},{6,7},{7,6},{8,9},{9,8},{10,11... | collective-permute-start | bytes 1769480 | tf_op jit(solution)/shard_map/ppermute | solution.py:196
  5.0 101.9 %collective-permute-start.2 = (bf16[96,3072]{1,0:T(8,128)(2,1)}, bf16[96,3072]{1,0:T(8,128)(2,1)}, u32[]{:S(2)}, u32[]{:S(2)}) collective-permute-start(bf16[96,3072]{1,0:T(8,128)(2,1)} %dynamic-slice_bitcast_fusion.2), channel_id=1, source_target_pairs={{0,1},{1,0},{2,3},{3,2},{4,5},{5,4},{6,7},{7,6},{8,9},{9,8},{10,11... | collective-permute-start | bytes 1769480 | tf_op jit(solution)/shard_map/ppermute | solution.py:196
  12.5 167.2 %collective-permute-start.11 = (bf16[384,768]{1,0:T(8,128)(2,1)}, bf16[384,768]{1,0:T(8,128)(2,1)}, u32[]{:S(2)}, u32[]{:S(2)}) collective-permute-start(bf16[384,768]{1,0:T(8,128)(2,1)} %get-tuple-element.264.refs_13_), channel_id=1, source_target_pairs={{0,4},{4,0},{1,5},{5,1},{2,6},{6,2},{3,7},{7,3},{8,12},{12,8},{9,1... | collective-permute-start | bytes 1769480 | tf_op jit(solution)/shard_map/ppermute | solution.py:196
  97.4 62.5 %all-to-all-start = ((bf16[8,128,768]{1,2,0:T(8,128)(2,1)}), bf16[8,128,768]{1,2,0:T(8,128)(2,1)}, u32[]{:S(2)}, u32[]{:S(2)}) async-start(bf16[8,128,768]{1,2,0:T(8,128)(2,1)} %copy.238), calls=%async_computation | async-start | bytes 3145728 | tf_op jit(solution)/shard_map/all_to_all | solution.py:561
  105.0 120.6 %collective-permute-start.5 = (bf16[192,3072]{1,0:T(8,128)(2,1)}, bf16[192,3072]{1,0:T(8,128)(2,1)}, u32[]{:S(2)}, u32[]{:S(2)}) collective-permute-start(bf16[192,3072]{1,0:T(8,128)(2,1)} %pad_maximum_fusion.5.refs_5_), channel_id=1, source_target_pairs={{0,4},{4,0},{1,5},{5,1},{2,6},{6,2},{3,7},{7,3},{8,12},{12,8},{9,1... | collective-permute-start | bytes 3538952 | tf_op jit(solution)/shard_map/ppermute | solution.py:196
  112.3 70.0 %collective-permute-start.19 = (bf16[48,4608]{1,0:T(8,128)(2,1)}, bf16[48,4608]{1,0:T(8,128)(2,1)}, u32[]{:S(2)}, u32[]{:S(2)}) collective-permute-start(bf16[48,4608]{1,0:T(8,128)(2,1)} %pad_maximum_fusion.11), channel_id=1, source_target_pairs={{0,16},{8,24},{16,0},{24,8},{1,17},{9,25},{17,1},{25,9},{2,18},{10... | collective-permute-start | bytes 1327112 | tf_op jit(solution)/shard_map/ppermute | solution.py:200
  115.0 68.7 %collective-permute-start.20 = (bf16[48,4608]{1,0:T(8,128)(2,1)}, bf16[48,4608]{1,0:T(8,128)(2,1)}, u32[]{:S(2)}, u32[]{:S(2)}) collective-permute-start(bf16[48,4608]{1,0:T(8,128)(2,1)} %pad_maximum_fusion.11), channel_id=1, source_target_pairs={{0,24},{8,16},{16,8},{24,0},{1,25},{9,17},{17,9},{25,1},{2,26},{10... | collective-permute-start | bytes 1327112 | tf_op jit(solution)/shard_map/ppermute | solution.py:200
  116.5 67.8 %collective-permute-start.18 = (bf16[48,4608]{1,0:T(8,128)(2,1)}, bf16[48,4608]{1,0:T(8,128)(2,1)}, u32[]{:S(2)}, u32[]{:S(2)}) collective-permute-start(bf16[48,4608]{1,0:T(8,128)(2,1)} %pad_maximum_fusion.11), channel_id=1, source_target_pairs={{0,8},{8,0},{16,24},{24,16},{1,9},{9,1},{17,25},{25,17},{2,10},{10... | collective-permute-start | bytes 1327112 | tf_op jit(solution)/shard_map/ppermute | solution.py:200
  166.0 119.5 %all-to-all-start.1 = ((bf16[8,128,768]{1,2,0:T(8,128)(2,1)}), bf16[8,128,768]{1,2,0:T(8,128)(2,1)}, u32[]{:S(2)}, u32[]{:S(2)}) async-start(bf16[8,128,768]{1,2,0:T(8,128)(2,1)} %copy.241), calls=%async_computation.1 | async-start | bytes 3145728 | tf_op jit(solution)/shard_map/all_to_all | solution.py:561
  182.2 46.3 %collective-permute-start.4 = (bf16[192,3072]{1,0:T(8,128)(2,1)}, bf16[192,3072]{1,0:T(8,128)(2,1)}, u32[]{:S(2)}, u32[]{:S(2)}) collective-permute-start(bf16[192,3072]{1,0:T(8,128)(2,1)} %pad_maximum_fusion.6.refs_6_), channel_id=1, source_target_pairs={{0,2},{2,0},{1,3},{3,1},{4,6},{6,4},{5,7},{7,5},{8,10},{10,8},{9,1... | collective-permute-start | bytes 3538952 | tf_op jit(solution)/shard_map/ppermute | solution.py:196
  183.7 40.3 %collective-permute-start.10 = (bf16[384,768]{1,0:T(8,128)(2,1)S(1)}, bf16[384,768]{1,0:T(8,128)(2,1)}, u32[]{:S(2)}, u32[]{:S(2)}) collective-permute-start(bf16[384,768]{1,0:T(8,128)(2,1)S(1)} %copy-done.61), channel_id=1, source_target_pairs={{0,2},{2,0},{1,3},{3,1},{4,6},{6,4},{5,7},{7,5},{8,10},{10,8},{9,1... | collective-permute-start | bytes 1769480 | tf_op jit(solution)/shard_map/ppermute | solution.py:196
  184.3 39.8 %collective-permute-start.12 = (bf16[384,768]{1,0:T(8,128)(2,1)S(1)}, bf16[384,768]{1,0:T(8,128)(2,1)S(1)}, u32[]{:S(2)}, u32[]{:S(2)}) collective-permute-start(bf16[384,768]{1,0:T(8,128)(2,1)S(1)} %copy-done.61), channel_id=1, source_target_pairs={{0,4},{4,0},{1,5},{5,1},{2,6},{6,2},{3,7},{7,3},{8,12},{12,8},{9,1... | collective-permute-start | bytes 1769480 | tf_op jit(solution)/shard_map/ppermute | solution.py:196
  187.1 49.5 %collective-permute-start.9 = (bf16[384,768]{1,0:T(8,128)(2,1)}, bf16[384,768]{1,0:T(8,128)(2,1)S(1)}, u32[]{:S(2)}, u32[]{:S(2)}) collective-permute-start(bf16[384,768]{1,0:T(8,128)(2,1)} %get-tuple-element.264.refs_13_), channel_id=1, source_target_pairs={{0,2},{2,0},{1,3},{3,1},{4,6},{6,4},{5,7},{7,5},{8,10},{10,8},{9,1... | collective-permute-start | bytes 1769480 | tf_op jit(solution)/shard_map/ppermute | solution.py:196
  224.0 25.2 %collective-permute-start.13 = (bf16[384,768]{1,0:T(8,128)(2,1)}, bf16[384,768]{1,0:T(8,128)(2,1)S(1)}, u32[]{:S(2)}, u32[]{:S(2)}) collective-permute-start(bf16[384,768]{1,0:T(8,128)(2,1)} %collective-permute-done.11.refs_17_), channel_id=1, source_target_pairs={{0,2},{2,0},{1,3},{3,1},{4,6},{6,4},{5,7},{7,5},{8,10},{10,8},{9,1... | collective-permute-start | bytes 1769480 | tf_op jit(solution)/shard_map/ppermute | solution.py:196
  225.6 42.6 %collective-permute-start.22 = (bf16[2,48,4608]{2,1,0:T(8,128)(2,1)S(1)}, bf16[2,48,4608]{2,1,0:T(8,128)(2,1)S(1)}, u32[]{:S(2)}, u32[]{:S(2)}) collective-permute-start(bf16[2,48,4608]{2,1,0:T(8,128)(2,1)S(1)} %pad_maximum_fusion.8.refs_1_.refs_9_.refs_17_), channel_id=1, source_target_pairs={{0,2},{2,0},{1,3},{3,1},{4,6},{6,4},{5,7},{7,5},{8,10},{10,8},{9,1... | collective-permute-start | bytes 2654216 | tf_op jit(solution)/shard_map/ppermute | solution.py:196
  228.5 43.4 %collective-permute-start.23 = (bf16[2,48,4608]{2,1,0:T(8,128)(2,1)}, bf16[2,48,4608]{2,1,0:T(8,128)(2,1)}, u32[]{:S(2)}, u32[]{:S(2)}) collective-permute-start(bf16[2,48,4608]{2,1,0:T(8,128)(2,1)} %pad_maximum_fusion.7.refs_0_.refs_8_.refs_16_), channel_id=1, source_target_pairs={{0,4},{4,0},{1,5},{5,1},{2,6},{6,2},{3,7},{7,3},{8,12},{12,8},{9,1... | collective-permute-start | bytes 2654216 | tf_op jit(solution)/shard_map/ppermute | solution.py:196
  236.6 78.8 %collective-permute-start.3 = (bf16[192,3072]{1,0:T(8,128)(2,1)}, bf16[192,3072]{1,0:T(8,128)(2,1)}, u32[]{:S(2)}, u32[]{:S(2)}) collective-permute-start(bf16[192,3072]{1,0:T(8,128)(2,1)} %pad_maximum_fusion.5.refs_5_), channel_id=1, source_target_pairs={{0,2},{2,0},{1,3},{3,1},{4,6},{6,4},{5,7},{7,5},{8,10},{10,8},{9,1... | collective-permute-start | bytes 3538952 | tf_op jit(solution)/shard_map/ppermute | solution.py:196
  238.1 78.2 %collective-permute-start.6 = (bf16[192,3072]{1,0:T(8,128)(2,1)}, bf16[192,3072]{1,0:T(8,128)(2,1)}, u32[]{:S(2)}, u32[]{:S(2)}) collective-permute-start(bf16[192,3072]{1,0:T(8,128)(2,1)} %pad_maximum_fusion.6.refs_6_), channel_id=1, source_target_pairs={{0,4},{4,0},{1,5},{5,1},{2,6},{6,2},{3,7},{7,3},{8,12},{12,8},{9,1... | collective-permute-start | bytes 3538952 | tf_op jit(solution)/shard_map/ppermute | solution.py:196
  249.2 69.6 %collective-permute-start.7 = (bf16[192,3072]{1,0:T(8,128)(2,1)}, bf16[192,3072]{1,0:T(8,128)(2,1)}, u32[]{:S(2)}, u32[]{:S(2)}) collective-permute-start(bf16[192,3072]{1,0:T(8,128)(2,1)} %collective-permute-done.5.refs_9_), channel_id=1, source_target_pairs={{0,2},{2,0},{1,3},{3,1},{4,6},{6,4},{5,7},{7,5},{8,10},{10,8},{9,1... | collective-permute-start | bytes 3538952 | tf_op jit(solution)/shard_map/ppermute | solution.py:196
  269.1 51.2 %collective-permute-start.8 = (bf16[192,3072]{1,0:T(8,128)(2,1)}, bf16[192,3072]{1,0:T(8,128)(2,1)}, u32[]{:S(2)}, u32[]{:S(2)}) collective-permute-start(bf16[192,3072]{1,0:T(8,128)(2,1)} %collective-permute-done.4.refs_8_), channel_id=1, source_target_pairs={{0,4},{4,0},{1,5},{5,1},{2,6},{6,2},{3,7},{7,3},{8,12},{12,8},{9,1... | collective-permute-start | bytes 3538952 | tf_op jit(solution)/shard_map/ppermute | solution.py:196
  271.9 41.9 %collective-permute-start.14 = (bf16[384,768]{1,0:T(8,128)(2,1)}, bf16[384,768]{1,0:T(8,128)(2,1)}, u32[]{:S(2)}, u32[]{:S(2)}) collective-permute-start(bf16[384,768]{1,0:T(8,128)(2,1)} %collective-permute-done.10.refs_16_), channel_id=1, source_target_pairs={{0,4},{4,0},{1,5},{5,1},{2,6},{6,2},{3,7},{7,3},{8,12},{12,8},{9,1... | collective-permute-start | bytes 1769480 | tf_op jit(solution)/shard_map/ppermute | solution.py:196
  313.8 92.2 %collective-permute-start.24 = (bf16[2,48,4608]{2,1,0:T(8,128)(2,1)}, bf16[2,48,4608]{2,1,0:T(8,128)(2,1)}, u32[]{:S(2)}, u32[]{:S(2)}) collective-permute-start(bf16[2,48,4608]{2,1,0:T(8,128)(2,1)} %copy-done.56), channel_id=1, source_target_pairs={{0,4},{4,0},{1,5},{5,1},{2,6},{6,2},{3,7},{7,3},{8,12},{12,8},{9,1... | collective-permute-start | bytes 2654216 | tf_op jit(solution)/shard_map/ppermute | solution.py:196
  315.3 90.7 %collective-permute-start.21 = (bf16[2,48,4608]{2,1,0:T(8,128)(2,1)}, bf16[2,48,4608]{2,1,0:T(8,128)(2,1)}, u32[]{:S(2)}, u32[]{:S(2)}) collective-permute-start(bf16[2,48,4608]{2,1,0:T(8,128)(2,1)} %pad_maximum_fusion.7.refs_0_.refs_8_.refs_16_), channel_id=1, source_target_pairs={{0,2},{2,0},{1,3},{3,1},{4,6},{6,4},{5,7},{7,5},{8,10},{10,8},{9,1... | collective-permute-start | bytes 2654216 | tf_op jit(solution)/shard_map/ppermute | solution.py:196
  316.3 89.8 %collective-permute-start.26 = (bf16[2,48,4608]{2,1,0:T(8,128)(2,1)}, bf16[2,48,4608]{2,1,0:T(8,128)(2,1)}, u32[]{:S(2)}, u32[]{:S(2)}) collective-permute-start(bf16[2,48,4608]{2,1,0:T(8,128)(2,1)} %copy-done.93), channel_id=1, source_target_pairs={{0,4},{4,0},{1,5},{5,1},{2,6},{6,2},{3,7},{7,3},{8,12},{12,8},{9,1... | collective-permute-start | bytes 2654216 | tf_op jit(solution)/shard_map/ppermute | solution.py:196
  318.8 87.2 %collective-permute-start.25 = (bf16[2,48,4608]{2,1,0:T(8,128)(2,1)}, bf16[2,48,4608]{2,1,0:T(8,128)(2,1)}, u32[]{:S(2)}, u32[]{:S(2)}) collective-permute-start(bf16[2,48,4608]{2,1,0:T(8,128)(2,1)} %collective-permute-done.23.refs_4_.refs_12_.refs_20_), channel_id=1, source_target_pairs={{0,2},{2,0},{1,3},{3,1},{4,6},{6,4},{5,7},{7,5},{8,10},{10,8},{9,1... | collective-permute-start | bytes 2654216 | tf_op jit(solution)/shard_map/ppermute | solution.py:196
  400.8 99.2 %all-to-all-start.2 = ((bf16[8,128,768]{2,1,0:T(8,128)(2,1)}), bf16[8,128,768]{2,1,0:T(8,128)(2,1)}, u32[]{:S(2)}, u32[]{:S(2)}) async-start(bf16[8,128,768]{2,1,0:T(8,128)(2,1)} %bitcast.281), calls=%async_computation.2 | async-start | bytes 3145728 | tf_op jit(solution)/shard_map/all_to_all | solution.py:561
  441.4 54.5 %collective-permute-start.47 = (f32[2,192,1536]{2,1,0:T(8,128)}, f32[2,192,1536]{2,1,0:T(8,128)}, u32[]{:S(2)}, u32[]{:S(2)}) collective-permute-start(f32[2,192,1536]{2,1,0:T(8,128)} %get-tuple-element.137), channel_id=1, source_target_pairs={{0,2},{2,0},{1,3},{3,1},{4,6},{6,4},{5,7},{7,5},{8,10},{10,8},{9,1... | collective-permute-start | bytes 7077896 | tf_op jit(solution)/shard_map/ppermute | solution.py:196
  445.1 59.0 %collective-permute-start.27 = (f32[512,768]{0,1:T(8,128)}, f32[512,768]{0,1:T(8,128)}, u32[]{:S(2)}, u32[]{:S(2)}) collective-permute-start(f32[512,768]{0,1:T(8,128)} %copy.249), channel_id=1, source_target_pairs={{0,1},{1,0},{2,3},{3,2},{4,5},{5,4},{6,7},{7,6},{8,9},{9,8},{10,11... | collective-permute-start | bytes 4718600 | tf_op jit(solution)/shard_map/ppermute | solution.py:196
  455.3 316.8 %collective-permute-start.41 = (f32[768,768]{1,0:T(8,128)}, f32[768,768]{1,0:T(8,128)}, u32[]{:S(2)}, u32[]{:S(2)}) collective-permute-start(f32[768,768]{1,0:T(8,128)} %get-tuple-element.126), channel_id=1, source_target_pairs={{0,2},{2,0},{1,3},{3,1},{4,6},{6,4},{5,7},{7,5},{8,10},{10,8},{9,1... | collective-permute-start | bytes 7077896 | tf_op jit(solution)/shard_map/ppermute | solution.py:196
  456.7 316.9 %collective-permute-start.42 = (f32[768,768]{1,0:T(8,128)}, f32[768,768]{1,0:T(8,128)}, u32[]{:S(2)}, u32[]{:S(2)}) collective-permute-start(f32[768,768]{1,0:T(8,128)} %get-tuple-element.129), channel_id=1, source_target_pairs={{0,2},{2,0},{1,3},{3,1},{4,6},{6,4},{5,7},{7,5},{8,10},{10,8},{9,1... | collective-permute-start | bytes 7077896 | tf_op jit(solution)/shard_map/ppermute | solution.py:196
  457.3 189.8 %collective-permute-start.58 = (f32[2,192,1536]{2,1,0:T(8,128)}, f32[2,192,1536]{2,1,0:T(8,128)}, u32[]{:S(2)}, u32[]{:S(2)}) collective-permute-start(f32[2,192,1536]{2,1,0:T(8,128)} %get-tuple-element.148), channel_id=1, source_target_pairs={{0,2},{2,0},{1,3},{3,1},{4,6},{6,4},{5,7},{7,5},{8,10},{10,8},{9,1... | collective-permute-start | bytes 7077896 | tf_op jit(solution)/shard_map/ppermute | solution.py:196
  548.1 123.2 %collective-permute-start.28 = (f32[768,1152]{1,0:T(8,128)}, f32[768,1152]{1,0:T(8,128)}, u32[]{:S(2)}, u32[]{:S(2)}) collective-permute-start(f32[768,1152]{1,0:T(8,128)} %fusion.39), channel_id=1, source_target_pairs={{0,1},{1,0},{2,3},{3,2},{4,5},{5,4},{6,7},{7,6},{8,9},{9,8},{10,11... | collective-permute-start | bytes 10616840 | tf_op jit(solution)/shard_map/ppermute | solution.py:196
  664.2 52.9 %collective-permute-start.40 = (f32[192,1536]{1,0:T(8,128)}, f32[192,1536]{1,0:T(8,128)S(1)}, u32[]{:S(2)}, u32[]{:S(2)}) collective-permute-start(f32[192,1536]{1,0:T(8,128)} %get-tuple-element.124), channel_id=1, source_target_pairs={{0,8},{8,0},{16,24},{24,16},{1,9},{9,1},{17,25},{25,17},{2,10},{10... | collective-permute-start | bytes 3538952 | tf_op jit(solution)/shard_map/ppermute | solution.py:200
  665.8 80.5 %collective-permute-start.43 = (f32[192,1536]{1,0:T(8,128)}, f32[192,1536]{1,0:T(8,128)S(1)}, u32[]{:S(2)}, u32[]{:S(2)}) collective-permute-start(f32[192,1536]{1,0:T(8,128)} %get-tuple-element.132), channel_id=1, source_target_pairs={{0,16},{8,24},{16,0},{24,8},{1,17},{9,25},{17,1},{25,9},{2,18},{10... | collective-permute-start | bytes 3538952 | tf_op jit(solution)/shard_map/ppermute | solution.py:200
  671.3 78.1 %collective-permute-start.44 = (f32[192,1536]{1,0:T(8,128)S(1)}, f32[192,1536]{1,0:T(8,128)S(1)}, u32[]{:S(2)}, u32[]{:S(2)}) collective-permute-start(f32[192,1536]{1,0:T(8,128)S(1)} %copy-done.92), channel_id=1, source_target_pairs={{0,24},{8,16},{16,8},{24,0},{1,25},{9,17},{17,9},{25,1},{2,26},{10... | collective-permute-start | bytes 3538952 | tf_op jit(solution)/shard_map/ppermute | solution.py:200
  717.1 62.9 %collective-permute-start.52 = (f32[192,1536]{1,0:T(8,128)S(1)}, f32[192,1536]{1,0:T(8,128)S(1)}, u32[]{:S(2)}, u32[]{:S(2)}) collective-permute-start(f32[192,1536]{1,0:T(8,128)S(1)} %copy-done.91), channel_id=1, source_target_pairs={{0,8},{8,0},{16,24},{24,16},{1,9},{9,1},{17,25},{25,17},{2,10},{10... | collective-permute-start | bytes 3538952 | tf_op jit(solution)/shard_map/ppermute | solution.py:200
  746.3 105.7 %collective-permute-start.61 = (f32[2,192,1536]{2,1,0:T(8,128)S(1)}, f32[2,192,1536]{2,1,0:T(8,128)S(1)}, u32[]{:S(2)}, u32[]{:S(2)}) collective-permute-start(f32[2,192,1536]{2,1,0:T(8,128)S(1)} %copy-done.88), channel_id=1, source_target_pairs={{0,4},{4,0},{1,5},{5,1},{2,6},{6,2},{3,7},{7,3},{8,12},{12,8},{9,1... | collective-permute-start | bytes 7077896 | tf_op jit(solution)/shard_map/ppermute | solution.py:196
  749.4 99.7 %collective-permute-start.53 = (f32[192,1536]{1,0:T(8,128)S(1)}, f32[192,1536]{1,0:T(8,128)S(1)}, u32[]{:S(2)}, u32[]{:S(2)}) collective-permute-start(f32[192,1536]{1,0:T(8,128)S(1)} %copy-done.90), channel_id=1, source_target_pairs={{0,16},{8,24},{16,0},{24,8},{1,17},{9,25},{17,1},{25,9},{2,18},{10... | collective-permute-start | bytes 3538952 | tf_op jit(solution)/shard_map/ppermute | solution.py:200
  772.1 77.0 %collective-permute-start.54 = (f32[192,1536]{1,0:T(8,128)S(1)}, f32[192,1536]{1,0:T(8,128)S(1)}, u32[]{:S(2)}, u32[]{:S(2)}) collective-permute-start(f32[192,1536]{1,0:T(8,128)S(1)} %copy-done.89), channel_id=1, source_target_pairs={{0,24},{8,16},{16,8},{24,0},{1,25},{9,17},{17,9},{25,1},{2,26},{10... | collective-permute-start | bytes 3538952 | tf_op jit(solution)/shard_map/ppermute | solution.py:200
  773.5 80.3 %collective-permute-start.60 = (f32[2,192,1536]{2,1,0:T(8,128)S(1)}, f32[2,192,1536]{2,1,0:T(8,128)S(1)}, u32[]{:S(2)}, u32[]{:S(2)}) collective-permute-start(f32[2,192,1536]{2,1,0:T(8,128)S(1)} %copy-done.87), channel_id=1, source_target_pairs={{0,2},{2,0},{1,3},{3,1},{4,6},{6,4},{5,7},{7,5},{8,10},{10,8},{9,1... | collective-permute-start | bytes 7077896 | tf_op jit(solution)/shard_map/ppermute | solution.py:196
  780.0 77.7 %collective-permute-start.62 = (f32[2,192,1536]{2,1,0:T(8,128)S(1)}, f32[2,192,1536]{2,1,0:T(8,128)S(1)}, u32[]{:S(2)}, u32[]{:S(2)}) collective-permute-start(f32[2,192,1536]{2,1,0:T(8,128)S(1)} %copy-done.86), channel_id=1, source_target_pairs={{0,4},{4,0},{1,5},{5,1},{2,6},{6,2},{3,7},{7,3},{8,12},{12,8},{9,1... | collective-permute-start | bytes 7077896 | tf_op jit(solution)/shard_map/ppermute | solution.py:196
  849.1 281.5 %collective-permute-start.31 = (f32[512,768]{0,1:T(8,128)}, f32[512,768]{0,1:T(8,128)}, u32[]{:S(2)}, u32[]{:S(2)}) collective-permute-start(f32[512,768]{0,1:T(8,128)} %copy.262), channel_id=1, source_target_pairs={{0,1},{1,0},{2,3},{3,2},{4,5},{5,4},{6,7},{7,6},{8,9},{9,8},{10,11... | collective-permute-start | bytes 4718600 | tf_op jit(solution)/shard_map/ppermute | solution.py:196
  849.1 54.9 %collective-permute-start.48 = (f32[192,1536]{1,0:T(8,128)S(1)}, f32[192,1536]{1,0:T(8,128)S(1)}, u32[]{:S(2)}, u32[]{:S(2)}) collective-permute-start(f32[192,1536]{1,0:T(8,128)S(1)} %copy-done.46), channel_id=1, source_target_pairs={{0,4},{4,0},{1,5},{5,1},{2,6},{6,2},{3,7},{7,3},{8,12},{12,8},{9,1... | collective-permute-start | bytes 3538952 | tf_op jit(solution)/shard_map/ppermute | solution.py:196
  852.0 50.8 %collective-permute-start.59 = (f32[192,1536]{1,0:T(8,128)S(1)}, f32[192,1536]{1,0:T(8,128)S(1)}, u32[]{:S(2)}, u32[]{:S(2)}) collective-permute-start(f32[192,1536]{1,0:T(8,128)S(1)} %copy-done.47), channel_id=1, source_target_pairs={{0,4},{4,0},{1,5},{5,1},{2,6},{6,2},{3,7},{7,3},{8,12},{12,8},{9,1... | collective-permute-start | bytes 3538952 | tf_op jit(solution)/shard_map/ppermute | solution.py:196
  853.8 104.7 %collective-permute-start.45 = (f32[2,1,48,1536]{3,2,1,0:T(8,128)}, f32[2,1,48,1536]{3,2,1,0:T(8,128)}, u32[]{:S(2)}, u32[]{:S(2)}) collective-permute-start(f32[2,1,48,1536]{3,2,1,0:T(8,128)} %split.43), channel_id=1, source_target_pairs={{0,2},{2,0},{1,3},{3,1},{4,6},{6,4},{5,7},{7,5},{8,10},{10,8},{9,1... | collective-permute-start | bytes 1769480 | tf_op jit(solution)/shard_map/ppermute | solution.py:196
  907.0 33.8 %collective-permute-start.49 = (f32[48,1536]{1,0:T(8,128)}, f32[48,1536]{1,0:T(8,128)}, u32[]{:S(2)}, u32[]{:S(2)}) collective-permute-start(f32[48,1536]{1,0:T(8,128)} %get-tuple-element.281), channel_id=1, source_target_pairs={{0,8},{8,0},{16,24},{24,16},{1,9},{9,1},{17,25},{25,17},{2,10},{10... | collective-permute-start | bytes 884744 | tf_op jit(solution)/shard_map/ppermute | solution.py:200
  929.9 25.3 %collective-permute-start.50 = (f32[48,1536]{1,0:T(8,128)}, f32[48,1536]{1,0:T(8,128)}, u32[]{:S(2)}, u32[]{:S(2)}) collective-permute-start(f32[48,1536]{1,0:T(8,128)} %get-tuple-element.283), channel_id=1, source_target_pairs={{0,16},{8,24},{16,0},{24,8},{1,17},{9,25},{17,1},{25,9},{2,18},{10... | collective-permute-start | bytes 884744 | tf_op jit(solution)/shard_map/ppermute | solution.py:200
  929.9 26.0 %collective-permute-start.51 = (f32[48,1536]{1,0:T(8,128)S(1)}, f32[48,1536]{1,0:T(8,128)}, u32[]{:S(2)}, u32[]{:S(2)}) collective-permute-start(f32[48,1536]{1,0:T(8,128)S(1)} %get-tuple-element.282), channel_id=1, source_target_pairs={{0,24},{8,16},{16,8},{24,0},{1,25},{9,17},{17,9},{25,1},{2,26},{10... | collective-permute-start | bytes 884744 | tf_op jit(solution)/shard_map/ppermute | solution.py:200
  936.5 191.5 %all-to-all-start.3 = ((bf16[8,128,768]{2,1,0:T(8,128)(2,1)}), bf16[8,128,768]{2,1,0:T(8,128)(2,1)}, u32[]{:S(2)}, u32[]{:S(2)}) async-start(bf16[8,128,768]{2,1,0:T(8,128)(2,1)} %bitcast.280), calls=%async_computation.3 | async-start | bytes 3145728 | tf_op jit(solution)/shard_map/all_to_all | solution.py:561
  940.8 170.0 %collective-permute-start.68 = (f32[768,768]{1,0:T(8,128)}, f32[768,768]{1,0:T(8,128)}, u32[]{:S(2)}, u32[]{:S(2)}) collective-permute-start(f32[768,768]{1,0:T(8,128)} %broadcast_select_fusion), channel_id=1, source_target_pairs={{0,4},{4,0},{1,5},{5,1},{2,6},{6,2},{3,7},{7,3},{8,12},{12,8},{9,1... | collective-permute-start | bytes 7077896 | tf_op jit(solution)/shard_map/ppermute | solution.py:196
  955.3 16.4 %collective-permute-start.55 = (f32[2,1,48,1536]{3,2,1,0:T(8,128)}, f32[2,1,48,1536]{3,2,1,0:T(8,128)S(1)}, u32[]{:S(2)}, u32[]{:S(2)}) collective-permute-start(f32[2,1,48,1536]{3,2,1,0:T(8,128)} %split.45), channel_id=1, source_target_pairs={{0,2},{2,0},{1,3},{3,1},{4,6},{6,4},{5,7},{7,5},{8,10},{10,8},{9,1... | collective-permute-start | bytes 1769480 | tf_op jit(solution)/shard_map/ppermute | solution.py:196
  955.9 58.3 %collective-permute-start.63 = (f32[192,1536]{1,0:T(8,128)}, f32[192,1536]{1,0:T(8,128)}, u32[]{:S(2)}, u32[]{:S(2)}) collective-permute-start(f32[192,1536]{1,0:T(8,128)} %slice_bitcast_fusion.4), channel_id=1, source_target_pairs={{0,2},{2,0},{1,3},{3,1},{4,6},{6,4},{5,7},{7,5},{8,10},{10,8},{9,1... | collective-permute-start | bytes 3538952 | tf_op jit(solution)/shard_map/ppermute | solution.py:196
  958.5 56.2 %collective-permute-start.66 = (f32[192,1536]{1,0:T(8,128)}, f32[192,1536]{1,0:T(8,128)}, u32[]{:S(2)}, u32[]{:S(2)}) collective-permute-start(f32[192,1536]{1,0:T(8,128)} %slice_bitcast_fusion.2), channel_id=1, source_target_pairs={{0,2},{2,0},{1,3},{3,1},{4,6},{6,4},{5,7},{7,5},{8,10},{10,8},{9,1... | collective-permute-start | bytes 3538952 | tf_op jit(solution)/shard_map/ppermute | solution.py:196
  971.7 29.2 %collective-permute-start.46 = (f32[1,48,1536]{2,1,0:T(8,128)S(1)}, f32[1,48,1536]{2,1,0:T(8,128)S(1)}, u32[]{:S(2)}, u32[]{:S(2)}) collective-permute-start(f32[1,48,1536]{2,1,0:T(8,128)S(1)} %slice_bitcast_fusion.14), channel_id=1, source_target_pairs={{0,4},{4,0},{1,5},{5,1},{2,6},{6,2},{3,7},{7,3},{8,12},{12,8},{9,1... | collective-permute-start | bytes 884744 | tf_op jit(solution)/shard_map/ppermute | solution.py:196
  1009.4 29.2 %collective-permute-start.65 = (f32[192,1536]{1,0:T(8,128)}, f32[192,1536]{1,0:T(8,128)}, u32[]{:S(2)}, u32[]{:S(2)}) collective-permute-start(f32[192,1536]{1,0:T(8,128)} %slice_bitcast_fusion.3), channel_id=1, source_target_pairs={{0,4},{4,0},{1,5},{5,1},{2,6},{6,2},{3,7},{7,3},{8,12},{12,8},{9,1... | collective-permute-start | bytes 3538952 | tf_op jit(solution)/shard_map/ppermute | solution.py:196
  1014.2 49.5 %collective-permute-start.34 = (f32[2,2,48,1664]{3,2,1,0:T(8,128)}, f32[2,2,48,1664]{3,2,1,0:T(8,128)S(1)}, u32[]{:S(2)}, u32[]{:S(2)}) collective-permute-start(f32[2,2,48,1664]{3,2,1,0:T(8,128)} %dynamic-slice_bitcast_fusion), channel_id=1, source_target_pairs={{0,4},{4,0},{1,5},{5,1},{2,6},{6,2},{3,7},{7,3},{8,12},{12,8},{9,1... | collective-permute-start | bytes 3833864 | tf_op jit(solution)/shard_map/ppermute | solution.py:196
  1014.7 52.2 %collective-permute-start.32 = (f32[2,2,48,1664]{3,2,1,0:T(8,128)}, f32[2,2,48,1664]{3,2,1,0:T(8,128)S(1)}, u32[]{:S(2)}, u32[]{:S(2)}) collective-permute-start(f32[2,2,48,1664]{3,2,1,0:T(8,128)} %dynamic-slice_bitcast_fusion.1), channel_id=1, source_target_pairs={{0,2},{2,0},{1,3},{3,1},{4,6},{6,4},{5,7},{7,5},{8,10},{10,8},{9,1... | collective-permute-start | bytes 3833864 | tf_op jit(solution)/shard_map/ppermute | solution.py:196
  1038.6 32.2 %collective-permute-start.57 = (f32[24,4608]{1,0:T(8,128)S(1)}, f32[24,4608]{1,0:T(8,128)}, u32[]{:S(2)}, u32[]{:S(2)}) collective-permute-start(f32[24,4608]{1,0:T(8,128)S(1)} %copy-done.62), channel_id=1, source_target_pairs={{0,1},{1,0},{2,3},{3,2},{4,5},{5,4},{6,7},{7,6},{8,9},{9,8},{10,11... | collective-permute-start | bytes 1327112 | tf_op jit(solution)/shard_map/ppermute | solution.py:196
  1066.2 14.6 %collective-permute-start.35 = (f32[2,48,1664]{2,1,0:T(8,128)}, f32[2,48,1664]{2,1,0:T(8,128)}, u32[]{:S(2)}, u32[]{:S(2)}) collective-permute-start(f32[2,48,1664]{2,1,0:T(8,128)} %bitcast_add_fusion), channel_id=1, source_target_pairs={{0,2},{2,0},{1,3},{3,1},{4,6},{6,4},{5,7},{7,5},{8,10},{10,8},{9,1... | collective-permute-start | bytes 1916936 | tf_op jit(solution)/shard_map/ppermute | solution.py:196
  1069.3 14.3 %collective-permute-start.33 = (f32[2,48,1664]{2,1,0:T(8,128)}, f32[2,48,1664]{2,1,0:T(8,128)}, u32[]{:S(2)}, u32[]{:S(2)}) collective-permute-start(f32[2,48,1664]{2,1,0:T(8,128)} %bitcast_add_fusion.2), channel_id=1, source_target_pairs={{0,4},{4,0},{1,5},{5,1},{2,6},{6,2},{3,7},{7,3},{8,12},{12,8},{9,1... | collective-permute-start | bytes 1916936 | tf_op jit(solution)/shard_map/ppermute | solution.py:196
  1086.2 23.8 %collective-permute-start.37 = (f32[48,1664]{1,0:T(8,128)S(1)}, f32[48,1664]{1,0:T(8,128)S(1)}, u32[]{:S(2)}, u32[]{:S(2)}) collective-permute-start(f32[48,1664]{1,0:T(8,128)S(1)} %get-tuple-element.274), channel_id=1, source_target_pairs={{0,16},{8,24},{16,0},{24,8},{1,17},{9,25},{17,1},{25,9},{2,18},{10... | collective-permute-start | bytes 958472 | tf_op jit(solution)/shard_map/ppermute | solution.py:200
  1088.6 21.4 %collective-permute-start.38 = (f32[48,1664]{1,0:T(8,128)S(1)}, f32[48,1664]{1,0:T(8,128)S(1)}, u32[]{:S(2)}, u32[]{:S(2)}) collective-permute-start(f32[48,1664]{1,0:T(8,128)S(1)} %get-tuple-element.275), channel_id=1, source_target_pairs={{0,24},{8,16},{16,8},{24,0},{1,25},{9,17},{17,9},{25,1},{2,26},{10... | collective-permute-start | bytes 958472 | tf_op jit(solution)/shard_map/ppermute | solution.py:200
  1098.0 17.8 %collective-permute-start.64 = (f32[2,96,1536]{2,1,0:T(8,128)S(1)}, f32[2,96,1536]{2,1,0:T(8,128)S(1)}, u32[]{:S(2)}, u32[]{:S(2)}) collective-permute-start(f32[2,96,1536]{2,1,0:T(8,128)S(1)} %copy-done.55), channel_id=1, source_target_pairs={{0,1},{1,0},{2,3},{3,2},{4,5},{5,4},{6,7},{7,6},{8,9},{9,8},{10,11... | collective-permute-start | bytes 3538952 | tf_op jit(solution)/shard_map/ppermute | solution.py:196
  1115.8 20.2 %collective-permute-start.69 = (f32[768,384]{1,0:T(8,128)}, f32[768,384]{1,0:T(8,128)}, u32[]{:S(2)}, u32[]{:S(2)}) collective-permute-start(f32[768,384]{1,0:T(8,128)} %slice_select_fusion), channel_id=1, source_target_pairs={{0,1},{1,0},{2,3},{3,2},{4,5},{5,4},{6,7},{7,6},{8,9},{9,8},{10,11... | collective-permute-start | bytes 3538952 | tf_op jit(solution)/shard_map/ppermute | solution.py:196
  (109 other events, 1802.7 us)

commit v3 on v2

--- a/solution.py
+++ b/solution.py
@@ -227,15 +227,14 @@
     return lax.optimization_barrier((value,) + anchors)[0]
 
 
-def z_parts(parts):
+def shared_chip(parts):
     half = parts[0].shape[1] // 2
     c_me = lax.axis_index('c')
 
     def side(core):
         return jnp.concatenate([lax.dynamic_slice_in_dim(part, core * half, half, axis=1) for part in parts], axis=1)
 
-    chip = in_core_order(side(c_me), hop(side(1 - c_me), 'c'), 0)
-    return [chip] + [z_hop(chip, step) for step in Z_STEPS]
+    return in_core_order(side(c_me), hop(side(1 - c_me), 'c'), 0)
 
 
 def weight_kernel(att_ref, small_ref, att_out, small_out, local_sems, send_sems, recv_sems):
@@ -359,8 +358,8 @@
     up_refs, down_refs, refs = refs[:8], refs[8:16], refs[16:]
     if half == 1:
         acc_in, refs = refs[:2], refs[2:]
-    out_ref, back_ref, g1_away, g1_near, g3_away, g3_near, g2_away, g2_near = refs[:8]
-    w1, w3, w2, act_s, dg_s, dl_s, out_acc, back_acc, lhs_s, sems = refs[8:]
+    out_ref, back_ref, g1_away, g1_near, g3_away, g3_near, g2_away, g2_near, g2_rest = refs[:9]
+    w1, w3, w2, act_s, dg_s, dl_s, out_acc, back_acc, lhs_s, sems = refs[9:]
     step, me = pl.program_id(0), info[0]
     same_y = (me // 2) == half
     pieces = [down_refs[2 * rel:2 * rel + 2] for rel in range(QUAD)]
@@ -398,10 +397,10 @@
 
     for near in range(2):
         @pl.when(step == near)
-        def _(g2_ref=(g2_away, g2_near)[near]):
-            for part in range(2):
-                at = slice(part * 384, part * 384 + 384)
-                g2_ref[at, :] = dot_nn(dd_t_ref[at, :], act_s[:])
+        def _(near=near, g2_ref=(g2_away, g2_near)[near]):
+            half_rows = dd_t_ref.shape[0] // 2
+            g2_ref[:] = dot_nn(dd_t_ref[:half_rows, :], act_s[:])
+            g2_rest[near] = dot_nn(dd_t_ref[half_rows:, :], act_s[:])
 
     @pl.when(step == 1)
     def _():
@@ -418,17 +417,17 @@
     up_spec = pl.BlockSpec((dim // QUAD, dim), lambda step, info_ref: (0, info_ref[1 + step]))
     any_spec = pl.BlockSpec(memory_space=pl.ANY)
     row_out = pl.BlockSpec((2, dim // QUAD, dim), lambda step, info_ref: (0, 0, info_ref[1 + step] - 2 * half))
-    square = fixed(dim, dim)
+    flat, pair = fixed(dim // 2, dim), fixed(2, dim // 2, dim)
     acc_type = F32 if half == 0 else BF16
-    row_shape, square_shape = jax.ShapeDtypeStruct((2, dim // QUAD, 2 * dim), F32), jax.ShapeDtypeStruct((dim, dim), F32)
+    grad_shapes = ((2, dim // QUAD, 2 * dim),) * 4 + ((dim // 2, dim),) * 2 + ((2, dim // 2, dim),)
     return pl.pallas_call(
         lambda *refs: expert_kernel(half, *refs),
         grid_spec=pltpu.PrefetchScalarGridSpec(
             num_scalar_prefetch=1, grid=(2,),
             in_specs=[whole, whole, turned, turned] + [up_spec] * 8 + [any_spec] * 8 + [whole] * len(acc),
-            out_specs=[whole, whole] + [row_out] * QUAD + [square] * 2,
+            out_specs=[whole, whole] + [row_out] * QUAD + [flat, flat, pair],
             scratch_shapes=[pltpu.VMEM((dim, dim), BF16)] * 3 + [pltpu.VMEM((tok, dim), BF16)] * 3 + [pltpu.VMEM((tok, dim), F32)] * 2 + [pltpu.VMEM((QUAD, dim // QUAD, tok), BF16), pltpu.SemaphoreType.DMA((2,))]),
-        out_shape=[jax.ShapeDtypeStruct((tok, dim), acc_type)] * 2 + [row_shape] * QUAD + [square_shape] * 2,
+        out_shape=[jax.ShapeDtypeStruct((tok, dim), acc_type)] * 2 + [jax.ShapeDtypeStruct(shape, F32) for shape in grad_shapes],
         compiler_params=pltpu.CompilerParams(vmem_limit_bytes=VMEM_LIMIT),
         cost_estimate=kernel_cost(36 * tok * dim * dim, dim * dim),
     )(info, rows, dd, rows_t, dd_t, *up, *down, *acc)
@@ -498,7 +497,7 @@
 
 def z_sum(plane):
     summed = plane[0]
-    for step in (1, 2, 3):
+    for step in Z_STEPS:
         summed = summed + z_hop(plane[step], step)
     return summed
 
@@ -518,7 +517,8 @@
         planes = []
         for give, (part, (axis_1, me_1, me_2, name_1, name_2)) in zip(gives, ways):
             got, keep = hop(give, name_1), pick(part, me_1, axis_1)
-            got_2 = hop(pick(keep, 1 - me_2, 1) + pick(got, 1 - me_2, 1), name_2)
+            again = pick(keep, 1 - me_2, 1) + pick(got, 1 - me_2, 1)
+            got_2 = hop(again, name_2)
             planes.append(pick(keep, me_2, 1) + pick(got, me_2, 1) + got_2)
         return jnp.concatenate(planes, axis=0)
 
@@ -537,34 +537,36 @@
 
     up_own, down_own = expert_halves(w1_expert, w3_expert, w2_expert)
     down_x, down_y = plane_near(down_own)
-    w_q, w_k, w_v, w_o = (after(weight, *down_own) for weight in (w_q, w_k, w_v, w_o))
+    up_x, up_y = plane_near(up_own)
+    sh_chip = shared_chip([after(weight, *up_own) for weight in (w1_shared, w3_shared, w2_shared.T)])
+
+    d_out = after(grad_y, sh_chip).reshape(n_tok, model_dim)
+    onehot, dest_row = route_slots(expert_ids.reshape(n_tok), n_experts, capacity)
+    place = (dest_row[:, None] == jnp.arange(n_slots)[None, :]).astype(BF16)
+
+    def exchange(values):
+        return lax.all_to_all(values.reshape(n_experts, capacity, model_dim), ('z', 'c'), 0, 0, tiled=True).reshape(n_slots, model_dim)
+
+    def dispatch(values):
+        return jnp.einsum('ts,td->sd', place, values, preferred_element_type=F32).astype(BF16)
+
+    give_d = dispatch(d_out)
+    d_down = exchange(give_d)
+    w_q, w_k, w_v, w_o = (after(weight, sh_chip) for weight in (w_q, w_k, w_v, w_o))
     att_parts = (w_q.reshape(-1, att_dim), w_k.reshape(-1, att_dim), w_v.reshape(-1, att_dim), w_o.reshape(att_dim, -1).T)
     att_block = jnp.concatenate([part[:, :att_half] for part in att_parts] + [part[:, att_half:] for part in att_parts], axis=1)
     small = jnp.concatenate([gamma_attn.astype(F32)[:, None], gamma_mlp.astype(F32)[:, None], w_router], axis=1)
     small = jnp.pad(small, ((0, 0), (0, LANES - small.shape[1])))
     att_all, small_all = gather_weights(att_block, small)
+
+    def far(from_x, from_y, *gates):
+        return [hop(after(from_y[0], *gates), 'x'), hop(after(from_x[1], *gates), 'y')]
+
+    down_far, up_far = far(down_x, down_y, small_all), far(up_x, up_y, small_all)
+    sh_parts = [sh_chip] + [z_hop(after(sh_chip, small_all), step) for step in Z_STEPS]
     att_all, small_all = att_all.reshape(model_dim, -1), small_all.reshape(model_dim, -1)
     ga_all, gm_all, wr_all = small_all[:, 0], small_all[:, 1], small_all[:, 2:2 + n_experts]
-
-    def far(from_x, from_y, *gates):
-        return [hop(after(from_y[0], *gates), 'x'), hop(after(from_x[1], *gates), 'y')]
-
-    down_far = far(down_x, down_y, small_all)
-    up_x, up_y = plane_near(up_own)
-    sh_parts = z_parts([after(weight, small_all) for weight in (w1_shared, w3_shared, w2_shared.T)])
-
-    d_out = grad_y.reshape(n_tok, model_dim)
-    onehot, dest_row = route_slots(expert_ids.reshape(n_tok), n_experts, capacity)
-    place = (dest_row[:, None] == jnp.arange(n_slots)[None, :]).astype(BF16)
-
-    def exchange(values):
-        return lax.all_to_all(values.reshape(n_experts, capacity, model_dim), ('z', 'c'), 0, 0, tiled=True).reshape(n_slots, model_dim)
-
-    def dispatch(values):
-        return jnp.einsum('ts,td->sd', place, values, preferred_element_type=F32).astype(BF16)
-
     d_out_both = jnp.concatenate([d_out, hop(d_out, 'c')], axis=0)
-    d_out_t = d_out_both.T
     tables = rope_tables(seq_len, head_dim)
 
     tokens = x_in.reshape(n_tok, model_dim)
@@ -581,34 +583,33 @@
     gate_val = jax.nn.sigmoid(jnp.sum(jnp.where(onehot, logits, 0.0), axis=1))
     routed_in = (gate_val[:, None] * normed2_f).astype(BF16)
     give_r = dispatch(routed_in)
-    give_d = dispatch(after(d_out, give_r))
     rows = exchange(give_r)
-    d_down = exchange(after(give_d, rows))
-    rows_t, d_down_t = rows.T, d_down.T
-
+    rows_t, d_down_t = rows.T, after(d_down, give_r).T
     normed2_both = jnp.concatenate([normed2, hop(normed2, 'c')], axis=0)
-    normed2_t = normed2_both.T
-    sh_parts = [after(part, heads) for part in sh_parts]
+    normed2_t, d_out_t = normed2_both.T, after(d_out_both, give_r).T
+    sh_parts = [after(part, qkv) for part in sh_parts]
     sh_own = jnp.stack(sh_parts[:2]), jnp.stack(sh_parts[2:])
     sh_x, sh_y = plane_near(sh_own)
-
-    up_far = far(up_x, up_y, give_r)
-    sh_far = far(sh_x, sh_y, give_r, give_d, normed2_t, d_out_t)
+    sh_far = far(sh_x, sh_y, give_r, normed2_t, d_out_t, d_down_t)
     sh_pieces, up_pieces, down_pieces = ([*own, *from_x, *from_y, *diag] for own, from_x, from_y, diag in ((sh_own, sh_x, sh_y, sh_far), (up_own, up_x, up_y, up_far), (down_own, down_x, down_y, down_far)))
-    shared_part, d_part, (s3_away, s3_near), s1, s2 = shared_ffn(rows_t, normed2_both, d_out_both, normed2_t, d_out_t, sh_pieces)
+    *acc, a1_away, a1_near, a3_away, a3_near, a2_away, a2_near, a2_rest = expert_half(0, rows, d_down, rows_t, d_down_t, up_pieces, down_pieces, ())
+    down_rows, d_rows, b1_away, b1_near, b3_away, b3_near, b2_away, b2_near, b2_rest = expert_half(1, rows, d_down, rows_t, d_down_t, up_pieces, down_pieces, acc)
+    low_y = lax.axis_index('y') == 0
+    rest_got = hop(jnp.where(low_y, b2_rest, a2_rest), 'y')
+    d_back = exchange(d_rows)
+    back_rows = exchange(down_rows)
+    shared_part, d_part, (s3_away, s3_near), s1, s2 = shared_ffn(d_rows, normed2_both, d_out_both, normed2_t, d_out_t, sh_pieces)
     shared_out = shared_part[0] + hop(shared_part[1], 'c')
     d_normed2 = d_part[0] + hop(d_part[1], 'c')
 
-    *acc, a1_away, a1_near, a3_away, a3_near, a2_away, a2_near = expert_half(0, rows, d_down, rows_t, d_down_t, up_pieces, down_pieces, ())
-    down_rows, d_rows, b1_away, b1_near, b3_away, b3_near, b2_away, b2_near = expert_half(1, rows, d_down, rows_t, d_down_t, up_pieces, down_pieces, acc)
-    d_back = exchange(d_rows)
-
-    def first_sum(away, near, axis, gate):
-        keep, give = near + after(hop(away, axis), *gate)
-        return keep, hop(give, 'y' if axis == 'x' else 'x')
-
-    s3 = first_sum(s3_away, s3_near, 'x', [d_rows])
-    a1 = first_sum(a1_away, a1_near, 'x', [d_rows])
+
+    def first_sum(away, near, axis):
+        got = hop(away, axis)
+        give = near[1] + got[1]
+        return near[0] + got[0], hop(give, 'y' if axis == 'x' else 'x')
+
+    a1 = first_sum(a1_away, a1_near, 'x')
+
     d_routed_in = jnp.einsum('ts,sd->td', place, d_back, preferred_element_type=F32)
     d_normed2 = d_normed2 + gate_val[:, None] * d_routed_in
     d_gate_val = jnp.sum(d_routed_in * normed2_f, axis=1) * gate_val * (1.0 - gate_val)
@@ -639,46 +640,43 @@
     g_att.append(mine + hop(other, 'c'))
     att_gives, att_rest = plane_sum_values(jnp.concatenate(g_att, axis=1).reshape(QUAD, 2, 2, ROWS, -1))
 
-    def later(value):
-        return after(value, *att_gives)
-
-    low_y = lax.axis_index('y') == 0
-    g2_low, g2_high = a2_near + later(hop(a2_away, 'x')), b2_near + later(hop(b2_away, 'x'))
-    g2_keep, g2_give = jnp.where(low_y, g2_low, g2_high), jnp.where(low_y, g2_high, g2_low)
+    g2_low, g2_high = a2_near + hop(a2_away, 'x'), b2_near + hop(b2_away, 'x')
+    g2_give = jnp.where(low_y, g2_high, g2_low)
+    rest_away, rest_near = jnp.where(low_y, a2_rest, b2_rest) + rest_got
+    s3, a3 = first_sum(s3_away, s3_near, 'x'), first_sum(a3_away, a3_near, 'y')
+    b3, b1 = first_sum(b3_away, b3_near, 'y'), first_sum(b1_away, b1_near, 'x')
+
+    def finish(pair):
+        mine, got = pair
+        return mine + got
+
+    def rows_by_expert(pairs):
+        both = jnp.stack([finish(pair) for pair in pairs])
+        halves = both.reshape(2, 2, both.shape[1] // 2, -1)
+        give = pick(halves, 1 - lax.axis_index('c'), 1)
+        return in_core_order(pick(halves, lax.axis_index('c'), 1)[None], hop(give, 'c')[None], 0)
+
+    g2_full = jnp.concatenate([jnp.where(low_y, g2_low, g2_high) + hop(g2_give, 'y'), rest_near + hop(rest_away, 'x')], axis=0)
+    g2_mine, g2_other = core_halves(g2_full, 1)
+    g_up = jnp.concatenate([rows_by_expert((a1, a3)), rows_by_expert((b1, b3))], axis=-1)
+    att_plane = att_rest()
 
     def z_first(parts):
         total = parts[0]
         for step in Z_STEPS:
-            total = total + after(z_hop(parts[step], step), g2_give)
-        return jnp.split(total.reshape(2, 2, ROWS, -1), 2, axis=1)
-
-    def z_last(pair):
-        keep, give = pair
+            total = total + z_hop(parts[step], step)
+        keep, give = jnp.split(total.reshape(2, 2, ROWS, -1), 2, axis=1)
         keep, give = keep + hop(give, 'x')
         return (keep + hop(give, 'y')).reshape(ROWS, -1)
 
-    s1, s2 = z_first(s1), z_first(s2)
-    b_gates = [s1[1], s2[1]]
-    routed = jnp.einsum('ts,sd->td', place, exchange(later(down_rows)), preferred_element_type=F32)
+    z_me = lax.axis_index('z')
+    att_planes = [pick(att_plane, z_me ^ step, 0) for step in range(QUAD)]
+    g_att_mine, g_att_other = swap_rows(z_sum(att_planes))
+    g_sh = jnp.concatenate([z_first(s1), z_sum(finish(s3).reshape(QUAD, ROWS, -1)), z_first(s2)], axis=1)
+    g_sh_mine, g_sh_other = swap_rows(g_sh)
+    g_w2e = in_core_order(g2_mine.T[None], hop(g2_other, 'c').T[None], 0)
+    routed = jnp.einsum('ts,sd->td', place, after(back_rows, *att_gives), preferred_element_type=F32)
     layer_out = (hidden.astype(F32) + routed + shared_out).astype(BF16)
-    a3 = first_sum(a3_away, a3_near, 'y', att_gives)
-    b1, b3 = first_sum(b1_away, b1_near, 'x', b_gates), first_sum(b3_away, b3_near, 'y', b_gates)
-
-    def finish(pair, *gates):
-        mine, got = pair
-        return mine + later(after(got, *gates) if gates else got)
-
-    def rows_by_expert(pairs, *gates):
-        return in_core_order(*(part[None] for part in swap_rows(jnp.stack([finish(pair, *gates) for pair in pairs]))), 0)
-
-    g_up = jnp.concatenate([rows_by_expert((a1, a3), b1[0], b3[0]), rows_by_expert((b1, b3))], axis=-1)
-    g2_mine, g2_other = core_halves(g2_keep + hop(g2_give, 'y'), 1)
-    g_w2e = in_core_order(g2_mine.T[None], hop(g2_other, 'c').T[None], 0)
-    g_sh = jnp.concatenate([z_last(s1), z_sum(finish(s3).reshape(QUAD, ROWS, -1)), z_last(s2)], axis=1)
-    g_sh_mine, g_sh_other = swap_rows(g_sh)
-    z_me = lax.axis_index('z')
-    att_plane = att_rest()
-    g_att_mine, g_att_other = swap_rows(z_sum([pick(att_plane, z_me ^ step, 0) for step in range(QUAD)]))
     d_x = (d_hidden.astype(F32) + d_tok_norm.astype(F32)).astype(BF16).reshape(n_batch, seq_len, model_dim)
 
     g_small = in_core_order(*(part[:, QUAD * att_half:QUAD * att_half + 8] for part in (g_att_mine, g_att_other)), 1)

time: 1150 us -> 1030 us (0.90)
  waiting for transfers between devices: 580 us -> 499 us
  starting transfers between devices: 140 us -> 93.5 us
  Pallas kernels: 215 us -> 245 us
  local copies, waits for them, and re-layouts: 91.5 us -> 75.8 us
    ppermute x55 -> x57, waiting for transfers between devices: 369 us -> 307 us  [hop(): return lax.ppermute(block, axis, SWAP)]
    all_to_all x4, waiting for transfers between devices: 43.5 us -> 0.01 us  [exchange(): lax.all_to_all(values.reshape(n_experts, capacity, model_dim), ('z', 'c')...]
    ppermute x15, starting transfers between devices: 62.5 us -> 24.3 us  [z_hop(): lax.ppermute(block, 'z', [(z_idx, z_idx ^ step) for z_idx in range(QUAD)])]
    pallas_call x1, Pallas kernels: 40.7 us -> 70.4 us  [gather_weights(): pl.pallas_call(weight_kernel, in_specs=[any_spec] * 2, out_specs=[any_spe...]
    ppermute x15, waiting for transfers between devices: 167 us -> 192 us  [z_hop(): lax.ppermute(block, 'z', [(z_idx, z_idx ^ step) for z_idx in range(QUAD)])]
    unnamed x222 -> x205, local copies, waits for them, and re-layouts: 26.2 us -> 19.6 us
    add x19 -> x21, other arithmetic: 25 us -> 28.1 us  [the longest x5 9.21 us: first_sum(): give = near[1] + got[1]]
    ppermute x55 -> x57, starting transfers between devices: 49.2 us -> 50.2 us  [hop(): return lax.ppermute(block, axis, SWAP)]
  transfers between devices with their start and end apart: 74 -> 76, of which waited for: 24 -> 29; matrix products, arithmetic and copies ran while one was open for 16% -> 16% of each run, Pallas kernels for 19% -> 24%
where the time goes in v3:
time: 1030 us; the launch traced here: 1020 us
  waiting for transfers between devices  499 us (48%)
  Pallas kernels  245 us (24%)
  starting transfers between devices  93.5 us (9%)
  local copies, waits for them, and re-layouts  75.8 us (7%)
  other arithmetic  69 us (7%)
  matrix products  33 us (3%)
    ppermute x57, waiting for transfers between devices, hop(): return lax.ppermute(block, axis, SWAP)  307 us
    ppermute x15, waiting for transfers between devices, z_hop(): lax.ppermute(block, 'z', [(z_idx, z_idx ^ step) for z_idx in range(QUAD)])  192 us
    pallas_call x2, Pallas kernels, expert_half(): pl.pallas_call(lambda *refs: expert_kernel(half, *refs), grid_spec=pltpu....  80.6 us
    pallas_call x1, Pallas kernels, gather_weights(): pl.pallas_call(weight_kernel, in_specs=[any_spec] * 2, out_specs=[any_spe...  70.4 us
    pallas_call x2, Pallas kernels, attn_call(): pl.pallas_call(kernel, grid=(6,), in_specs=head_specs + extra + [table, t...  51 us
    ppermute x57, starting transfers between devices, hop(): return lax.ppermute(block, axis, SWAP)  50.2 us
    pallas_call x1, Pallas kernels, shared_ffn(): pl.pallas_call(shared_kernel, grid_spec=pltpu.PrefetchScalarGridSpec(num_...  35.4 us
    ppermute x15, starting transfers between devices, z_hop(): lax.ppermute(block, 'z', [(z_idx, z_idx ^ step) for z_idx in range(QUAD)])  24.3 us
  transfers between devices with their start and end apart: 76, of which 29 were waited for; matrix products, arithmetic and copies ran while one was open for 16% of the time, Pallas kernels for 24%

profile of v3, /device:TPU:0, one launch (start us, length us, event | category | flops | bytes accessed | tf_op | source)
XLA Modules:
  0.0 1016.9 jit_solution(3126824136960222118)
XLA Ops:
  8.6 2.5 collective-permute-start.4
  21.4 2.6 copy.241
  24.0 4.9 all-to-all-start.1
  28.9 70.4 %shard_map.289 = (bf16[32,24,3072]{2,1,0:T(8,128)(2,1)}, f32[32,24,128]{2,1,0:T(8,128)}) custom-call(bf16[24,3072]{1,0:T(8,128)(2,1)} %copy-done.82, f32[24,128]{1,0:T(8,128)} %select_maximum_fusion.small_ref), custom_call_target="tpu_custom_call" | custom-call | flops 7372800000 | bytes 73728 | tf_op jit(solution)/shard_map/pallas_call | solution.py:307
  99.3 4.4 collective-permute-start.19
  108.0 7.2 shard_map.290
  115.2 19.4 %shard_map.291 = bf16[512,768]{1,0:T(8,128)(2,1)} custom-call(bf16[512,2304]{1,0:T(8,128)(2,1)} %get-tuple-element.83.q_ref.k_ref.v_ref, bf16[512,2304]{1,0:T(8,128)(2,1)} %get-tuple-element.83.q_ref.k_ref.v_ref, bf16[512,2304]{1,0:T(8,128)(2,1)} %get-tuple-element.83.q_ref.k_ref.v_ref, f32[512,128]{1,0:T(8,128)} %constant.226.clone.cos_ref, ...), custom_call_target="tpu_custom_call" | custom-call | flops 1073741824 | bytes 1179648 | tf_op jit(solution)/shard_map/pallas_call | solution.py:176
  142.3 2.6 copy.238
  144.9 4.8 all-to-all-start
  155.2 2.4 pad_maximum_fusion.9.refs_1_.refs_9_.refs_17_
  157.7 10.0 collective-permute-done.11.refs_16_
  167.7 11.8 %collective-permute-done.10.refs_15_ = bf16[384,768]{1,0:T(8,128)(2,1)} collective-permute-done((bf16[384,768]{1,0:T(8,128)(2,1)}, bf16[384,768]{1,0:T(8,128)(2,1)}, u32[]{:S(2)}, u32[]{:S(2)}) %collective-permute-start.10) | collective-permute-done | bytes 589856 | tf_op jit(solution)/shard_map/ppermute | solution.py:196
  179.6 11.4 %collective-permute-done.13.refs_18_ = bf16[384,768]{1,0:T(8,128)(2,1)} collective-permute-done((bf16[384,768]{1,0:T(8,128)(2,1)}, bf16[384,768]{1,0:T(8,128)(2,1)}, u32[]{:S(2)}, u32[]{:S(2)}) %collective-permute-start.13) | collective-permute-done | bytes 589856 | tf_op jit(solution)/shard_map/ppermute | solution.py:196
  198.6 9.0 collective-permute-done.14.refs_19_
  209.0 17.5 %collective-permute-done.22.refs_3_.refs_11_.refs_19_ = bf16[2,48,4608]{2,1,0:T(8,128)(2,1)} collective-permute-done((bf16[2,48,4608]{2,1,0:T(8,128)(2,1)}, bf16[2,48,4608]{2,1,0:T(8,128)(2,1)}, u32[]{:S(2)}, u32[]{:S(2)}) %collective-permute-start.22) | collective-permute-done | bytes 884768 | tf_op jit(solution)/shard_map/ppermute | solution.py:196
  229.1 2.5 pad_maximum_fusion.4
  231.6 2.6 copy.248.dd_ref
  234.3 3.2 fusion.128
  237.5 2.6 copy.247.rows_ref
  240.7 2.8 copy_bitcast_fusion
  243.5 2.6 copy.246.refs_2_
  246.0 3.5 fusion.127
  249.5 2.6 copy.245.refs_1_
  252.1 27.0 %collective-permute-done.15.refs_20_ = bf16[384,768]{1,0:T(8,128)(2,1)S(1)} collective-permute-done((bf16[384,768]{1,0:T(8,128)(2,1)}, bf16[384,768]{1,0:T(8,128)(2,1)S(1)}, u32[]{:S(2)}, u32[]{:S(2)}) %collective-permute-start.15) | collective-permute-done | bytes 589856 | tf_op jit(solution)/shard_map/ppermute | solution.py:196
  283.2 39.7 %shard_map.292 = (f32[1024,768]{1,0:T(8,128)}, f32[1024,768]{1,0:T(8,128)}, f32[2,192,1536]{2,1,0:T(8,128)}, f32[2,192,1536]{2,1,0:T(8,128)}, f32[2,192,1536]{2,...) custom-call(s32[3]{0:T(128)} %get-tuple-element.277.refs_0_, ...), custom_call_target="tpu_custom_call" | custom-call | flops 21743271936 | bytes 589824 | tf_op jit(solution)/shard_map/pallas_call | solution.py:423
  322.9 40.9 %shard_map.293 = (bf16[1024,768]{1,0:T(8,128)(2,1)}, bf16[1024,768]{1,0:T(8,128)(2,1)}, f32[2,192,1536]{2,1,0:T(8,128)}, f32[2,192,1536]{2,1,0:T(8,128)}, f32[2,...) custom-call(s32[3]{0:T(128)} %get-tuple-element.276.refs_0_, ...), custom_call_target="tpu_custom_call" | custom-call | flops 21743271936 | bytes 589824 | tf_op jit(solution)/shard_map/pallas_call | solution.py:423
  365.9 35.4 %shard_map.294 = (f32[512,768]{1,0:T(8,128)}, f32[512,768]{1,0:T(8,128)}, f32[512,768]{1,0:T(8,128)}, f32[512,768]{1,0:T(8,128)}, f32[2,192,1536]{2,1,0:T(8,128)...) custom-call(s32[2]{0:T(128)} %pad_add_fusion.3.info, ...), custom_call_target="tpu_custom_call" | custom-call | flops 21743271936 | bytes 1179648 | tf_op jit(solution)/shard_map/pallas_call | solution.py:484
  406.1 8.2 collective-permute-done.66
  416.3 36.5 %collective-permute-done.40 = f32[192,1536]{1,0:T(8,128)} collective-permute-done((f32[192,1536]{1,0:T(8,128)}, f32[192,1536]{1,0:T(8,128)}, u32[]{:S(2)}, u32[]{:S(2)}) %collective-permute-start.40) | collective-permute-done | bytes 1179680 | tf_op jit(solution)/shard_map/ppermute | solution.py:200
  455.1 4.5 all-to-all-start.3
  459.7 23.6 %collective-permute-done.41 = f32[192,1536]{1,0:T(8,128)} collective-permute-done((f32[192,1536]{1,0:T(8,128)}, f32[192,1536]{1,0:T(8,128)}, u32[]{:S(2)}, u32[]{:S(2)}) %collective-permute-start.41) | collective-permute-done | bytes 1179680 | tf_op jit(solution)/shard_map/ppermute | solution.py:200
  487.1 3.3 broadcast_select_fusion
  490.5 3.0 copy.249
  493.5 3.0 copy.250
  496.5 3.0 copy.262
  499.6 3.1 copy.263
  502.6 2.8 broadcast_select_fusion.1
  506.7 94.6 %collective-permute-done.51 = f32[192,1536]{1,0:T(8,128)} collective-permute-done((f32[192,1536]{1,0:T(8,128)}, f32[192,1536]{1,0:T(8,128)}, u32[]{:S(2)}, u32[]{:S(2)}) %collective-permute-start.51) | collective-permute-done | bytes 1179680 | tf_op jit(solution)/shard_map/ppermute | solution.py:200
  602.7 2.5 add_add_fusion.3
  610.1 2.6 fusion.44
  612.7 2.6 fusion.47
  618.0 37.5 %collective-permute-done.61 = f32[2,192,1536]{2,1,0:T(8,128)S(1)} collective-permute-done((f32[2,192,1536]{2,1,0:T(8,128)S(1)}, f32[2,192,1536]{2,1,0:T(8,128)S(1)}, u32[]{:S(2)}, u32[]{:S(2)}) %collective-permute-start.61) | collective-permute-done | bytes 2359328 | tf_op jit(solution)/shard_map/ppermute | solution.py:196
  660.6 13.0 %collective-permute-done.68 = f32[384,768]{1,0:T(8,128)S(1)} collective-permute-done((f32[384,768]{1,0:T(8,128)S(1)}, f32[384,768]{1,0:T(8,128)S(1)}, u32[]{:S(2)}, u32[]{:S(2)}) %collective-permute-start.68) | collective-permute-done | bytes 1179680 | tf_op jit(solution)/shard_map/ppermute | solution.py:196
  674.2 3.0 select_add_fusion.1
  678.3 40.3 %collective-permute-done.43 = f32[2,1,48,1536]{3,2,1,0:T(8,128)S(1)} collective-permute-done((f32[2,1,48,1536]{3,2,1,0:T(8,128)S(1)}, f32[2,1,48,1536]{3,2,1,0:T(8,128)S(1)}, u32[]{:S(2)}, u32[]{:S(2)}) %collective-permute-start.43) | collective-permute-done | bytes 589856 | tf_op jit(solution)/shard_map/ppermute | solution.py:196
  720.1 11.1 %collective-permute-done.53 = f32[2,1,48,1536]{3,2,1,0:T(8,128)S(1)} collective-permute-done((f32[2,1,48,1536]{3,2,1,0:T(8,128)S(1)}, f32[2,1,48,1536]{3,2,1,0:T(8,128)S(1)}, u32[]{:S(2)}, u32[]{:S(2)}) %collective-permute-start.53) | collective-permute-done | bytes 589856 | tf_op jit(solution)/shard_map/ppermute | solution.py:196
  734.5 4.9 all-to-all-start.2
  739.4 2.6 fusion.12
  752.7 31.6 %shard_map.295 = bf16[512,2304]{1,0:T(8,128)(2,1)} custom-call(bf16[512,2304]{1,0:T(8,128)(2,1)} %get-tuple-element.83.q_ref.k_ref.v_ref, bf16[512,2304]{1,0:T(8,128)(2,1)} %get-tuple-element.83.q_ref.k_ref.v_ref, bf16[512,2304]{1,0:T(8,128)(2,1)} %get-tuple-element.83.q_ref.k_ref.v_ref, bf16[512,768]{1,0:T(8,128)(2,1)} %pad_maximum_fusion.11.do_ref, ...), custom_call_target="tpu_custom_call" | custom-call | flops 2147483648 | bytes 1179648 | tf_op jit(solution)/shard_map/pallas_call | solution.py:176
  784.3 3.2 fusion.6
  787.6 3.8 fusion.19
  794.6 3.0 fusion.53
  803.4 6.7 collective-permute-done.54
  819.0 21.8 %collective-permute-done.57 = f32[192,1536]{1,0:T(8,128)S(1)} collective-permute-done((f32[192,1536]{1,0:T(8,128)}, f32[192,1536]{1,0:T(8,128)S(1)}, u32[]{:S(2)}, u32[]{:S(2)}) %collective-permute-start.57) | collective-permute-done | bytes 1179680 | tf_op jit(solution)/shard_map/ppermute | solution.py:196
  843.3 22.0 %collective-permute-done.62 = f32[192,1536]{1,0:T(8,128)S(1)} collective-permute-done((f32[192,1536]{1,0:T(8,128)S(1)}, f32[192,1536]{1,0:T(8,128)S(1)}, u32[]{:S(2)}, u32[]{:S(2)}) %collective-permute-start.62) | collective-permute-done | bytes 1179680 | tf_op jit(solution)/shard_map/ppermute | solution.py:196
  870.2 22.3 %collective-permute-done.46 = f32[192,1536]{1,0:T(8,128)S(1)} collective-permute-done((f32[192,1536]{1,0:T(8,128)S(1)}, f32[192,1536]{1,0:T(8,128)S(1)}, u32[]{:S(2)}, u32[]{:S(2)}) %collective-permute-start.46) | collective-permute-done | bytes 1179680 | tf_op jit(solution)/shard_map/ppermute | solution.py:196
  899.1 7.2 collective-permute-done.47
  906.3 12.9 %collective-permute-done.48 = f32[48,1536]{1,0:T(8,128)S(1)} collective-permute-done((f32[48,1536]{1,0:T(8,128)S(1)}, f32[48,1536]{1,0:T(8,128)S(1)}, u32[]{:S(2)}, u32[]{:S(2)}) %collective-permute-start.48) | collective-permute-done | bytes 294944 | tf_op jit(solution)/shard_map/ppermute | solution.py:200
  932.4 2.7 slice_bitcast_fusion
  941.9 17.7 %collective-permute-done.34 = f32[2,2,48,1664]{3,2,1,0:T(8,128)} collective-permute-done((f32[2,2,48,1664]{3,2,1,0:T(8,128)}, f32[2,2,48,1664]{3,2,1,0:T(8,128)}, u32[]{:S(2)}, u32[]{:S(2)}) %collective-permute-start.34) | collective-permute-done | bytes 1277984 | tf_op jit(solution)/shard_map/ppermute | solution.py:196
  964.5 12.1 %collective-permute-done.35 = f32[2,48,1664]{2,1,0:T(8,128)S(1)} collective-permute-done((f32[2,48,1664]{2,1,0:T(8,128)S(1)}, f32[2,48,1664]{2,1,0:T(8,128)S(1)}, u32[]{:S(2)}, u32[]{:S(2)}) %collective-permute-start.35) | collective-permute-done | bytes 639008 | tf_op jit(solution)/shard_map/ppermute | solution.py:196
  988.7 2.6 fusion.1
  991.4 3.0 collective-permute-done.36
  994.4 13.9 %collective-permute-done.37 = f32[48,1664]{1,0:T(8,128)S(1)} collective-permute-done((f32[48,1664]{1,0:T(8,128)S(1)}, f32[48,1664]{1,0:T(8,128)S(1)}, u32[]{:S(2)}, u32[]{:S(2)}) %collective-permute-start.37) | collective-permute-done | bytes 319520 | tf_op jit(solution)/shard_map/ppermute | solution.py:200
  (450 shorter events, 175.9 us)
Async XLA Ops:
  8.6 183.9 %collective-permute-start.4 = (bf16[192,3072]{1,0:T(8,128)(2,1)}, bf16[192,3072]{1,0:T(8,128)(2,1)}, u32[]{:S(2)}, u32[]{:S(2)}) collective-permute-start(bf16[192,3072]{1,0:T(8,128)(2,1)} %pad_maximum_fusion.7.refs_6_), channel_id=1, source_target_pairs={{0,2},{2,0},{1,3},{3,1},{4,6},{6,4},{5,7},{7,5},{8,10},{10,8},{9,1... | collective-permute-start | bytes 3538952 | tf_op jit(solution)/shard_map/ppermute | solution.py:196
  16.3 133.3 %collective-permute-start.12 = (bf16[384,768]{1,0:T(8,128)(2,1)}, bf16[384,768]{1,0:T(8,128)(2,1)}, u32[]{:S(2)}, u32[]{:S(2)}) collective-permute-start(bf16[384,768]{1,0:T(8,128)(2,1)} %get-tuple-element.228.refs_13_), channel_id=1, source_target_pairs={{0,4},{4,0},{1,5},{5,1},{2,6},{6,2},{3,7},{7,3},{8,12},{12,8},{9,1... | collective-permute-start | bytes 1769480 | tf_op jit(solution)/shard_map/ppermute | solution.py:196
  24.0 120.9 %all-to-all-start.1 = ((bf16[8,128,768]{1,2,0:T(8,128)(2,1)}), bf16[8,128,768]{1,2,0:T(8,128)(2,1)}, u32[]{:S(2)}, u32[]{:S(2)}) async-start(bf16[8,128,768]{1,2,0:T(8,128)(2,1)} %copy.241), calls=%async_computation.1 | async-start | bytes 3145728 | tf_op jit(solution)/shard_map/all_to_all | solution.py:548
  99.3 52.0 %collective-permute-start.19 = (bf16[48,4608]{1,0:T(8,128)(2,1)S(1)}, bf16[48,4608]{1,0:T(8,128)(2,1)}, u32[]{:S(2)}, u32[]{:S(2)}) collective-permute-start(bf16[48,4608]{1,0:T(8,128)(2,1)S(1)} %pad_maximum_fusion.12), channel_id=1, source_target_pairs={{0,16},{8,24},{16,0},{24,8},{1,17},{9,25},{17,1},{25,9},{2,18},{10... | collective-permute-start | bytes 1327112 | tf_op jit(solution)/shard_map/ppermute | solution.py:200
  103.7 48.1 %collective-permute-start.20 = (bf16[48,4608]{1,0:T(8,128)(2,1)S(1)}, bf16[48,4608]{1,0:T(8,128)(2,1)}, u32[]{:S(2)}, u32[]{:S(2)}) collective-permute-start(bf16[48,4608]{1,0:T(8,128)(2,1)S(1)} %pad_maximum_fusion.12), channel_id=1, source_target_pairs={{0,24},{8,16},{16,8},{24,0},{1,25},{9,17},{17,9},{25,1},{2,26},{10... | collective-permute-start | bytes 1327112 | tf_op jit(solution)/shard_map/ppermute | solution.py:200
  104.6 48.6 %collective-permute-start.18 = (bf16[48,4608]{1,0:T(8,128)(2,1)S(1)}, bf16[48,4608]{1,0:T(8,128)(2,1)}, u32[]{:S(2)}, u32[]{:S(2)}) collective-permute-start(bf16[48,4608]{1,0:T(8,128)(2,1)S(1)} %pad_maximum_fusion.12), channel_id=1, source_target_pairs={{0,8},{8,0},{16,24},{24,16},{1,9},{9,1},{17,25},{25,17},{2,10},{10... | collective-permute-start | bytes 1327112 | tf_op jit(solution)/shard_map/ppermute | solution.py:200
  144.9 101.2 %all-to-all-start = ((bf16[8,128,768]{1,2,0:T(8,128)(2,1)}), bf16[8,128,768]{1,2,0:T(8,128)(2,1)}, u32[]{:S(2)}, u32[]{:S(2)}) async-start(bf16[8,128,768]{1,2,0:T(8,128)(2,1)} %copy.238), calls=%async_computation | async-start | bytes 3145728 | tf_op jit(solution)/shard_map/all_to_all | solution.py:548
  149.7 45.4 %collective-permute-start.5 = (bf16[192,3072]{1,0:T(8,128)(2,1)}, bf16[192,3072]{1,0:T(8,128)(2,1)}, u32[]{:S(2)}, u32[]{:S(2)}) collective-permute-start(bf16[192,3072]{1,0:T(8,128)(2,1)} %pad_maximum_fusion.6.refs_5_), channel_id=1, source_target_pairs={{0,4},{4,0},{1,5},{5,1},{2,6},{6,2},{3,7},{7,3},{8,12},{12,8},{9,1... | collective-permute-start | bytes 3538952 | tf_op jit(solution)/shard_map/ppermute | solution.py:196
  151.2 16.5 %collective-permute-start.11 = (bf16[384,768]{1,0:T(8,128)(2,1)}, bf16[384,768]{1,0:T(8,128)(2,1)}, u32[]{:S(2)}, u32[]{:S(2)}) collective-permute-start(bf16[384,768]{1,0:T(8,128)(2,1)} %get-tuple-element.227.refs_14_), channel_id=1, source_target_pairs={{0,2},{2,0},{1,3},{3,1},{4,6},{6,4},{5,7},{7,5},{8,10},{10,8},{9,1... | collective-permute-start | bytes 1769480 | tf_op jit(solution)/shard_map/ppermute | solution.py:196
  151.8 27.8 %collective-permute-start.10 = (bf16[384,768]{1,0:T(8,128)(2,1)}, bf16[384,768]{1,0:T(8,128)(2,1)}, u32[]{:S(2)}, u32[]{:S(2)}) collective-permute-start(bf16[384,768]{1,0:T(8,128)(2,1)} %get-tuple-element.228.refs_13_), channel_id=1, source_target_pairs={{0,2},{2,0},{1,3},{3,1},{4,6},{6,4},{5,7},{7,5},{8,10},{10,8},{9,1... | collective-permute-start | bytes 1769480 | tf_op jit(solution)/shard_map/ppermute | solution.py:196
  153.2 37.8 %collective-permute-start.13 = (bf16[384,768]{1,0:T(8,128)(2,1)}, bf16[384,768]{1,0:T(8,128)(2,1)}, u32[]{:S(2)}, u32[]{:S(2)}) collective-permute-start(bf16[384,768]{1,0:T(8,128)(2,1)} %get-tuple-element.227.refs_14_), channel_id=1, source_target_pairs={{0,4},{4,0},{1,5},{5,1},{2,6},{6,2},{3,7},{7,3},{8,12},{12,8},{9,1... | collective-permute-start | bytes 1769480 | tf_op jit(solution)/shard_map/ppermute | solution.py:196
  167.7 28.8 %collective-permute-start.16 = (bf16[512,768]{0,1:T(8,128)(2,1)S(1)}, bf16[512,768]{0,1:T(8,128)(2,1)}, u32[]{:S(2)}, u32[]{:S(2)}) collective-permute-start(bf16[512,768]{0,1:T(8,128)(2,1)S(1)} %fusion.10), channel_id=1, source_target_pairs={{0,1},{1,0},{2,3},{3,2},{4,5},{5,4},{6,7},{7,6},{8,9},{9,8},{10,11... | collective-permute-start | bytes 2359304 | tf_op jit(solution)/shard_map/ppermute | solution.py:196
  179.6 17.6 %collective-permute-start.17 = (bf16[512,768]{0,1:T(8,128)(2,1)S(1)}, bf16[512,768]{0,1:T(8,128)(2,1)}, u32[]{:S(2)}, u32[]{:S(2)}) collective-permute-start(bf16[512,768]{0,1:T(8,128)(2,1)S(1)} %bitcast.274), channel_id=1, source_target_pairs={{0,1},{1,0},{2,3},{3,2},{4,5},{5,4},{6,7},{7,6},{8,9},{9,8},{10,11... | collective-permute-start | bytes 2359304 | tf_op jit(solution)/shard_map/ppermute | solution.py:196
  191.0 16.5 %collective-permute-start.14 = (bf16[384,768]{1,0:T(8,128)(2,1)}, bf16[384,768]{1,0:T(8,128)(2,1)}, u32[]{:S(2)}, u32[]{:S(2)}) collective-permute-start(bf16[384,768]{1,0:T(8,128)(2,1)} %collective-permute-done.12.refs_17_), channel_id=1, source_target_pairs={{0,2},{2,0},{1,3},{3,1},{4,6},{6,4},{5,7},{7,5},{8,10},{10,8},{9,1... | collective-permute-start | bytes 1769480 | tf_op jit(solution)/shard_map/ppermute | solution.py:196
  192.5 34.0 %collective-permute-start.22 = (bf16[2,48,4608]{2,1,0:T(8,128)(2,1)}, bf16[2,48,4608]{2,1,0:T(8,128)(2,1)}, u32[]{:S(2)}, u32[]{:S(2)}) collective-permute-start(bf16[2,48,4608]{2,1,0:T(8,128)(2,1)} %pad_maximum_fusion.9.refs_1_.refs_9_.refs_17_), channel_id=1, source_target_pairs={{0,2},{2,0},{1,3},{3,1},{4,6},{6,4},{5,7},{7,5},{8,10},{10,8},{9,1... | collective-permute-start | bytes 2654216 | tf_op jit(solution)/shard_map/ppermute | solution.py:196
  195.1 44.9 %collective-permute-start.23 = (bf16[2,48,4608]{2,1,0:T(8,128)(2,1)}, bf16[2,48,4608]{2,1,0:T(8,128)(2,1)}, u32[]{:S(2)}, u32[]{:S(2)}) collective-permute-start(bf16[2,48,4608]{2,1,0:T(8,128)(2,1)} %pad_maximum_fusion.8.refs_0_.refs_8_.refs_16_), channel_id=1, source_target_pairs={{0,4},{4,0},{1,5},{5,1},{2,6},{6,2},{3,7},{7,3},{8,12},{12,8},{9,1... | collective-permute-start | bytes 2654216 | tf_op jit(solution)/shard_map/ppermute | solution.py:196
  196.6 84.0 %collective-permute-start.6 = (bf16[192,3072]{1,0:T(8,128)(2,1)}, bf16[192,3072]{1,0:T(8,128)(2,1)}, u32[]{:S(2)}, u32[]{:S(2)}) collective-permute-start(bf16[192,3072]{1,0:T(8,128)(2,1)} %pad_maximum_fusion.7.refs_6_), channel_id=1, source_target_pairs={{0,4},{4,0},{1,5},{5,1},{2,6},{6,2},{3,7},{7,3},{8,12},{12,8},{9,1... | collective-permute-start | bytes 3538952 | tf_op jit(solution)/shard_map/ppermute | solution.py:196
  197.1 84.0 %collective-permute-start.3 = (bf16[192,3072]{1,0:T(8,128)(2,1)}, bf16[192,3072]{1,0:T(8,128)(2,1)}, u32[]{:S(2)}, u32[]{:S(2)}) collective-permute-start(bf16[192,3072]{1,0:T(8,128)(2,1)} %pad_maximum_fusion.6.refs_5_), channel_id=1, source_target_pairs={{0,2},{2,0},{1,3},{3,1},{4,6},{6,4},{5,7},{7,5},{8,10},{10,8},{9,1... | collective-permute-start | bytes 3538952 | tf_op jit(solution)/shard_map/ppermute | solution.py:196
  207.5 75.0 %collective-permute-start.8 = (bf16[192,3072]{1,0:T(8,128)(2,1)}, bf16[192,3072]{1,0:T(8,128)(2,1)}, u32[]{:S(2)}, u32[]{:S(2)}) collective-permute-start(bf16[192,3072]{1,0:T(8,128)(2,1)} %collective-permute-done.4.refs_8_), channel_id=1, source_target_pairs={{0,4},{4,0},{1,5},{5,1},{2,6},{6,2},{3,7},{7,3},{8,12},{12,8},{9,1... | collective-permute-start | bytes 3538952 | tf_op jit(solution)/shard_map/ppermute | solution.py:196
  226.5 56.7 %collective-permute-start.7 = (bf16[192,3072]{1,0:T(8,128)(2,1)}, bf16[192,3072]{1,0:T(8,128)(2,1)}, u32[]{:S(2)}, u32[]{:S(2)}) collective-permute-start(bf16[192,3072]{1,0:T(8,128)(2,1)} %collective-permute-done.5.refs_9_), channel_id=1, source_target_pairs={{0,2},{2,0},{1,3},{3,1},{4,6},{6,4},{5,7},{7,5},{8,10},{10,8},{9,1... | collective-permute-start | bytes 3538952 | tf_op jit(solution)/shard_map/ppermute | solution.py:196
  240.0 39.1 %collective-permute-start.15 = (bf16[384,768]{1,0:T(8,128)(2,1)}, bf16[384,768]{1,0:T(8,128)(2,1)S(1)}, u32[]{:S(2)}, u32[]{:S(2)}) collective-permute-start(bf16[384,768]{1,0:T(8,128)(2,1)} %collective-permute-done.11.refs_16_), channel_id=1, source_target_pairs={{0,4},{4,0},{1,5},{5,1},{2,6},{6,2},{3,7},{7,3},{8,12},{12,8},{9,1... | collective-permute-start | bytes 1769480 | tf_op jit(solution)/shard_map/ppermute | solution.py:196
  279.1 86.2 %collective-permute-start.24 = (bf16[2,48,4608]{2,1,0:T(8,128)(2,1)}, bf16[2,48,4608]{2,1,0:T(8,128)(2,1)}, u32[]{:S(2)}, u32[]{:S(2)}) collective-permute-start(bf16[2,48,4608]{2,1,0:T(8,128)(2,1)} %pad_maximum_fusion.9.refs_1_.refs_9_.refs_17_), channel_id=1, source_target_pairs={{0,4},{4,0},{1,5},{5,1},{2,6},{6,2},{3,7},{7,3},{8,12},{12,8},{9,1... | collective-permute-start | bytes 2654216 | tf_op jit(solution)/shard_map/ppermute | solution.py:196
  280.6 85.3 %collective-permute-start.21 = (bf16[2,48,4608]{2,1,0:T(8,128)(2,1)}, bf16[2,48,4608]{2,1,0:T(8,128)(2,1)}, u32[]{:S(2)}, u32[]{:S(2)}) collective-permute-start(bf16[2,48,4608]{2,1,0:T(8,128)(2,1)} %pad_maximum_fusion.8.refs_0_.refs_8_.refs_16_), channel_id=1, source_target_pairs={{0,2},{2,0},{1,3},{3,1},{4,6},{6,4},{5,7},{7,5},{8,10},{10,8},{9,1... | collective-permute-start | bytes 2654216 | tf_op jit(solution)/shard_map/ppermute | solution.py:196
  281.2 84.7 %collective-permute-start.26 = (bf16[2,48,4608]{2,1,0:T(8,128)(2,1)}, bf16[2,48,4608]{2,1,0:T(8,128)(2,1)}, u32[]{:S(2)}, u32[]{:S(2)}) collective-permute-start(bf16[2,48,4608]{2,1,0:T(8,128)(2,1)} %collective-permute-done.22.refs_3_.refs_11_.refs_19_), channel_id=1, source_target_pairs={{0,4},{4,0},{1,5},{5,1},{2,6},{6,2},{3,7},{7,3},{8,12},{12,8},{9,1... | collective-permute-start | bytes 2654216 | tf_op jit(solution)/shard_map/ppermute | solution.py:196
  282.6 83.3 %collective-permute-start.25 = (bf16[2,48,4608]{2,1,0:T(8,128)(2,1)}, bf16[2,48,4608]{2,1,0:T(8,128)(2,1)}, u32[]{:S(2)}, u32[]{:S(2)}) collective-permute-start(bf16[2,48,4608]{2,1,0:T(8,128)(2,1)} %collective-permute-done.23.refs_4_.refs_12_.refs_20_), channel_id=1, source_target_pairs={{0,2},{2,0},{1,3},{3,1},{4,6},{6,4},{5,7},{7,5},{8,10},{10,8},{9,1... | collective-permute-start | bytes 2654216 | tf_op jit(solution)/shard_map/ppermute | solution.py:196
  363.8 41.9 %collective-permute-start.67 = (f32[384,768]{1,0:T(8,128)}, f32[384,768]{1,0:T(8,128)}, u32[]{:S(2)}, u32[]{:S(2)}) collective-permute-start(f32[384,768]{1,0:T(8,128)} %get-tuple-element.130), channel_id=1, source_target_pairs={{0,2},{2,0},{1,3},{3,1},{4,6},{6,4},{5,7},{7,5},{8,10},{10,8},{9,1... | collective-permute-start | bytes 3538952 | tf_op jit(solution)/shard_map/ppermute | solution.py:196
  365.3 49.1 %collective-permute-start.66 = (f32[384,768]{1,0:T(8,128)}, f32[384,768]{1,0:T(8,128)}, u32[]{:S(2)}, u32[]{:S(2)}) collective-permute-start(f32[384,768]{1,0:T(8,128)} %get-tuple-element.128), channel_id=1, source_target_pairs={{0,2},{2,0},{1,3},{3,1},{4,6},{6,4},{5,7},{7,5},{8,10},{10,8},{9,1... | collective-permute-start | bytes 3538952 | tf_op jit(solution)/shard_map/ppermute | solution.py:196
  401.3 51.5 %collective-permute-start.40 = (f32[192,1536]{1,0:T(8,128)}, f32[192,1536]{1,0:T(8,128)}, u32[]{:S(2)}, u32[]{:S(2)}) collective-permute-start(f32[192,1536]{1,0:T(8,128)} %get-tuple-element.110), channel_id=1, source_target_pairs={{0,8},{8,0},{16,24},{24,16},{1,9},{9,1},{17,25},{25,17},{2,10},{10... | collective-permute-start | bytes 3538952 | tf_op jit(solution)/shard_map/ppermute | solution.py:200
  402.7 80.7 %collective-permute-start.41 = (f32[192,1536]{1,0:T(8,128)}, f32[192,1536]{1,0:T(8,128)}, u32[]{:S(2)}, u32[]{:S(2)}) collective-permute-start(f32[192,1536]{1,0:T(8,128)} %get-tuple-element.111), channel_id=1, source_target_pairs={{0,16},{8,24},{16,0},{24,8},{1,17},{9,25},{17,1},{25,9},{2,18},{10... | collective-permute-start | bytes 3538952 | tf_op jit(solution)/shard_map/ppermute | solution.py:200
  405.0 79.7 %collective-permute-start.42 = (f32[192,1536]{1,0:T(8,128)}, f32[192,1536]{1,0:T(8,128)}, u32[]{:S(2)}, u32[]{:S(2)}) collective-permute-start(f32[192,1536]{1,0:T(8,128)} %get-tuple-element.112), channel_id=1, source_target_pairs={{0,24},{8,16},{16,8},{24,0},{1,25},{9,17},{17,9},{25,1},{2,26},{10... | collective-permute-start | bytes 3538952 | tf_op jit(solution)/shard_map/ppermute | solution.py:200
  405.7 99.7 %collective-permute-start.50 = (f32[192,1536]{1,0:T(8,128)}, f32[192,1536]{1,0:T(8,128)}, u32[]{:S(2)}, u32[]{:S(2)}) collective-permute-start(f32[192,1536]{1,0:T(8,128)} %get-tuple-element.116), channel_id=1, source_target_pairs={{0,8},{8,0},{16,24},{24,16},{1,9},{9,1},{17,25},{25,17},{2,10},{10... | collective-permute-start | bytes 3538952 | tf_op jit(solution)/shard_map/ppermute | solution.py:200
  414.4 186.9 %collective-permute-start.51 = (f32[192,1536]{1,0:T(8,128)}, f32[192,1536]{1,0:T(8,128)}, u32[]{:S(2)}, u32[]{:S(2)}) collective-permute-start(f32[192,1536]{1,0:T(8,128)} %get-tuple-element.117), channel_id=1, source_target_pairs={{0,16},{8,24},{16,0},{24,8},{1,17},{9,25},{17,1},{25,9},{2,18},{10... | collective-permute-start | bytes 3538952 | tf_op jit(solution)/shard_map/ppermute | solution.py:200
  452.8 155.8 %collective-permute-start.58 = (f32[2,192,1536]{2,1,0:T(8,128)}, f32[2,192,1536]{2,1,0:T(8,128)}, u32[]{:S(2)}, u32[]{:S(2)}) collective-permute-start(f32[2,192,1536]{2,1,0:T(8,128)} %get-tuple-element.122), channel_id=1, source_target_pairs={{0,4},{4,0},{1,5},{5,1},{2,6},{6,2},{3,7},{7,3},{8,12},{12,8},{9,1... | collective-permute-start | bytes 7077896 | tf_op jit(solution)/shard_map/ppermute | solution.py:196
  455.1 279.3 %all-to-all-start.3 = ((bf16[8,128,768]{2,1,0:T(8,128)(2,1)}), bf16[8,128,768]{2,1,0:T(8,128)(2,1)}, u32[]{:S(2)}, u32[]{:S(2)}) async-start(bf16[8,128,768]{2,1,0:T(8,128)(2,1)} %bitcast.288), calls=%async_computation.3 | async-start | bytes 3145728 | tf_op jit(solution)/shard_map/all_to_all | solution.py:548
  483.3 129.4 %collective-permute-start.56 = (f32[2,192,1536]{2,1,0:T(8,128)}, f32[2,192,1536]{2,1,0:T(8,128)}, u32[]{:S(2)}, u32[]{:S(2)}) collective-permute-start(f32[2,192,1536]{2,1,0:T(8,128)} %get-tuple-element.120), channel_id=1, source_target_pairs={{0,2},{2,0},{1,3},{3,1},{4,6},{6,4},{5,7},{7,5},{8,10},{10,8},{9,1... | collective-permute-start | bytes 7077896 | tf_op jit(solution)/shard_map/ppermute | solution.py:196
  484.7 120.5 %collective-permute-start.52 = (f32[192,1536]{1,0:T(8,128)}, f32[192,1536]{1,0:T(8,128)}, u32[]{:S(2)}, u32[]{:S(2)}) collective-permute-start(f32[192,1536]{1,0:T(8,128)} %get-tuple-element.118), channel_id=1, source_target_pairs={{0,24},{8,16},{16,8},{24,0},{1,25},{9,17},{17,9},{25,1},{2,26},{10... | collective-permute-start | bytes 3538952 | tf_op jit(solution)/shard_map/ppermute | solution.py:200
  505.7 109.6 %collective-permute-start.63 = (f32[2,192,1536]{2,1,0:T(8,128)S(1)}, f32[2,192,1536]{2,1,0:T(8,128)S(1)}, u32[]{:S(2)}, u32[]{:S(2)}) collective-permute-start(f32[2,192,1536]{2,1,0:T(8,128)S(1)} %copy-done.87), channel_id=1, source_target_pairs={{0,4},{4,0},{1,5},{5,1},{2,6},{6,2},{3,7},{7,3},{8,12},{12,8},{9,1... | collective-permute-start | bytes 7077896 | tf_op jit(solution)/shard_map/ppermute | solution.py:196
  601.3 54.1 %collective-permute-start.61 = (f32[2,192,1536]{2,1,0:T(8,128)S(1)}, f32[2,192,1536]{2,1,0:T(8,128)S(1)}, u32[]{:S(2)}, u32[]{:S(2)}) collective-permute-start(f32[2,192,1536]{2,1,0:T(8,128)S(1)} %copy-done.86), channel_id=1, source_target_pairs={{0,2},{2,0},{1,3},{3,1},{4,6},{6,4},{5,7},{7,5},{8,10},{10,8},{9,1... | collective-permute-start | bytes 7077896 | tf_op jit(solution)/shard_map/ppermute | solution.py:196
  605.4 54.1 %collective-permute-start.69 = (f32[2,384,768]{2,1,0:T(8,128)S(1)}, f32[2,384,768]{2,1,0:T(8,128)S(1)}, u32[]{:S(2)}, u32[]{:S(2)}) collective-permute-start(f32[2,384,768]{2,1,0:T(8,128)S(1)} %copy-done.25), channel_id=1, source_target_pairs={{0,4},{4,0},{1,5},{5,1},{2,6},{6,2},{3,7},{7,3},{8,12},{12,8},{9,1... | collective-permute-start | bytes 7077896 | tf_op jit(solution)/shard_map/ppermute | solution.py:196
  608.6 204.7 %collective-permute-start.45 = (f32[2,192,1536]{2,1,0:T(8,128)}, f32[2,192,1536]{2,1,0:T(8,128)}, u32[]{:S(2)}, u32[]{:S(2)}) collective-permute-start(f32[2,192,1536]{2,1,0:T(8,128)} %get-tuple-element.114), channel_id=1, source_target_pairs={{0,2},{2,0},{1,3},{3,1},{4,6},{6,4},{5,7},{7,5},{8,10},{10,8},{9,1... | collective-permute-start | bytes 7077896 | tf_op jit(solution)/shard_map/ppermute | solution.py:196
  612.7 130.7 %collective-permute-start.27 = (f32[512,768]{0,1:T(8,128)}, f32[512,768]{0,1:T(8,128)}, u32[]{:S(2)}, u32[]{:S(2)}) collective-permute-start(f32[512,768]{0,1:T(8,128)} %copy.249), channel_id=1, source_target_pairs={{0,1},{1,0},{2,3},{3,2},{4,5},{5,4},{6,7},{7,6},{8,9},{9,8},{10,11... | collective-permute-start | bytes 4718600 | tf_op jit(solution)/shard_map/ppermute | solution.py:196
  615.3 58.3 %collective-permute-start.68 = (f32[384,768]{1,0:T(8,128)S(1)}, f32[384,768]{1,0:T(8,128)S(1)}, u32[]{:S(2)}, u32[]{:S(2)}) collective-permute-start(f32[384,768]{1,0:T(8,128)S(1)} %broadcast_select_fusion.1), channel_id=1, source_target_pairs={{0,4},{4,0},{1,5},{5,1},{2,6},{6,2},{3,7},{7,3},{8,12},{12,8},{9,1... | collective-permute-start | bytes 3538952 | tf_op jit(solution)/shard_map/ppermute | solution.py:196
  655.4 353.2 %collective-permute-start.31 = (f32[512,768]{0,1:T(8,128)}, f32[512,768]{0,1:T(8,128)}, u32[]{:S(2)}, u32[]{:S(2)}) collective-permute-start(f32[512,768]{0,1:T(8,128)} %copy.262), channel_id=1, source_target_pairs={{0,1},{1,0},{2,3},{3,2},{4,5},{5,4},{6,7},{7,6},{8,9},{9,8},{10,11... | collective-permute-start | bytes 4718600 | tf_op jit(solution)/shard_map/ppermute | solution.py:196
  659.6 59.0 %collective-permute-start.43 = (f32[2,1,48,1536]{3,2,1,0:T(8,128)S(1)}, f32[2,1,48,1536]{3,2,1,0:T(8,128)S(1)}, u32[]{:S(2)}, u32[]{:S(2)}) collective-permute-start(f32[2,1,48,1536]{3,2,1,0:T(8,128)S(1)} %split.43), channel_id=1, source_target_pairs={{0,2},{2,0},{1,3},{3,1},{4,6},{6,4},{5,7},{7,5},{8,10},{10,8},{9,1... | collective-permute-start | bytes 1769480 | tf_op jit(solution)/shard_map/ppermute | solution.py:196
  673.6 57.6 %collective-permute-start.53 = (f32[2,1,48,1536]{3,2,1,0:T(8,128)S(1)}, f32[2,1,48,1536]{3,2,1,0:T(8,128)S(1)}, u32[]{:S(2)}, u32[]{:S(2)}) collective-permute-start(f32[2,1,48,1536]{3,2,1,0:T(8,128)S(1)} %split.45), channel_id=1, source_target_pairs={{0,2},{2,0},{1,3},{3,1},{4,6},{6,4},{5,7},{7,5},{8,10},{10,8},{9,1... | collective-permute-start | bytes 1769480 | tf_op jit(solution)/shard_map/ppermute | solution.py:196
  718.6 148.5 %collective-permute-start.70 = (f32[384,768]{1,0:T(8,128)}, f32[384,768]{1,0:T(8,128)}, u32[]{:S(2)}, u32[]{:S(2)}) collective-permute-start(f32[384,768]{1,0:T(8,128)} %slice_bitcast_fusion.2), channel_id=1, source_target_pairs={{0,2},{2,0},{1,3},{3,1},{4,6},{6,4},{5,7},{7,5},{8,10},{10,8},{9,1... | collective-permute-start | bytes 3538952 | tf_op jit(solution)/shard_map/ppermute | solution.py:196
  731.2 84.3 %collective-permute-start.59 = (f32[192,1536]{1,0:T(8,128)}, f32[192,1536]{1,0:T(8,128)}, u32[]{:S(2)}, u32[]{:S(2)}) collective-permute-start(f32[192,1536]{1,0:T(8,128)} %fusion.44), channel_id=1, source_target_pairs={{0,2},{2,0},{1,3},{3,1},{4,6},{6,4},{5,7},{7,5},{8,10},{10,8},{9,1... | collective-permute-start | bytes 3538952 | tf_op jit(solution)/shard_map/ppermute | solution.py:196
  734.5 254.2 %all-to-all-start.2 = ((bf16[8,128,768]{2,1,0:T(8,128)(2,1)}), bf16[8,128,768]{2,1,0:T(8,128)(2,1)}, u32[]{:S(2)}, u32[]{:S(2)}) async-start(bf16[8,128,768]{2,1,0:T(8,128)(2,1)} %bitcast.287), calls=%async_computation.2 | async-start | bytes 3145728 | tf_op jit(solution)/shard_map/all_to_all | solution.py:548
  743.4 57.4 %collective-permute-start.44 = (f32[1,48,1536]{2,1,0:T(8,128)}, f32[1,48,1536]{2,1,0:T(8,128)}, u32[]{:S(2)}, u32[]{:S(2)}) collective-permute-start(f32[1,48,1536]{2,1,0:T(8,128)} %slice_bitcast_fusion.6), channel_id=1, source_target_pairs={{0,4},{4,0},{1,5},{5,1},{2,6},{6,2},{3,7},{7,3},{8,12},{12,8},{9,1... | collective-permute-start | bytes 884744 | tf_op jit(solution)/shard_map/ppermute | solution.py:196
  811.8 29.0 %collective-permute-start.57 = (f32[192,1536]{1,0:T(8,128)}, f32[192,1536]{1,0:T(8,128)S(1)}, u32[]{:S(2)}, u32[]{:S(2)}) collective-permute-start(f32[192,1536]{1,0:T(8,128)} %fusion.47), channel_id=1, source_target_pairs={{0,4},{4,0},{1,5},{5,1},{2,6},{6,2},{3,7},{7,3},{8,12},{12,8},{9,1... | collective-permute-start | bytes 3538952 | tf_op jit(solution)/shard_map/ppermute | solution.py:196
  813.3 29.1 %collective-permute-start.64 = (f32[192,1536]{1,0:T(8,128)S(1)}, f32[192,1536]{1,0:T(8,128)S(1)}, u32[]{:S(2)}, u32[]{:S(2)}) collective-permute-start(f32[192,1536]{1,0:T(8,128)S(1)} %copy-done.53), channel_id=1, source_target_pairs={{0,2},{2,0},{1,3},{3,1},{4,6},{6,4},{5,7},{7,5},{8,10},{10,8},{9,1... | collective-permute-start | bytes 3538952 | tf_op jit(solution)/shard_map/ppermute | solution.py:196
  815.6 49.7 %collective-permute-start.62 = (f32[192,1536]{1,0:T(8,128)S(1)}, f32[192,1536]{1,0:T(8,128)S(1)}, u32[]{:S(2)}, u32[]{:S(2)}) collective-permute-start(f32[192,1536]{1,0:T(8,128)S(1)} %copy-done.52), channel_id=1, source_target_pairs={{0,4},{4,0},{1,5},{5,1},{2,6},{6,2},{3,7},{7,3},{8,12},{12,8},{9,1... | collective-permute-start | bytes 3538952 | tf_op jit(solution)/shard_map/ppermute | solution.py:196
  840.9 83.6 %collective-permute-start.28 = (f32[768,1152]{1,0:T(8,128)}, f32[768,1152]{1,0:T(8,128)S(1)}, u32[]{:S(2)}, u32[]{:S(2)}) collective-permute-start(f32[768,1152]{1,0:T(8,128)} %fusion.53), channel_id=1, source_target_pairs={{0,1},{1,0},{2,3},{3,2},{4,5},{5,4},{6,7},{7,6},{8,9},{9,8},{10,11... | collective-permute-start | bytes 10616840 | tf_op jit(solution)/shard_map/ppermute | solution.py:196
  842.4 55.8 %collective-permute-start.29 = (f32[768,384]{1,0:T(8,128)S(1)}, f32[768,384]{1,0:T(8,128)S(1)}, u32[]{:S(2)}, u32[]{:S(2)}) collective-permute-start(f32[768,384]{1,0:T(8,128)S(1)} %fusion.82), channel_id=1, source_target_pairs={{0,1},{1,0},{2,3},{3,2},{4,5},{5,4},{6,7},{7,6},{8,9},{9,8},{10,11... | collective-permute-start | bytes 3538952 | tf_op jit(solution)/shard_map/ppermute | solution.py:196
  865.3 27.2 %collective-permute-start.46 = (f32[192,1536]{1,0:T(8,128)S(1)}, f32[192,1536]{1,0:T(8,128)S(1)}, u32[]{:S(2)}, u32[]{:S(2)}) collective-permute-start(f32[192,1536]{1,0:T(8,128)S(1)} %fusion.50), channel_id=1, source_target_pairs={{0,4},{4,0},{1,5},{5,1},{2,6},{6,2},{3,7},{7,3},{8,12},{12,8},{9,1... | collective-permute-start | bytes 3538952 | tf_op jit(solution)/shard_map/ppermute | solution.py:196
  895.8 23.4 %collective-permute-start.48 = (f32[48,1536]{1,0:T(8,128)S(1)}, f32[48,1536]{1,0:T(8,128)S(1)}, u32[]{:S(2)}, u32[]{:S(2)}) collective-permute-start(f32[48,1536]{1,0:T(8,128)S(1)} %get-tuple-element.247), channel_id=1, source_target_pairs={{0,16},{8,24},{16,0},{24,8},{1,17},{9,25},{17,1},{25,9},{2,18},{10... | collective-permute-start | bytes 884744 | tf_op jit(solution)/shard_map/ppermute | solution.py:200
  898.2 21.0 %collective-permute-start.49 = (f32[48,1536]{1,0:T(8,128)S(1)}, f32[48,1536]{1,0:T(8,128)S(1)}, u32[]{:S(2)}, u32[]{:S(2)}) collective-permute-start(f32[48,1536]{1,0:T(8,128)S(1)} %get-tuple-element.246), channel_id=1, source_target_pairs={{0,24},{8,16},{16,8},{24,0},{1,25},{9,17},{17,9},{25,1},{2,26},{10... | collective-permute-start | bytes 884744 | tf_op jit(solution)/shard_map/ppermute | solution.py:200
  906.3 28.8 %collective-permute-start.71 = (f32[768,384]{1,0:T(8,128)S(1)}, f32[768,384]{1,0:T(8,128)S(1)}, u32[]{:S(2)}, u32[]{:S(2)}) collective-permute-start(f32[768,384]{1,0:T(8,128)S(1)} %broadcast_select_fusion.2), channel_id=1, source_target_pairs={{0,1},{1,0},{2,3},{3,2},{4,5},{5,4},{6,7},{7,6},{8,9},{9,8},{10,11... | collective-permute-start | bytes 3538952 | tf_op jit(solution)/shard_map/ppermute | solution.py:196
  922.0 17.6 %collective-permute-start.55 = (f32[24,4608]{1,0:T(8,128)}, f32[24,4608]{1,0:T(8,128)}, u32[]{:S(2)}, u32[]{:S(2)}) collective-permute-start(f32[24,4608]{1,0:T(8,128)} %get-tuple-element.249), channel_id=1, source_target_pairs={{0,1},{1,0},{2,3},{3,2},{4,5},{5,4},{6,7},{7,6},{8,9},{9,8},{10,11... | collective-permute-start | bytes 1327112 | tf_op jit(solution)/shard_map/ppermute | solution.py:196
  929.2 30.4 %collective-permute-start.34 = (f32[2,2,48,1664]{3,2,1,0:T(8,128)}, f32[2,2,48,1664]{3,2,1,0:T(8,128)}, u32[]{:S(2)}, u32[]{:S(2)}) collective-permute-start(f32[2,2,48,1664]{3,2,1,0:T(8,128)} %dynamic-slice_bitcast_fusion), channel_id=1, source_target_pairs={{0,4},{4,0},{1,5},{5,1},{2,6},{6,2},{3,7},{7,3},{8,12},{12,8},{9,1... | collective-permute-start | bytes 3833864 | tf_op jit(solution)/shard_map/ppermute | solution.py:196
  931.7 30.7 %collective-permute-start.32 = (f32[2,2,48,1664]{3,2,1,0:T(8,128)}, f32[2,2,48,1664]{3,2,1,0:T(8,128)}, u32[]{:S(2)}, u32[]{:S(2)}) collective-permute-start(f32[2,2,48,1664]{3,2,1,0:T(8,128)} %dynamic-slice_bitcast_fusion.1), channel_id=1, source_target_pairs={{0,2},{2,0},{1,3},{3,1},{4,6},{6,4},{5,7},{7,5},{8,10},{10,8},{9,1... | collective-permute-start | bytes 3833864 | tf_op jit(solution)/shard_map/ppermute | solution.py:196
  960.9 15.6 %collective-permute-start.35 = (f32[2,48,1664]{2,1,0:T(8,128)S(1)}, f32[2,48,1664]{2,1,0:T(8,128)S(1)}, u32[]{:S(2)}, u32[]{:S(2)}) collective-permute-start(f32[2,48,1664]{2,1,0:T(8,128)S(1)} %bitcast_add_fusion), channel_id=1, source_target_pairs={{0,2},{2,0},{1,3},{3,1},{4,6},{6,4},{5,7},{7,5},{8,10},{10,8},{9,1... | collective-permute-start | bytes 1916936 | tf_op jit(solution)/shard_map/ppermute | solution.py:196
  983.4 25.0 %collective-permute-start.37 = (f32[48,1664]{1,0:T(8,128)S(1)}, f32[48,1664]{1,0:T(8,128)S(1)}, u32[]{:S(2)}, u32[]{:S(2)}) collective-permute-start(f32[48,1664]{1,0:T(8,128)S(1)} %get-tuple-element.238), channel_id=1, source_target_pairs={{0,16},{8,24},{16,0},{24,8},{1,17},{9,25},{17,1},{25,9},{2,18},{10... | collective-permute-start | bytes 958472 | tf_op jit(solution)/shard_map/ppermute | solution.py:200
  984.3 24.1 %collective-permute-start.38 = (f32[48,1664]{1,0:T(8,128)S(1)}, f32[48,1664]{1,0:T(8,128)S(1)}, u32[]{:S(2)}, u32[]{:S(2)}) collective-permute-start(f32[48,1664]{1,0:T(8,128)S(1)} %get-tuple-element.239), channel_id=1, source_target_pairs={{0,24},{8,16},{16,8},{24,0},{1,25},{9,17},{17,9},{25,1},{2,26},{10... | collective-permute-start | bytes 958472 | tf_op jit(solution)/shard_map/ppermute | solution.py:200
  (103 other events, 1237.0 us)
